TPU v7x, 128 devices: a whole 4x4x4 slice. The times are simulated.
128 devices in a mesh: group: 4 (over x_lo, core), blk: 32 (over y, z, x_hi).
Axes of the slice: x: 4 (x_hi: 2, x_lo: 2; x = x_hi * 2 + x_lo), y: 4, z: 4, core: 2. Of those that a mesh axis runs over, the one named last changes fastest.
Arguments:
- orbitals: float32 [128, 64, 4096], P(('group', 'blk')), may hold values from -6 to 6
- occupation: float32 [128], P(('group', 'blk')), may hold values from 0.3 to 1
Outputs:
- exchange: float32 [128, 64, 4096], P(('group', 'blk'))
All inputs are finite; a program needn't handle non-finite values.
Results may differ from a plain program's by a relative error of at most 0.0003.
Values sent between devices are 32-bit elements; how exact they have to be, the bound alone decides.
No kernel may reach another device: no remote copies, remote signals or barrier semaphores. Data moves between devices by JAX's collectives and lax.ppermute only.
A program may use at most 128 MiB of HBM per device.

v0:
```python
import jax
import jax.numpy as jnp
from jax import lax
from jax.sharding import PartitionSpec as P

STEPS = 3


HIGH = lax.Precision.HIGHEST


def from_behind(value, axis, steps):
    count = lax.axis_size(axis)
    pairs = [(source, (source + steps) % count) for source in range(count)]
    return lax.ppermute(value, axis, pairs)


def tables(size):
    index = jnp.arange(size, dtype=jnp.int32)
    product = index[:, None] * index[None, :] % size
    angle = product.astype(jnp.float32) * (2.0 * jnp.pi / size)
    cosine = jnp.cos(angle)
    sine = jnp.sin(angle)
    forward = jnp.stack([jnp.stack([cosine, sine]), jnp.stack([-sine, cosine])])
    inverse = jnp.stack([jnp.stack([cosine, -sine]), jnp.stack([sine, cosine])])
    signed = jnp.where(index < size // 2, index, index - size).astype(jnp.float32)
    square = signed * signed
    total = square[:, None, None] + square[None, :, None] + square[None, None, :]
    step = 2.0 * jnp.pi / size
    kernel = jnp.pi / (step * step * total + 0.25)
    return (forward, inverse, kernel)


def complex_along(table, field, axis):
    if axis == 0:
        return jnp.einsum("rska,spabc->rpkbc", table, field, precision=HIGH)
    if axis == 1:
        return jnp.einsum("rskb,spabc->rpakc", table, field, precision=HIGH)
    return jnp.einsum("rskc,spabc->rpabk", table, field, precision=HIGH)


def solve_pairs(home, visit, forward, inverse, kernel):
    size = home.shape[1]
    count = home.shape[0]
    density = (home[:, None] * visit[None, :]).reshape(count * count, size, size, size)
    field = jnp.einsum("rka,pabc->rpkbc", forward[:, 0], density, precision=HIGH)
    field = complex_along(forward, field, 1)
    field = complex_along(forward, field, 2)
    field = field * kernel
    field = complex_along(inverse, field, 0)
    field = complex_along(inverse, field, 1)
    final = jnp.einsum("skc,spabc->pabk", inverse[0], field, precision=HIGH)
    final = final * (1.0 / (size * size * size))
    return final.reshape(count, count, size, size * size)


def local(orbitals, occupation):
    size = orbitals.shape[1]
    forward, inverse, kernel = tables(size)
    home_acc = jnp.zeros(orbitals.shape, jnp.float32)

    def meet_home(home_acc, visit_orb, visit_occ):
        potential = solve_pairs(orbitals, visit_orb, forward, inverse, kernel)
        home_acc = home_acc - jnp.sum(
            visit_occ[None, :, None, None] * visit_orb[None, :] * potential, axis=1
        )
        return (home_acc, potential)

    def collect(visit_acc, potential):
        return visit_acc - jnp.sum(
            occupation[:, None, None, None] * orbitals[:, None] * potential, axis=0
        )

    visit_acc = jnp.zeros(orbitals.shape, jnp.float32)
    visit_orb, visit_occ = (orbitals, occupation)
    for turn in range(STEPS):
        visit_orb, visit_occ = from_behind((visit_orb, visit_occ), "blk", 1)
        if turn > 0:
            visit_acc = from_behind(visit_acc, "blk", 1)
        home_acc, potential = meet_home(home_acc, visit_orb, visit_occ)
        visit_acc = collect(visit_acc, potential)
    visit_orb, visit_occ = from_behind((visit_orb, visit_occ), "group", 1)
    visit_acc = from_behind(visit_acc, "group", 1)
    home_acc, potential = meet_home(home_acc, visit_orb, visit_occ)
    visit_acc = collect(visit_acc, potential)
    visit_acc = from_behind(visit_acc, "group", -1)
    visit_acc = from_behind(visit_acc, "blk", -STEPS)
    return home_acc + visit_acc


def solution(mesh):
    return jax.shard_map(
        local,
        mesh=mesh,
        in_specs=(P(("group", "blk"), None, None), P(("group", "blk"))),
        out_specs=P(("group", "blk"), None, None),
        check_vma=False,
    )
```

profile of v0, /device:TPU:0, one launch (start us, length us, event | category | flops | bytes accessed | tf_op | source)
XLA Modules:
  0.0 412.8 jit_solution(761390395377968702)
XLA Ops:
  3.1 29.3 %collective-permute-done.1 = f32[1,64,4096]{2,1,0:T(8,128)S(1)} collective-permute-done((f32[1,64,4096]{2,1,0:T(8,128)}, f32[1,64,4096]{2,1,0:T(8,128)S(1)}, u32[]{:S(2)}, u32[]{:S(2)}) %collective-permute-start.1) | collective-permute-done | bytes 1048608 | tf_op jit(solution)/shard_map/ppermute | solution.py:15
  34.2 28.3 %collective-permute-done.3 = f32[1,64,4096]{2,1,0:T(8,128)S(1)} collective-permute-done((f32[1,64,4096]{2,1,0:T(8,128)S(1)}, f32[1,64,4096]{2,1,0:T(8,128)S(1)}, u32[]{:S(2)}, u32[]{:S(2)}) %collective-permute-start.3) | collective-permute-done | bytes 1048608 | tf_op jit(solution)/shard_map/ppermute | solution.py:15
  70.5 7.0 %convolution_bitcast_fusion.3 = f32[2,64,64,64,1]{1,3,0,2,4:T(8,128)} fusion(f32[64,64,64,1]{0,2,3,1:T(8,128)} %bitcast.339, f32[2,64,64,1]{2,1,0,3:T(8,128)S(1)} %fusion.80), kind=kOutput, calls=%fused_computation.39 | convolution fusion | flops 402653184 | bytes 3178496 | tf_op jit(solution)/shard_map/rka,pabc->rpkbc/dot_general | solution.py:46
  77.4 6.6 %copy.37 = f32[2,64,64,64,1]{2,3,0,4,1:T(8,128)} copy(f32[2,64,64,64,1]{1,3,0,2,4:T(8,128)} %convolution_bitcast_fusion.3) | data formatting | bytes 4194304 | tf_op jit(solution)/shard_map/reshape.3
  89.8 7.2 %fusion.27 = f32[2,64,64,64,1]{3,2,0,1,4:T(8,128)S(1)} fusion(f32[64,64,2,64,1]{3,1,4,2,0:T(8,128)S(1)} %fusion.66, f32[64,64,64]{2,1,0:T(8,128)S(1)} %add_divide_fusion, f32[1,2,64,64]{3,2,0,1:T(8,128)S(1)} %get-tuple-element.11, f32[1,2,64,64]{3,2,0,1:T(8,128)S(1)} %get-tuple-element.14), kind=kOutput, calls=%fused_computation.31 | convolution fusion | flops 805847040 | bytes 5308416 | tf_op jit(solution)/shard_map/rskc,spabc->rpabk/dot_general | solution.py:39
  97.0 11.7 %fusion.28 = f32[2,64,64,64,1]{1,3,0,2,4:T(8,128)} fusion(f32[2,64,64,64,1]{3,2,0,1,4:T(8,128)S(1)} %fusion.27, f32[1,2,64,64]{3,2,1,0:T(8,128)S(1)} %get-tuple-element.15, f32[1,2,64,64]{3,2,1,0:T(8,128)S(1)} %get-tuple-element.10), kind=kOutput, calls=%fused_computation.32 | convolution fusion | flops 805322752 | bytes 4259840 | tf_op jit(solution)/shard_map/rska,spabc->rpkbc/dot_general | solution.py:36
  120.8 8.4 %bitcast_multiply_fusion.7 = f32[64,64,64]{2,1,0:T(8,128)} fusion(f32[64,64,2,64,1]{3,1,4,2,0:T(8,128)S(1)} %fusion.104, f32[1,64,64]{2,1,0:T(8,128)S(1)} %get-tuple-element.17, f32[1,64,64]{2,1,0:T(8,128)S(1)} %fusion.94), kind=kOutput, calls=%fused_computation.43 | convolution fusion | flops 402923520 | bytes 3178496 | tf_op jit(solution)/shard_map/skc,spabc->pabk/dot_general | solution.py:52
  151.8 7.2 %fusion.24 = f32[2,64,64,64,1]{3,2,0,1,4:T(8,128)S(1)} fusion(f32[64,64,2,64,1]{3,1,4,2,0:T(8,128)S(1)} %fusion.63, f32[64,64,64]{2,1,0:T(8,128)S(1)} %add_divide_fusion, f32[1,2,64,64]{3,2,0,1:T(8,128)S(1)} %get-tuple-element.11, f32[1,2,64,64]{3,2,0,1:T(8,128)S(1)} %get-tuple-element.14), kind=kOutput, calls=%fused_computation.27 | convolution fusion | flops 805847040 | bytes 5308416 | tf_op jit(solution)/shard_map/rskc,spabc->rpabk/dot_general | solution.py:39
  159.0 7.6 %collective-permute-done.5 = f32[1,64,4096]{2,1,0:T(8,128)} collective-permute-done((f32[1,64,4096]{2,1,0:T(8,128)}, f32[1,64,4096]{2,1,0:T(8,128)}, u32[]{:S(2)}, u32[]{:S(2)}) %collective-permute-start.5) | collective-permute-done | bytes 1048608 | tf_op jit(solution)/shard_map/ppermute | solution.py:15
  166.6 11.7 %fusion.31 = f32[2,64,64,64,1]{1,3,0,2,4:T(8,128)} fusion(f32[2,64,64,64,1]{3,2,0,1,4:T(8,128)S(1)} %fusion.24, f32[1,2,64,64]{3,2,1,0:T(8,128)S(1)} %get-tuple-element.15, f32[1,2,64,64]{3,2,1,0:T(8,128)S(1)} %get-tuple-element.10), kind=kOutput, calls=%fused_computation.33 | convolution fusion | flops 805322752 | bytes 4259840 | tf_op jit(solution)/shard_map/rska,spabc->rpkbc/dot_general | solution.py:36
  190.5 8.4 %bitcast_multiply_fusion.6 = f32[64,64,64]{2,1,0:T(8,128)} fusion(f32[64,64,2,64,1]{3,1,4,2,0:T(8,128)S(1)} %fusion.103, f32[1,64,64]{2,1,0:T(8,128)S(1)} %get-tuple-element.17, f32[1,64,64]{2,1,0:T(8,128)S(1)} %fusion.94), kind=kOutput, calls=%fused_computation.42 | convolution fusion | flops 402923520 | bytes 3178496 | tf_op jit(solution)/shard_map/skc,spabc->pabk/dot_general | solution.py:52
  212.5 7.0 %convolution_bitcast_fusion.1 = f32[2,64,64,64,1]{1,3,0,2,4:T(8,128)} fusion(f32[64,64,64,1]{0,2,3,1:T(8,128)} %bitcast.340, f32[2,64,64,1]{2,1,0,3:T(8,128)S(1)} %fusion.80), kind=kOutput, calls=%fused_computation.37 | convolution fusion | flops 402653184 | bytes 3178496 | tf_op jit(solution)/shard_map/rka,pabc->rpkbc/dot_general | solution.py:46
  225.5 6.2 %fusion.60 = f32[64,64,2,64,1]{3,1,4,2,0:T(8,128)S(1)} fusion(f32[2,64,64,64,1]{2,3,0,4,1:T(8,128)} %copy.59, f32[1,2,64,64]{3,2,0,1:T(8,128)S(1)} %get-tuple-element.11, f32[1,2,64,64]{3,2,0,1:T(8,128)S(1)} %get-tuple-element.14), kind=kOutput, calls=%fused_computation.58 | convolution fusion | flops 805322752 | bytes 4259840 | tf_op jit(solution)/shard_map/rskb,spabc->rpakc/dot_general | solution.py:38
  231.7 7.2 %fusion.21 = f32[2,64,64,64,1]{3,2,0,1,4:T(8,128)S(1)} fusion(f32[64,64,2,64,1]{3,1,4,2,0:T(8,128)S(1)} %fusion.60, f32[64,64,64]{2,1,0:T(8,128)S(1)} %add_divide_fusion, f32[1,2,64,64]{3,2,0,1:T(8,128)S(1)} %get-tuple-element.11, f32[1,2,64,64]{3,2,0,1:T(8,128)S(1)} %get-tuple-element.14), kind=kOutput, calls=%fused_computation.23 | convolution fusion | flops 805847040 | bytes 5308416 | tf_op jit(solution)/shard_map/rskc,spabc->rpabk/dot_general | solution.py:39
  238.9 11.7 %fusion.34 = f32[2,64,64,64,1]{1,3,0,2,4:T(8,128)} fusion(f32[2,64,64,64,1]{3,2,0,1,4:T(8,128)S(1)} %fusion.21, f32[1,2,64,64]{3,2,1,0:T(8,128)S(1)} %get-tuple-element.15, f32[1,2,64,64]{3,2,1,0:T(8,128)S(1)} %get-tuple-element.10), kind=kOutput, calls=%fused_computation.34 | convolution fusion | flops 805322752 | bytes 4259840 | tf_op jit(solution)/shard_map/rska,spabc->rpkbc/dot_general | solution.py:36
  262.8 8.4 %bitcast_multiply_fusion.5 = f32[64,64,64]{2,1,0:T(8,128)} fusion(f32[64,64,2,64,1]{3,1,4,2,0:T(8,128)S(1)} %fusion.102, f32[1,64,64]{2,1,0:T(8,128)S(1)} %get-tuple-element.17, f32[1,64,64]{2,1,0:T(8,128)S(1)} %fusion.94), kind=kOutput, calls=%fused_computation.41 | convolution fusion | flops 402923520 | bytes 3178496 | tf_op jit(solution)/shard_map/skc,spabc->pabk/dot_general | solution.py:52
  285.6 6.2 %fusion.57 = f32[64,64,2,64,1]{3,1,4,2,0:T(8,128)S(1)} fusion(f32[2,64,64,64,1]{2,3,0,4,1:T(8,128)} %copy.70, f32[1,2,64,64]{3,2,0,1:T(8,128)S(1)} %get-tuple-element.11, f32[1,2,64,64]{3,2,0,1:T(8,128)S(1)} %get-tuple-element.14), kind=kOutput, calls=%fused_computation.55 | convolution fusion | flops 805322752 | bytes 4259840 | tf_op jit(solution)/shard_map/rskb,spabc->rpakc/dot_general | solution.py:38
  291.8 7.2 %fusion.18 = f32[2,64,64,64,1]{3,2,0,1,4:T(8,128)S(1)} fusion(f32[64,64,2,64,1]{3,1,4,2,0:T(8,128)S(1)} %fusion.57, f32[64,64,64]{2,1,0:T(8,128)S(1)} %add_divide_fusion, f32[1,2,64,64]{3,2,0,1:T(8,128)S(1)} %get-tuple-element.11, f32[1,2,64,64]{3,2,0,1:T(8,128)S(1)} %get-tuple-element.14), kind=kOutput, calls=%fused_computation.19 | convolution fusion | flops 805847040 | bytes 5308416 | tf_op jit(solution)/shard_map/rskc,spabc->rpabk/dot_general | solution.py:39
  305.4 11.7 %fusion.37 = f32[2,64,64,64,1]{1,3,0,2,4:T(8,128)} fusion(f32[2,64,64,64,1]{3,2,0,1,4:T(8,128)S(1)} %fusion.18, f32[1,2,64,64]{3,2,1,0:T(8,128)S(1)} %get-tuple-element.15, f32[1,2,64,64]{3,2,1,0:T(8,128)S(1)} %get-tuple-element.10), kind=kOutput, calls=%fused_computation.35 | convolution fusion | flops 805322752 | bytes 4259840 | tf_op jit(solution)/shard_map/rska,spabc->rpkbc/dot_general | solution.py:36
  329.2 8.4 %bitcast_multiply_fusion.4 = f32[64,64,64]{2,1,0:T(8,128)} fusion(f32[64,64,2,64,1]{3,1,4,2,0:T(8,128)S(1)} %fusion.101, f32[1,64,64]{2,1,0:T(8,128)S(1)} %get-tuple-element.17, f32[1,64,64]{2,1,0:T(8,128)S(1)} %fusion.94), kind=kOutput, calls=%fused_computation.40 | convolution fusion | flops 402923520 | bytes 3178496 | tf_op jit(solution)/shard_map/skc,spabc->pabk/dot_general | solution.py:52
  344.4 12.3 %collective-permute-done.11 = f32[1,64,4096]{2,1,0:T(8,128)S(1)} collective-permute-done((f32[1,64,4096]{2,1,0:T(8,128)S(1)}, f32[1,64,4096]{2,1,0:T(8,128)S(1)}, u32[]{:S(2)}, u32[]{:S(2)}) %collective-permute-start.11) | collective-permute-done | bytes 1048608 | tf_op jit(solution)/shard_map/ppermute | solution.py:15
  357.6 26.8 %collective-permute-done = f32[1]{0:T(128)} collective-permute-done((f32[1]{0:T(128)}, f32[1]{0:T(128)}, u32[]{:S(2)}, u32[]{:S(2)}) %collective-permute-start) | collective-permute-done | bytes 36 | tf_op jit(solution)/shard_map/ppermute | solution.py:15
  385.1 9.0 %collective-permute-done.2 = f32[1]{0:T(128)} collective-permute-done((f32[1]{0:T(128)}, f32[1]{0:T(128)}, u32[]{:S(2)}, u32[]{:S(2)}) %collective-permute-start.2) | collective-permute-done | bytes 36 | tf_op jit(solution)/shard_map/ppermute | solution.py:15
  394.0 9.6 %collective-permute-done.4 = f32[1]{0:T(128)} collective-permute-done((f32[1]{0:T(128)}, f32[1]{0:T(128)}, u32[]{:S(2)}, u32[]{:S(2)}) %collective-permute-start.4) | collective-permute-done | bytes 36 | tf_op jit(solution)/shard_map/ppermute | solution.py:15
  (79 shorter events, 146.7 us)
Async XLA Ops:
  0.0 32.4 %collective-permute-start.1 = (f32[1,64,4096]{2,1,0:T(8,128)}, f32[1,64,4096]{2,1,0:T(8,128)S(1)}, u32[]{:S(2)}, u32[]{:S(2)}) collective-permute-start(f32[1,64,4096]{2,1,0:T(8,128)} %param.2), channel_id=1, source_target_pairs={{0,1},{1,2},{2,3},{3,4},{4,5},{5,6},{6,7},{7,8},{8,9},{9,10},{10,1... | collective-permute-start | bytes 3145736 | tf_op jit(solution)/shard_map/ppermute | solution.py:15
  32.4 30.1 %copy-start.8 = (f32[1,64,4096]{2,1,0:T(8,128)}, f32[1,64,4096]{2,1,0:T(8,128)S(1)}, u32[]{:S(2)}) copy-start(f32[1,64,4096]{2,1,0:T(8,128)S(1)} %collective-permute-done.1) | copy-start | bytes 3145732
  32.4 30.0 %collective-permute-start.3 = (f32[1,64,4096]{2,1,0:T(8,128)S(1)}, f32[1,64,4096]{2,1,0:T(8,128)S(1)}, u32[]{:S(2)}, u32[]{:S(2)}) collective-permute-start(f32[1,64,4096]{2,1,0:T(8,128)S(1)} %collective-permute-done.1), channel_id=1, source_target_pairs={{0,1},{1,2},{2,3},{3,4},{4,5},{5,6},{6,7},{7,8},{8,9},{9,10},{10,1... | collective-permute-start | bytes 3145736 | tf_op jit(solution)/shard_map/ppermute | solution.py:15
  62.5 2.8 copy-start.10
  120.8 11.3 %copy-start = (f32[1,64,4096]{2,1,0:T(8,128)S(1)}, f32[1,64,4096]{2,1,0:T(8,128)}, u32[]{:S(2)}) copy-start(f32[1,64,4096]{2,1,0:T(8,128)} %param.2) | copy-start | bytes 3145732
  134.6 32.1 %collective-permute-start.5 = (f32[1,64,4096]{2,1,0:T(8,128)}, f32[1,64,4096]{2,1,0:T(8,128)}, u32[]{:S(2)}, u32[]{:S(2)}) collective-permute-start(f32[1,64,4096]{2,1,0:T(8,128)} %copy-done.10), channel_id=1, source_target_pairs={{0,1},{1,2},{2,3},{3,4},{4,5},{5,6},{6,7},{7,8},{8,9},{9,10},{10,1... | collective-permute-start | bytes 3145736 | tf_op jit(solution)/shard_map/ppermute | solution.py:15
  145.7 56.3 %collective-permute-start.8 = (f32[1,64,4096]{2,1,0:T(8,128)}, f32[1,64,4096]{2,1,0:T(8,128)}, u32[]{:S(2)}, u32[]{:S(2)}) collective-permute-start(f32[1,64,4096]{2,1,0:T(8,128)} %multiply_subtract_fusion.3), channel_id=1, source_target_pairs={{0,1},{1,2},{2,3},{3,4},{4,5},{5,6},{6,7},{7,8},{8,9},{9,10},{10,1... | collective-permute-start | bytes 3145736 | tf_op jit(solution)/shard_map/ppermute | solution.py:15
  166.6 35.4 %collective-permute-start.7 = (f32[1,64,4096]{2,1,0:T(8,128)}, f32[1,64,4096]{2,1,0:T(8,128)}, u32[]{:S(2)}, u32[]{:S(2)}) collective-permute-start(f32[1,64,4096]{2,1,0:T(8,128)} %collective-permute-done.5), channel_id=1, source_target_pairs={{0,32},{32,64},{64,96},{96,0},{1,33},{33,65},{65,97},{97,1},{2,34}... | collective-permute-start | bytes 3145736 | tf_op jit(solution)/shard_map/ppermute | solution.py:15
  262.8 8.4 %copy-start.7 = (f32[1,64,4096]{1,2,0:T(8,128)S(1)}, f32[1,64,4096]{1,2,0:T(8,128)}, u32[]{:S(2)}) copy-start(f32[1,64,4096]{1,2,0:T(8,128)} %copy.107) | copy-start | bytes 3145732
  271.2 31.8 %collective-permute-start.9 = (f32[1,64,4096]{2,1,0:T(8,128)}, f32[1,64,4096]{2,1,0:T(8,128)}, u32[]{:S(2)}, u32[]{:S(2)}) collective-permute-start(f32[1,64,4096]{2,1,0:T(8,128)} %get-tuple-element.6), channel_id=1, source_target_pairs={{0,1},{1,2},{2,3},{3,4},{4,5},{5,6},{6,7},{7,8},{8,9},{9,10},{10,1... | collective-permute-start | bytes 3145736 | tf_op jit(solution)/shard_map/ppermute | solution.py:15
  291.7 11.3 %copy-start.2 = (f32[1,64,4096]{2,1,0:T(8,128)S(1)}, f32[1,64,4096]{2,1,0:T(8,128)}, u32[]{:S(2)}) copy-start(f32[1,64,4096]{2,1,0:T(8,128)} %reshape.412) | copy-start | bytes 3145732
  305.4 35.3 %collective-permute-start.10 = (f32[1,64,4096]{2,1,0:T(8,128)}, f32[1,64,4096]{2,1,0:T(8,128)}, u32[]{:S(2)}, u32[]{:S(2)}) collective-permute-start(f32[1,64,4096]{2,1,0:T(8,128)} %multiply_subtract_fusion.1), channel_id=1, source_target_pairs={{0,32},{32,64},{64,96},{96,0},{1,33},{33,65},{65,97},{97,1},{2,34}... | collective-permute-start | bytes 3145736 | tf_op jit(solution)/shard_map/ppermute | solution.py:15
  337.6 69.2 %copy-start.1 = (f32[1,64,4096]{2,1,0:T(8,128)S(1)}, f32[1,64,4096]{2,1,0:T(8,128)}, u32[]{:S(2)}) copy-start(f32[1,64,4096]{2,1,0:T(8,128)} %reshape.406) | copy-start | bytes 3145732
  337.6 69.2 %copy-start.3 = (f32[1,64,4096]{2,1,0:T(8,128)S(1)}, f32[1,64,4096]{2,1,0:T(8,128)}, u32[]{:S(2)}) copy-start(f32[1,64,4096]{2,1,0:T(8,128)} %reshape.412) | copy-start | bytes 3145732
  340.7 66.1 %copy-start.4 = (f32[1,64,4096]{2,1,0:T(8,128)S(1)}, f32[1,64,4096]{2,1,0:T(8,128)}, u32[]{:S(2)}) copy-start(f32[1,64,4096]{2,1,0:T(8,128)} %reshape.418) | copy-start | bytes 3145732
  340.7 66.1 %copy-start.5 = (f32[1,64,4096]{2,1,0:T(8,128)S(1)}, f32[1,64,4096]{2,1,0:T(8,128)}, u32[]{:S(2)}) copy-start(f32[1,64,4096]{2,1,0:T(8,128)} %reshape.400) | copy-start | bytes 3145732
  340.7 66.1 %copy-start.9 = (f32[1,64,4096]{2,1,0:T(8,128)S(1)}, f32[1,64,4096]{2,1,0:T(8,128)}, u32[]{:S(2)}) copy-start(f32[1,64,4096]{2,1,0:T(8,128)} %copy-done.8) | copy-start | bytes 3145732
  340.7 66.1 %copy-start.11 = (f32[1,64,4096]{2,1,0:T(8,128)S(1)}, f32[1,64,4096]{2,1,0:T(8,128)}, u32[]{:S(2)}) copy-start(f32[1,64,4096]{2,1,0:T(8,128)} %copy-done.10) | copy-start | bytes 3145732
  342.6 14.1 %collective-permute-start.11 = (f32[1,64,4096]{2,1,0:T(8,128)S(1)}, f32[1,64,4096]{2,1,0:T(8,128)S(1)}, u32[]{:S(2)}, u32[]{:S(2)}) collective-permute-start(f32[1,64,4096]{2,1,0:T(8,128)S(1)} %multiply_subtract_fusion), channel_id=1, source_target_pairs={{0,96},{32,0},{64,32},{96,64},{1,97},{33,1},{65,33},{97,65},{2,98}... | collective-permute-start | bytes 3145736 | tf_op jit(solution)/shard_map/ppermute | solution.py:15
  356.7 50.1 %collective-permute-start.12 = (f32[1,64,4096]{2,1,0:T(8,128)S(1)}, f32[1,64,4096]{2,1,0:T(8,128)S(1)}, u32[]{:S(2)}, u32[]{:S(2)}) collective-permute-start(f32[1,64,4096]{2,1,0:T(8,128)S(1)} %collective-permute-done.11), channel_id=1, source_target_pairs={{0,29},{1,30},{2,31},{3,0},{4,1},{5,2},{6,3},{7,4},{8,5},{9,6},{10... | collective-permute-start | bytes 3145736 | tf_op jit(solution)/shard_map/ppermute | solution.py:15
  357.6 26.8 %collective-permute-start = (f32[1]{0:T(128)}, f32[1]{0:T(128)}, u32[]{:S(2)}, u32[]{:S(2)}) collective-permute-start(f32[1]{0:T(128)} %param.3), channel_id=1, source_target_pairs={{0,1},{1,2},{2,3},{3,4},{4,5},{5,6},{6,7},{7,8},{8,9},{9,10},{10,1... | collective-permute-start | bytes 20 | tf_op jit(solution)/shard_map/ppermute | solution.py:15
  384.4 9.6 %collective-permute-start.2 = (f32[1]{0:T(128)}, f32[1]{0:T(128)}, u32[]{:S(2)}, u32[]{:S(2)}) collective-permute-start(f32[1]{0:T(128)} %collective-permute-done), channel_id=1, source_target_pairs={{0,1},{1,2},{2,3},{3,4},{4,5},{5,6},{6,7},{7,8},{8,9},{9,10},{10,1... | collective-permute-start | bytes 20 | tf_op jit(solution)/shard_map/ppermute | solution.py:15
  394.0 9.6 %collective-permute-start.4 = (f32[1]{0:T(128)}, f32[1]{0:T(128)}, u32[]{:S(2)}, u32[]{:S(2)}) collective-permute-start(f32[1]{0:T(128)} %collective-permute-done.2), channel_id=1, source_target_pairs={{0,1},{1,2},{2,3},{3,4},{4,5},{5,6},{6,7},{7,8},{8,9},{9,10},{10,1... | collective-permute-start | bytes 20 | tf_op jit(solution)/shard_map/ppermute | solution.py:15
  403.6 3.2 collective-permute-start.6
  (1 other events, 2.5 us)
where the time goes:
time: 418 us; the launch traced here: 413 us
  matrix products  182 us (44%)
  waiting for transfers between devices  130 us (31%)
  local copies, waits for them, and re-layouts  73 us (17%)
  other arithmetic  20.2 us (5%)
  starting transfers between devices  6.57 us (2%)
    ppermute x13, waiting for transfers between devices, from_behind(): return lax.ppermute(value, axis, pairs)  130 us
    another operation x8, local copies, waits for them, and re-layouts  49.3 us
    dot_general x8, matrix products, complex_along(): return jnp.einsum('rskb,spabc->rpakc', table, field, precision=HIGH)  48.3 us
    dot_general x4, matrix products, complex_along(): return jnp.einsum('rska,spabc->rpkbc', table, field, precision=HIGH)  46.8 us
    dot_general x4, matrix products, solve_pairs(): final = jnp.einsum('skc,spabc->pabk', inverse[0], field, precision=HIGH)  33.6 us
    dot_general x4, matrix products, complex_along(): return jnp.einsum('rskc,spabc->rpabk', table, field, precision=HIGH)  28.8 us
    dot_general x4, matrix products, solve_pairs(): jnp.einsum('rka,pabc->rpkbc', forward[:, 0], density, precision=HIGH)  24.4 us
    reshape x4, local copies, waits for them, and re-layouts, solve_pairs(): return final.reshape(count, count, size, size * size)  12.1 us
  transfers between devices with their start and end apart: 13, of which 9 were waited for; matrix products, arithmetic and copies ran while one was open for 30% of the time, Pallas kernels for 0%

commit v1 on v0

v1 whole, which is shorter than its diff:
```python
import jax
import jax.numpy as jnp
import numpy as np
from jax import lax
from jax.experimental import pallas as pl
from jax.experimental.pallas import tpu as pltpu
from jax.sharding import PartitionSpec as P

SIZE = 64
HALF = 32
ROWS = 36
BF = jnp.bfloat16
F32 = jnp.float32


def two_parts(matrix):
    high = np.asarray(matrix, np.float64).astype(BF)
    low = (np.asarray(matrix, np.float64) - high.astype(np.float64)).astype(BF)
    return high, low


def real_basis(points, freqs, period):
    place = np.arange(points)
    rows, marks = [], []
    for freq in freqs:
        waves = [np.cos(2 * np.pi * freq * place / period)]
        waves.append(np.sin(2 * np.pi * freq * place / period))
        for wave in waves:
            norm = np.sqrt(np.sum(wave * wave))
            if norm > 1e-6:
                rows.append(wave / norm)
                marks.append(freq)
    return np.stack(rows), np.asarray(marks, np.float64)


def left_form(matrix):
    high, low = two_parts(matrix)
    return np.concatenate([high, high, low], axis=1)


def right_form(matrix):
    high, low = two_parts(matrix)
    row = np.concatenate([high, low], axis=1)
    return np.concatenate([row, row], axis=0)


def constants():
    full, marks = real_basis(SIZE, range(HALF + 1), SIZE)
    even, even_marks = real_basis(HALF, range(0, HALF + 1, 2), SIZE)
    odd, odd_marks = real_basis(HALF, range(1, HALF, 2), SIZE)
    mix = np.array([[1.0, 1.0], [1.0, -1.0]]) / np.sqrt(2.0)
    lane = np.kron(mix, full)
    mid_marks = np.stack([even_marks, odd_marks], axis=1)
    total = (
        marks[:, None, None, None] ** 2
        + mid_marks[None, :, :, None] ** 2
        + marks[None, None, None, :] ** 2
    )
    step = 2.0 * np.pi / SIZE
    kernel = (np.pi / (step * step * total + 0.25)).astype(np.float32)
    kernel = kernel.reshape(SIZE * HALF, 2 * SIZE)
    return (
        left_form(full),
        left_form(full.T),
        right_form(lane.T),
        right_form(lane),
        left_form(np.concatenate([even, odd], axis=0)),
        left_form(np.concatenate([even.T, odd.T], axis=0)),
        kernel,
    )


def split(value):
    high = value.astype(BF)
    low = (value - high.astype(F32)).astype(BF)
    return high, low


def along_rows(matrix, value):
    high, low = split(value)
    stack = jnp.concatenate([high, low, high], axis=0)
    return jnp.dot(matrix, stack, preferred_element_type=F32)


def along_lanes(value, matrix):
    high, low = split(value)
    both = jnp.dot(
        jnp.concatenate([high, low], axis=1), matrix, preferred_element_type=F32
    )
    return both[:, :128] + both[:, 128:]


def to_rows(value):
    count = value.shape[1] // 128
    return jnp.concatenate(
        [value[:, n * 128 : (n + 1) * 128] for n in range(count)], axis=0
    )


def to_lanes(value, rows):
    count = value.shape[0] // rows
    return jnp.concatenate(
        [value[n * rows : (n + 1) * rows] for n in range(count)], axis=1
    )


def pick(value):
    lane = lax.broadcasted_iota(jnp.int32, (HALF, value.shape[1]), 1)
    return jnp.where((lane & 127) < SIZE, value[:HALF], value[HALF:])


def forward(left, right, mats, area, tiles=8):
    fa, _, fl, _, _, _, _ = mats
    for base in range(0, HALF, tiles):
        lanes = pl.ds(base * 128, tiles * 128)
        value = along_rows(fa[...], left[:, lanes] * right[:, lanes])
        value = along_lanes(to_rows(value), fl[...])
        for n in range(tiles):
            area[pl.ds(base + n, SIZE, stride=ROWS), :] = value[n * SIZE : (n + 1) * SIZE]


def middle(mats, area, count=8):
    _, _, _, _, fm, bm, kernel = mats
    for base in range(0, SIZE, count):
        value = jnp.concatenate(
            [area[pl.ds((base + n) * ROWS, HALF), :] for n in range(count)], axis=1
        )
        value = pick(along_rows(fm[...], value))
        value = value * to_lanes(kernel[pl.ds(base * HALF, count * HALF), :], HALF)
        value = pick(along_rows(bm[...], value))
        for n in range(count):
            area[pl.ds((base + n) * ROWS, HALF), :] = value[:, n * 128 : (n + 1) * 128]


def backward(mats, area, base, tiles=8):
    _, ba, _, bl, _, _, _ = mats
    value = jnp.concatenate(
        [area[pl.ds(base + n, SIZE, stride=ROWS), :] for n in range(tiles)], axis=0
    )
    value = along_lanes(value, bl[...])
    return along_rows(ba[...], to_lanes(value, SIZE))


def pack_body(occ, orb, out):
    scale = jnp.sqrt(jnp.full((1, 128), occ[0], F32))
    low = lax.broadcasted_iota(jnp.int32, (SIZE, 128), 1) < SIZE
    for n in range(HALF // 2):
        first = orb[:, n * 128 : (n + 1) * 128] * scale
        second = orb[:, (n + 16) * 128 : (n + 17) * 128] * scale
        even = jnp.where(low, first, pltpu.roll(second, SIZE, 1))
        odd = jnp.where(low, pltpu.roll(first, SIZE, 1), second)
        out[:, 2 * n * 128 : (2 * n + 1) * 128] = even
        out[:, (2 * n + 1) * 128 : (2 * n + 2) * 128] = odd


def unpack_body(occ, one, two, three, out):
    scale = -lax.rsqrt(jnp.full((1, 128), occ[0], F32))
    low = lax.broadcasted_iota(jnp.int32, (SIZE, 128), 1) < SIZE
    for n in range(HALF // 2):
        parts = []
        for m in (2 * n, 2 * n + 1):
            lanes = slice(m * 128, (m + 1) * 128)
            parts.append((one[:, lanes] + two[:, lanes] + three[:, lanes]) * scale)
        even, odd = parts
        out[:, n * 128 : (n + 1) * 128] = jnp.where(low, even, pltpu.roll(odd, SIZE, 1))
        out[:, (n + 16) * 128 : (n + 17) * 128] = jnp.where(
            low, pltpu.roll(even, SIZE, 1), odd
        )


SHAPE = jax.ShapeDtypeStruct((SIZE, SIZE * SIZE), F32)
SMEM = pl.BlockSpec(memory_space=pltpu.SMEM)
VMEM = pl.BlockSpec(memory_space=pltpu.VMEM)
COST = 2 * 6 * SIZE**4 * 200


def call(body, name, outs, scratch=(), work=1, first=VMEM, count=1, limit=20):
    return pl.pallas_call(
        body,
        out_shape=[SHAPE] * outs,
        in_specs=[first] + [VMEM] * (count - 1),
        out_specs=[VMEM] * outs,
        scratch_shapes=list(scratch),
        cost_estimate=pl.CostEstimate(
            flops=work * COST, bytes_accessed=1 << 20, transcendentals=0
        ),
        compiler_params=pltpu.CompilerParams(vmem_limit_bytes=limit << 20),
        name=name,
    )


def three_body(left, home, right, *rest):
    mats, outs, area = rest[:7], rest[7:10], rest[10]
    refs = (left, home, right)
    fresh = [True] * 3
    for one, two in ((1, 2), (0, 1), (0, 2)):
        forward(refs[one], refs[two], mats, area)
        middle(mats, area)
        for base in range(0, HALF, 8):
            value = backward(mats, area, base)
            lanes = pl.ds(base * 128, 1024)
            for own, other in ((one, two), (two, one)):
                term = value * refs[other][:, lanes]
                if fresh[own]:
                    outs[own][:, lanes] = term
                else:
                    outs[own][:, lanes] += term
        fresh[one] = fresh[two] = False


def last_body(left, far, acc, *rest):
    mats, outs, area = rest[:7], rest[7:9], rest[9]
    forward(left, far, mats, area)
    middle(mats, area)
    for base in range(0, HALF, 8):
        value = backward(mats, area, base)
        lanes = pl.ds(base * 128, 1024)
        outs[0][:, lanes] = acc[:, lanes] + value * far[:, lanes]
        outs[1][:, lanes] = value * left[:, lanes]


def shift(value, axis, steps):
    count = lax.axis_size(axis)
    pairs = [(source, (source + steps) % count) for source in range(count)]
    return lax.ppermute(value, axis, pairs)


def local(orbitals, occupation):
    mats = [jnp.asarray(item) for item in constants()]
    area = [pltpu.VMEM((SIZE * ROWS, 128), F32)]
    home = call(pack_body, "pack", 1, first=SMEM, count=2, work=0)(
        occupation, orbitals[0]
    )[0]
    left = shift(home, "blk", -1)
    right = shift(home, "blk", 2)
    far = shift(right, "group", 1)
    acc_left, acc_home, acc_right = call(three_body, "three", 3, area, 3, count=10)(
        left, home, right, *mats
    )
    acc_left, acc_far = call(last_body, "last", 2, area, 1, count=10)(
        left, far, acc_left, *mats
    )
    from_far = shift(acc_far, "group", -1)
    from_left = shift(acc_left, "blk", 1)
    from_right = shift(acc_right + from_far, "blk", -2)
    out = call(unpack_body, "unpack", 1, first=SMEM, count=4, work=0)(
        occupation, acc_home, from_left, from_right
    )[0]
    return out[None]


def solution(mesh):
    spec = P(("group", "blk"))
    return jax.shard_map(
        local,
        mesh=mesh,
        in_specs=(P(("group", "blk"), None, None), spec),
        out_specs=P(("group", "blk"), None, None),
        check_vma=False,
    )
```

time: 418 us -> 102 us (0.24)
  the two profiles are of different devices: /device:TPU:0 before, /device:TPU:5 now
where the time goes in v1:
time: 102 us
  waiting for transfers between devices  75.7 us (74%)
  Pallas kernels  16 us (16%)
  starting transfers between devices  8.13 us (8%)
  local copies, waits for them, and re-layouts  1.25 us (1%)
    ppermute x6, waiting for transfers between devices, shift(): return lax.ppermute(value, axis, pairs)  75.7 us
    pallas_call x1, Pallas kernels, local(): call(three_body, 'three', 3, area, 3, count=10)(left, home, right, *mats)  10.7 us
    ppermute x6, starting transfers between devices, shift(): return lax.ppermute(value, axis, pairs)  8.13 us
    pallas_call x1, Pallas kernels, local(): call(last_body, 'last', 2, area, 1, count=10)(left, far, acc_left, *mats)  3.64 us
  transfers between devices with their start and end apart: 6, of which 4 were waited for; matrix products, arithmetic and copies ran while one was open for 0% of the time, Pallas kernels for 10%

profile of v1, /device:TPU:5, one launch (start us, length us, event | category | flops | bytes accessed | tf_op | source)
XLA Modules:
  0.0 101.9 jit_solution(12609093130571592851)
XLA Ops:
  0.7 0.0 copy-start
  0.7 1.2 %copy-done = f32[1,64,4096]{2,1,0:T(8,128)S(1)} copy-done((f32[1,64,4096]{2,1,0:T(8,128)S(1)}, f32[1,64,4096]{2,1,0:T(8,128)}, u32[]{:S(2)}) %copy-start) | copy-done | bytes 1048600
  1.9 0.0 copy-start.5
  1.9 0.0 copy-start.6
  1.9 0.0 copy-start.7
  1.9 0.3 pack.1.home
  2.3 1.7 %collective-permute-start.1 = (f32[64,4096]{1,0:T(8,128)S(1)}, f32[64,4096]{1,0:T(8,128)S(1)}, u32[]{:S(2)}, u32[]{:S(2)}) collective-permute-start(f32[64,4096]{1,0:T(8,128)S(1)} %pack.1.home), channel_id=1, source_target_pairs={{0,2},{1,3},{2,4},{3,5},{4,6},{5,7},{6,8},{7,9},{8,10},{9,11},{10,... | collective-permute-start | bytes 3145736 | tf_op jit(solution)/shard_map/ppermute | solution.py:225
  4.0 0.2 collective-permute-start
  4.2 27.2 %collective-permute-done.1.right = f32[64,4096]{1,0:T(8,128)S(1)} collective-permute-done((f32[64,4096]{1,0:T(8,128)S(1)}, f32[64,4096]{1,0:T(8,128)S(1)}, u32[]{:S(2)}, u32[]{:S(2)}) %collective-permute-start.1) | collective-permute-done | bytes 1048608 | tf_op jit(solution)/shard_map/ppermute | solution.py:225
  31.4 2.1 %collective-permute-start.2 = (f32[64,4096]{1,0:T(8,128)S(1)}, f32[64,4096]{1,0:T(8,128)S(1)}, u32[]{:S(2)}, u32[]{:S(2)}) collective-permute-start(f32[64,4096]{1,0:T(8,128)S(1)} %collective-permute-done.1.right), channel_id=1, source_target_pairs={{0,32},{32,64},{64,96},{96,0},{1,33},{33,65},{65,97},{97,1},{2,34}... | collective-permute-start | bytes 3145736 | tf_op jit(solution)/shard_map/ppermute | solution.py:225
  33.5 0.0 collective-permute-done.left
  33.5 0.0 copy-done.1
  33.5 0.0 copy-done.2
  33.5 10.7 %three.1 = (f32[64,4096]{1,0:T(8,128)S(1)}, f32[64,4096]{1,0:T(8,128)S(1)}, f32[64,4096]{1,0:T(8,128)S(1)}) custom-call(f32[64,4096]{1,0:T(8,128)S(1)} %collective-permute-done.left, f32[64,4096]{1,0:T(8,128)S(1)} %pack.1.home, f32[64,4096]{1,0:T(8,128)S(1)} %collective-permute-done.1.right, bf16[64,192]{1,0:T(8,128)(2,1)S(1)} %copy-done.5, ...), custom_call_target="tpu_custom_call" | custom-call | flops 120795955200 | bytes 1048576 | tf_op jit(solution)/shard_map/three/pallas_call | solution.py:237
  44.2 1.0 collective-permute-done.2.far
  45.2 3.6 %last.1 = (f32[64,4096]{1,0:T(8,128)S(1)}, f32[64,4096]{1,0:T(8,128)S(1)}) custom-call(f32[64,4096]{1,0:T(8,128)S(1)} %collective-permute-done.left, f32[64,4096]{1,0:T(8,128)S(1)} %collective-permute-done.2.far, f32[64,4096]{1,0:T(8,128)S(1)} %get-tuple-element.11.acc, bf16[64,192]{1,0:T(8,128)(2,1)S(1)} %copy-done.5, bf16[64,192]{1,0:T(8,128)(2,1)S(1)} %copy-done.4, ...), custom_call_target="tpu_custom_call" | custom-call | flops 40265318400 | bytes 1048576 | tf_op jit(solution)/shard_map/last/pallas_call | solution.py:240
  48.9 1.7 %collective-permute-start.4 = (f32[64,4096]{1,0:T(8,128)S(1)}, f32[64,4096]{1,0:T(8,128)S(1)}, u32[]{:S(2)}, u32[]{:S(2)}) collective-permute-start(f32[64,4096]{1,0:T(8,128)S(1)} %get-tuple-element.14), channel_id=1, source_target_pairs={{0,96},{32,0},{64,32},{96,64},{1,97},{33,1},{65,33},{97,65},{2,98}... | collective-permute-start | bytes 3145736 | tf_op jit(solution)/shard_map/ppermute | solution.py:225
  50.6 0.0 collective-permute-start.3
  50.6 24.6 %collective-permute-done.4 = f32[64,4096]{1,0:T(8,128)S(1)} collective-permute-done((f32[64,4096]{1,0:T(8,128)S(1)}, f32[64,4096]{1,0:T(8,128)S(1)}, u32[]{:S(2)}, u32[]{:S(2)}) %collective-permute-start.4) | collective-permute-done | bytes 1048608 | tf_op jit(solution)/shard_map/ppermute | solution.py:225
  75.2 0.1 add.3
  75.3 2.4 %collective-permute-start.5 = (f32[64,4096]{1,0:T(8,128)S(1)}, f32[64,4096]{1,0:T(8,128)S(1)}, u32[]{:S(2)}, u32[]{:S(2)}) collective-permute-start(f32[64,4096]{1,0:T(8,128)S(1)} %add.3), channel_id=1, source_target_pairs={{0,30},{1,31},{2,0},{3,1},{4,2},{5,3},{6,4},{7,5},{8,6},{9,7},{10,... | collective-permute-start | bytes 3145736 | tf_op jit(solution)/shard_map/ppermute | solution.py:225
  77.7 0.0 collective-permute-done.3.two
  77.8 22.9 %collective-permute-done.5.three = f32[64,4096]{1,0:T(8,128)S(1)} collective-permute-done((f32[64,4096]{1,0:T(8,128)S(1)}, f32[64,4096]{1,0:T(8,128)S(1)}, u32[]{:S(2)}, u32[]{:S(2)}) %collective-permute-start.5) | collective-permute-done | bytes 1048608 | tf_op jit(solution)/shard_map/ppermute | solution.py:225
  100.6 1.3 %unpack.1 = f32[64,4096]{1,0:T(8,128)} custom-call(f32[1]{0:T(128)S(6)} %copy.10.occ, f32[64,4096]{1,0:T(8,128)S(1)} %get-tuple-element.10.one, f32[64,4096]{1,0:T(8,128)S(1)} %collective-permute-done.3.two, f32[64,4096]{1,0:T(8,128)S(1)} %collective-permute-done.5.three), custom_call_target="tpu_custom_call" | custom-call | bytes 1048576 | tf_op jit(solution)/shard_map/unpack/pallas_call | solution.py:246
  (9 shorter events, 0.0 us)
Async XLA Ops:
  0.7 1.2 %copy-start = (f32[1,64,4096]{2,1,0:T(8,128)S(1)}, f32[1,64,4096]{2,1,0:T(8,128)}, u32[]{:S(2)}) copy-start(f32[1,64,4096]{2,1,0:T(8,128)} %param.9) | copy-start | bytes 3145732
  1.9 31.6 %copy-start.1 = (f32[2048,128]{1,0:T(8,128)S(1)}, f32[2048,128]{1,0:T(8,128)}, u32[]{:S(2)}) copy-start(f32[2048,128]{1,0:T(8,128)} %constant.20.clone.rest_6_) | copy-start | bytes 3145732
  1.9 31.6 %copy-start.2 = (bf16[256,256]{1,0:T(8,128)(2,1)S(1)}, bf16[256,256]{1,0:T(8,128)(2,1)}, u32[]{:S(2)}) copy-start(bf16[256,256]{1,0:T(8,128)(2,1)} %constant.17.clone.rest_3_) | copy-start | bytes 393220
  1.9 31.6 %copy-start.3 = (bf16[256,256]{1,0:T(8,128)(2,1)S(1)}, bf16[256,256]{1,0:T(8,128)(2,1)}, u32[]{:S(2)}) copy-start(bf16[256,256]{1,0:T(8,128)(2,1)} %constant.16.clone.rest_2_) | copy-start | bytes 393220
  1.9 31.6 %copy-start.4 = (bf16[64,192]{1,0:T(8,128)(2,1)S(1)}, bf16[64,192]{1,0:T(8,128)(2,1)}, u32[]{:S(2)}) copy-start(bf16[64,192]{1,0:T(8,128)(2,1)} %constant.15.clone.rest_1_) | copy-start | bytes 73732
  1.9 31.6 %copy-start.5 = (bf16[64,192]{1,0:T(8,128)(2,1)S(1)}, bf16[64,192]{1,0:T(8,128)(2,1)}, u32[]{:S(2)}) copy-start(bf16[64,192]{1,0:T(8,128)(2,1)} %constant.14.clone.rest_0_) | copy-start | bytes 73732
  1.9 31.6 %copy-start.6 = (bf16[64,96]{1,0:T(8,128)(2,1)S(1)}, bf16[64,96]{1,0:T(8,128)(2,1)}, u32[]{:S(2)}) copy-start(bf16[64,96]{1,0:T(8,128)(2,1)} %constant.19.clone.rest_5_) | copy-start | bytes 36868
  1.9 31.6 %copy-start.7 = (bf16[64,96]{1,0:T(8,128)(2,1)S(1)}, bf16[64,96]{1,0:T(8,128)(2,1)}, u32[]{:S(2)}) copy-start(bf16[64,96]{1,0:T(8,128)(2,1)} %constant.18.clone.rest_4_) | copy-start | bytes 36868
  2.3 29.1 %collective-permute-start.1 = (f32[64,4096]{1,0:T(8,128)S(1)}, f32[64,4096]{1,0:T(8,128)S(1)}, u32[]{:S(2)}, u32[]{:S(2)}) collective-permute-start(f32[64,4096]{1,0:T(8,128)S(1)} %pack.1.home), channel_id=1, source_target_pairs={{0,2},{1,3},{2,4},{3,5},{4,6},{5,7},{6,8},{7,9},{8,10},{9,11},{10,... | collective-permute-start | bytes 3145736 | tf_op jit(solution)/shard_map/ppermute | solution.py:225
  4.0 29.5 %collective-permute-start = (f32[64,4096]{1,0:T(8,128)S(1)}, f32[64,4096]{1,0:T(8,128)S(1)}, u32[]{:S(2)}, u32[]{:S(2)}) collective-permute-start(f32[64,4096]{1,0:T(8,128)S(1)} %pack.1.home), channel_id=1, source_target_pairs={{0,31},{1,0},{2,1},{3,2},{4,3},{5,4},{6,5},{7,6},{8,7},{9,8},{10,9... | collective-permute-start | bytes 3145736 | tf_op jit(solution)/shard_map/ppermute | solution.py:225
  31.4 13.8 %collective-permute-start.2 = (f32[64,4096]{1,0:T(8,128)S(1)}, f32[64,4096]{1,0:T(8,128)S(1)}, u32[]{:S(2)}, u32[]{:S(2)}) collective-permute-start(f32[64,4096]{1,0:T(8,128)S(1)} %collective-permute-done.1.right), channel_id=1, source_target_pairs={{0,32},{32,64},{64,96},{96,0},{1,33},{33,65},{65,97},{97,1},{2,34}... | collective-permute-start | bytes 3145736 | tf_op jit(solution)/shard_map/ppermute | solution.py:225
  48.9 26.4 %collective-permute-start.4 = (f32[64,4096]{1,0:T(8,128)S(1)}, f32[64,4096]{1,0:T(8,128)S(1)}, u32[]{:S(2)}, u32[]{:S(2)}) collective-permute-start(f32[64,4096]{1,0:T(8,128)S(1)} %get-tuple-element.14), channel_id=1, source_target_pairs={{0,96},{32,0},{64,32},{96,64},{1,97},{33,1},{65,33},{97,65},{2,98}... | collective-permute-start | bytes 3145736 | tf_op jit(solution)/shard_map/ppermute | solution.py:225
  50.6 27.1 %collective-permute-start.3 = (f32[64,4096]{1,0:T(8,128)S(1)}, f32[64,4096]{1,0:T(8,128)S(1)}, u32[]{:S(2)}, u32[]{:S(2)}) collective-permute-start(f32[64,4096]{1,0:T(8,128)S(1)} %get-tuple-element.12), channel_id=1, source_target_pairs={{0,1},{1,2},{2,3},{3,4},{4,5},{5,6},{6,7},{7,8},{8,9},{9,10},{10,1... | collective-permute-start | bytes 3145736 | tf_op jit(solution)/shard_map/ppermute | solution.py:225
  75.3 25.3 %collective-permute-start.5 = (f32[64,4096]{1,0:T(8,128)S(1)}, f32[64,4096]{1,0:T(8,128)S(1)}, u32[]{:S(2)}, u32[]{:S(2)}) collective-permute-start(f32[64,4096]{1,0:T(8,128)S(1)} %add.3), channel_id=1, source_target_pairs={{0,30},{1,31},{2,0},{3,1},{4,2},{5,3},{6,4},{7,5},{8,6},{9,7},{10,... | collective-permute-start | bytes 3145736 | tf_op jit(solution)/shard_map/ppermute | solution.py:225

commit v2 on v1

--- a/solution.py
+++ b/solution.py
@@ -109,11 +109,21 @@
     return jnp.where((lane & 127) < SIZE, value[:HALF], value[HALF:])
 
 
+def take(refs, lanes):
+    parts = [ref[:, lanes] for ref in refs]
+    return parts[0] if len(parts) == 1 else jnp.concatenate(parts, axis=0)
+
+
+def put(refs, lanes, value):
+    refs[0][:, lanes] = value[:HALF]
+    refs[1][:, lanes] = value[HALF:]
+
+
 def forward(left, right, mats, area, tiles=8):
     fa, _, fl, _, _, _, _ = mats
     for base in range(0, HALF, tiles):
         lanes = pl.ds(base * 128, tiles * 128)
-        value = along_rows(fa[...], left[:, lanes] * right[:, lanes])
+        value = along_rows(fa[...], take(left, lanes) * take(right, lanes))
         value = along_lanes(to_rows(value), fl[...])
         for n in range(tiles):
             area[pl.ds(base + n, SIZE, stride=ROWS), :] = value[n * SIZE : (n + 1) * SIZE]
@@ -140,8 +150,7 @@
     value = along_lanes(value, bl[...])
     return along_rows(ba[...], to_lanes(value, SIZE))
 
-
-def pack_body(occ, orb, out):
+def pack_body(occ, orb, out, top, bottom):
     scale = jnp.sqrt(jnp.full((1, 128), occ[0], F32))
     low = lax.broadcasted_iota(jnp.int32, (SIZE, 128), 1) < SIZE
     for n in range(HALF // 2):
@@ -149,18 +158,22 @@
         second = orb[:, (n + 16) * 128 : (n + 17) * 128] * scale
         even = jnp.where(low, first, pltpu.roll(second, SIZE, 1))
         odd = jnp.where(low, pltpu.roll(first, SIZE, 1), second)
-        out[:, 2 * n * 128 : (2 * n + 1) * 128] = even
-        out[:, (2 * n + 1) * 128 : (2 * n + 2) * 128] = odd
-
-
-def unpack_body(occ, one, two, three, out):
+        for m, value in ((2 * n, even), (2 * n + 1, odd)):
+            lanes = slice(m * 128, (m + 1) * 128)
+            out[:, lanes] = value
+            top[:, lanes] = value[:HALF]
+            bottom[:, lanes] = value[HALF:]
+
+
+def unpack_body(occ, one, two, top, bottom, out):
     scale = -lax.rsqrt(jnp.full((1, 128), occ[0], F32))
     low = lax.broadcasted_iota(jnp.int32, (SIZE, 128), 1) < SIZE
     for n in range(HALF // 2):
         parts = []
         for m in (2 * n, 2 * n + 1):
             lanes = slice(m * 128, (m + 1) * 128)
-            parts.append((one[:, lanes] + two[:, lanes] + three[:, lanes]) * scale)
+            three = take((top, bottom), lanes)
+            parts.append((one[:, lanes] + two[:, lanes] + three) * scale)
         even, odd = parts
         out[:, n * 128 : (n + 1) * 128] = jnp.where(low, even, pltpu.roll(odd, SIZE, 1))
         out[:, (n + 16) * 128 : (n + 17) * 128] = jnp.where(
@@ -168,55 +181,72 @@
         )
 
 
-SHAPE = jax.ShapeDtypeStruct((SIZE, SIZE * SIZE), F32)
+WHOLE = jax.ShapeDtypeStruct((SIZE, SIZE * SIZE), F32)
+PART = jax.ShapeDtypeStruct((HALF, SIZE * SIZE), F32)
 SMEM = pl.BlockSpec(memory_space=pltpu.SMEM)
 VMEM = pl.BlockSpec(memory_space=pltpu.VMEM)
 COST = 2 * 6 * SIZE**4 * 200
-
-
-def call(body, name, outs, scratch=(), work=1, first=VMEM, count=1, limit=20):
+AREA = pltpu.VMEM((SIZE * ROWS, 128), F32)
+
+
+def call(body, name, count, outs, scratch=(), work=0, first=VMEM):
     return pl.pallas_call(
         body,
-        out_shape=[SHAPE] * outs,
+        out_shape=list(outs),
         in_specs=[first] + [VMEM] * (count - 1),
-        out_specs=[VMEM] * outs,
+        out_specs=[VMEM] * len(outs),
         scratch_shapes=list(scratch),
         cost_estimate=pl.CostEstimate(
             flops=work * COST, bytes_accessed=1 << 20, transcendentals=0
         ),
-        compiler_params=pltpu.CompilerParams(vmem_limit_bytes=limit << 20),
+        compiler_params=pltpu.CompilerParams(vmem_limit_bytes=20 << 20),
         name=name,
     )
 
 
-def three_body(left, home, right, *rest):
-    mats, outs, area = rest[:7], rest[7:10], rest[10]
-    refs = (left, home, right)
-    fresh = [True] * 3
-    for one, two in ((1, 2), (0, 1), (0, 2)):
-        forward(refs[one], refs[two], mats, area)
-        middle(mats, area)
-        for base in range(0, HALF, 8):
-            value = backward(mats, area, base)
-            lanes = pl.ds(base * 128, 1024)
-            for own, other in ((one, two), (two, one)):
-                term = value * refs[other][:, lanes]
-                if fresh[own]:
-                    outs[own][:, lanes] = term
-                else:
-                    outs[own][:, lanes] += term
-        fresh[one] = fresh[two] = False
-
-
-def last_body(left, far, acc, *rest):
-    mats, outs, area = rest[:7], rest[7:9], rest[9]
-    forward(left, far, mats, area)
+def edge(one, two, mats, area, finish):
+    forward(one, two, mats, area)
     middle(mats, area)
     for base in range(0, HALF, 8):
         value = backward(mats, area, base)
         lanes = pl.ds(base * 128, 1024)
-        outs[0][:, lanes] = acc[:, lanes] + value * far[:, lanes]
-        outs[1][:, lanes] = value * left[:, lanes]
+        finish(lanes, value * take(two, lanes), value * take(one, lanes))
+
+
+def right_body(home, top, bottom, *rest):
+    mats, (home_out, top_out, bottom_out, area) = rest[:7], rest[7:]
+
+    def finish(lanes, first, second):
+        home_out[:, lanes] = first
+        put((top_out, bottom_out), lanes, second)
+
+    edge((home,), (top, bottom), mats, area, finish)
+
+
+def far_body(left, top, bottom, *rest):
+    mats, (left_out, top_out, bottom_out, area) = rest[:7], rest[7:]
+
+    def finish(lanes, first, second):
+        left_out[:, lanes] = first
+        put((top_out, bottom_out), lanes, second)
+
+    edge((left,), (top, bottom), mats, area, finish)
+
+
+def left_body(left, home, top, bottom, left_in, home_in, top_in, bottom_in, *rest):
+    mats, outs = rest[:7], rest[7:]
+    left_out, home_out, top_out, bottom_out, area = outs
+
+    def finish_home(lanes, first, second):
+        left_out[:, lanes] = left_in[:, lanes] + first
+        home_out[:, lanes] = home_in[:, lanes] + second
+
+    def finish_right(lanes, first, second):
+        left_out[:, lanes] += first
+        put((top_out, bottom_out), lanes, take((top_in, bottom_in), lanes) + second)
+
+    edge((left,), (home,), mats, area, finish_home)
+    edge((left,), (top, bottom), mats, area, finish_right)
 
 
 def shift(value, axis, steps):
@@ -227,24 +257,29 @@
 
 def local(orbitals, occupation):
     mats = [jnp.asarray(item) for item in constants()]
-    area = [pltpu.VMEM((SIZE * ROWS, 128), F32)]
-    home = call(pack_body, "pack", 1, first=SMEM, count=2, work=0)(
+    pair = [WHOLE, PART, PART]
+    home, top, bottom = call(pack_body, "pack", 2, pair, first=SMEM)(
         occupation, orbitals[0]
-    )[0]
+    )
+    right = [shift(part, "blk", 2) for part in (top, bottom)]
     left = shift(home, "blk", -1)
-    right = shift(home, "blk", 2)
-    far = shift(right, "group", 1)
-    acc_left, acc_home, acc_right = call(three_body, "three", 3, area, 3, count=10)(
-        left, home, right, *mats
-    )
-    acc_left, acc_far = call(last_body, "last", 2, area, 1, count=10)(
-        left, far, acc_left, *mats
-    )
-    from_far = shift(acc_far, "group", -1)
+    far = [shift(part, "group", 1) for part in right]
+    acc_home, *acc_right = call(right_body, "right", 10, pair, [AREA], 1)(
+        home, *right, *mats
+    )
+    acc_left, *acc_far = call(far_body, "far", 10, pair, [AREA], 1)(
+        left, *far, *mats
+    )
+    from_far = [shift(part, "group", -1) for part in acc_far]
+    acc_left, acc_home, *acc_right = call(
+        left_body, "left", 15, [WHOLE, WHOLE, PART, PART], [AREA], 2
+    )(left, home, *right, acc_left, acc_home, *acc_right, *mats)
     from_left = shift(acc_left, "blk", 1)
-    from_right = shift(acc_right + from_far, "blk", -2)
-    out = call(unpack_body, "unpack", 1, first=SMEM, count=4, work=0)(
-        occupation, acc_home, from_left, from_right
+    from_right = [
+        shift(one + two, "blk", -2) for one, two in zip(acc_right, from_far)
+    ]
+    out = call(unpack_body, "unpack", 5, [WHOLE], first=SMEM)(
+        occupation, acc_home, from_left, *from_right
     )[0]
     return out[None]
 

time: 102 us -> 90.6 us (0.89)
  the two profiles are of different devices: /device:TPU:5 before, /device:TPU:0 now
where the time goes in v2:
time: 90.6 us; the launch traced here: 90.2 us
  waiting for transfers between devices  52.9 us (58%)
  Pallas kernels  16.2 us (18%)
  starting transfers between devices  14.3 us (16%)
  local copies, waits for them, and re-layouts  5.98 us (7%)
    ppermute x10, waiting for transfers between devices, shift(): return lax.ppermute(value, axis, pairs)  52.9 us
    ppermute x10, starting transfers between devices, shift(): return lax.ppermute(value, axis, pairs)  14.3 us
    pallas_call x1, Pallas kernels, local(): call(left_body, 'left', 15, [WHOLE, WHOLE, PART, PART], [AREA], 2)  7.18 us
    unnamed x16, local copies, waits for them, and re-layouts  5.98 us
    pallas_call x1, Pallas kernels, local(): call(far_body, 'far', 10, pair, [AREA], 1)(left, *far, *mats)  3.64 us
    pallas_call x1, Pallas kernels, local(): call(right_body, 'right', 10, pair, [AREA], 1)(home, *right, *mats)  3.63 us
  transfers between devices with their start and end apart: 10, of which 8 were waited for; matrix products, arithmetic and copies ran while one was open for 0% of the time, Pallas kernels for 12%

profile of v2, /device:TPU:0, one launch (start us, length us, event | category | flops | bytes accessed | tf_op | source)
XLA Modules:
  0.0 90.2 jit_solution(9194132764488709563)
XLA Ops:
  0.7 1.2 %copy-done = f32[1,64,4096]{2,1,0:T(8,128)S(1)} copy-done((f32[1,64,4096]{2,1,0:T(8,128)S(1)}, f32[1,64,4096]{2,1,0:T(8,128)}, u32[]{:S(2)}) %copy-start) | copy-done | bytes 1048600
  2.3 2.1 %collective-permute-start.1 = (f32[32,4096]{1,0:T(8,128)S(1)}, f32[32,4096]{1,0:T(8,128)S(1)}, u32[]{:S(2)}, u32[]{:S(2)}) collective-permute-start(f32[32,4096]{1,0:T(8,128)S(1)} %get-tuple-element.19), channel_id=1, source_target_pairs={{0,2},{1,3},{2,4},{3,5},{4,6},{5,7},{6,8},{7,9},{8,10},{9,11},{10,... | collective-permute-start | bytes 1572872 | tf_op jit(solution)/shard_map/ppermute | solution.py:255
  4.4 1.9 %collective-permute-start.2 = (f32[32,4096]{1,0:T(8,128)S(1)}, f32[32,4096]{1,0:T(8,128)S(1)}, u32[]{:S(2)}, u32[]{:S(2)}) collective-permute-start(f32[32,4096]{1,0:T(8,128)S(1)} %get-tuple-element.20), channel_id=1, source_target_pairs={{0,2},{1,3},{2,4},{3,5},{4,6},{5,7},{6,8},{7,9},{8,10},{9,11},{10,... | collective-permute-start | bytes 1572872 | tf_op jit(solution)/shard_map/ppermute | solution.py:255
  6.3 5.9 %collective-permute-start = (f32[64,4096]{1,0:T(8,128)S(1)}, f32[64,4096]{1,0:T(8,128)S(1)}, u32[]{:S(2)}, u32[]{:S(2)}) collective-permute-start(f32[64,4096]{1,0:T(8,128)S(1)} %get-tuple-element.18.home), channel_id=1, source_target_pairs={{0,31},{1,0},{2,1},{3,2},{4,3},{5,4},{6,5},{7,6},{8,7},{9,8},{10,9... | collective-permute-start | bytes 3145736 | tf_op jit(solution)/shard_map/ppermute | solution.py:255
  12.2 9.5 %collective-permute-done.1.top = f32[32,4096]{1,0:T(8,128)S(1)} collective-permute-done((f32[32,4096]{1,0:T(8,128)S(1)}, f32[32,4096]{1,0:T(8,128)S(1)}, u32[]{:S(2)}, u32[]{:S(2)}) %collective-permute-start.1) | collective-permute-done | bytes 524320 | tf_op jit(solution)/shard_map/ppermute | solution.py:255
  21.7 10.4 %collective-permute-done.2.bottom = f32[32,4096]{1,0:T(8,128)S(1)} collective-permute-done((f32[32,4096]{1,0:T(8,128)S(1)}, f32[32,4096]{1,0:T(8,128)S(1)}, u32[]{:S(2)}, u32[]{:S(2)}) %collective-permute-start.2) | collective-permute-done | bytes 524320 | tf_op jit(solution)/shard_map/ppermute | solution.py:255
  32.1 0.9 copy-done.2
  33.0 0.9 %copy-done.3 = bf16[256,256]{1,0:T(8,128)(2,1)S(1)} copy-done((bf16[256,256]{1,0:T(8,128)(2,1)S(1)}, bf16[256,256]{1,0:T(8,128)(2,1)}, u32[]{:S(2)}) %copy-start.3) | copy-done | bytes 131096
  33.9 0.8 copy-done.4
  34.7 0.8 copy-done.5
  35.4 0.7 copy-done.6
  36.1 0.7 copy-done.7
  36.9 3.6 %right.1 = (f32[64,4096]{1,0:T(8,128)S(1)}, f32[32,4096]{1,0:T(8,128)S(1)}, f32[32,4096]{1,0:T(8,128)S(1)}) custom-call(f32[64,4096]{1,0:T(8,128)S(1)} %get-tuple-element.18.home, f32[32,4096]{1,0:T(8,128)S(1)} %collective-permute-done.1.top, f32[32,4096]{1,0:T(8,128)S(1)} %collective-permute-done.2.bottom, bf16[64,192]{1,0:T(8,128)(2,1)S(1)} %copy-done.5, ...), custom_call_target="tpu_custom_call" | custom-call | flops 40265318400 | bytes 1048576 | tf_op jit(solution)/shard_map/right/pallas_call | solution.py:267
  40.7 5.6 %collective-permute-done.4.bottom = f32[32,4096]{1,0:T(8,128)S(1)} collective-permute-done((f32[32,4096]{1,0:T(8,128)S(1)}, f32[32,4096]{1,0:T(8,128)S(1)}, u32[]{:S(2)}, u32[]{:S(2)}) %collective-permute-start.4) | collective-permute-done | bytes 524320 | tf_op jit(solution)/shard_map/ppermute | solution.py:255
  46.3 3.6 %far.1 = (f32[64,4096]{1,0:T(8,128)S(1)}, f32[32,4096]{1,0:T(8,128)S(1)}, f32[32,4096]{1,0:T(8,128)S(1)}) custom-call(f32[64,4096]{1,0:T(8,128)S(1)} %collective-permute-done.left, f32[32,4096]{1,0:T(8,128)S(1)} %collective-permute-done.3.top, f32[32,4096]{1,0:T(8,128)S(1)} %collective-permute-done.4.bottom, bf16[64,192]{1,0:T(8,128)(2,1)S(1)} %copy-done.5, ...), custom_call_target="tpu_custom_call" | custom-call | flops 40265318400 | bytes 1048576 | tf_op jit(solution)/shard_map/far/pallas_call | solution.py:270
  50.0 1.5 %collective-permute-start.8 = (f32[32,4096]{1,0:T(8,128)S(1)}, f32[32,4096]{1,0:T(8,128)S(1)}, u32[]{:S(2)}, u32[]{:S(2)}) collective-permute-start(f32[32,4096]{1,0:T(8,128)S(1)} %get-tuple-element.30), channel_id=1, source_target_pairs={{0,96},{32,0},{64,32},{96,64},{1,97},{33,1},{65,33},{97,65},{2,98}... | collective-permute-start | bytes 1572872 | tf_op jit(solution)/shard_map/ppermute | solution.py:255
  51.6 7.2 %left.1 = (f32[64,4096]{1,0:T(8,128)S(1)}, f32[64,4096]{1,0:T(8,128)S(1)}, f32[32,4096]{1,0:T(8,128)S(1)}, f32[32,4096]{1,0:T(8,128)S(1)}) custom-call(f32[64,4096]{1,0:T(8,128)S(1)} %collective-permute-done.left, f32[64,4096]{1,0:T(8,128)S(1)} %get-tuple-element.18.home, f32[32,4096]{1,0:T(8,128)S(1)} %collective-permute-done.1.top, ...), custom_call_target="tpu_custom_call" | custom-call | flops 80530636800 | bytes 1048576 | tf_op jit(solution)/shard_map/left/pallas_call | solution.py:274
  58.9 1.7 %collective-permute-start.7 = (f32[32,4096]{1,0:T(8,128)S(1)}, f32[32,4096]{1,0:T(8,128)S(1)}, u32[]{:S(2)}, u32[]{:S(2)}) collective-permute-start(f32[32,4096]{1,0:T(8,128)S(1)} %add.6), channel_id=1, source_target_pairs={{0,30},{1,31},{2,0},{3,1},{4,2},{5,3},{6,4},{7,5},{8,6},{9,7},{10,... | collective-permute-start | bytes 1572872 | tf_op jit(solution)/shard_map/ppermute | solution.py:255
  60.6 5.6 %collective-permute-done.8 = f32[32,4096]{1,0:T(8,128)S(1)} collective-permute-done((f32[32,4096]{1,0:T(8,128)S(1)}, f32[32,4096]{1,0:T(8,128)S(1)}, u32[]{:S(2)}, u32[]{:S(2)}) %collective-permute-start.8) | collective-permute-done | bytes 524320 | tf_op jit(solution)/shard_map/ppermute | solution.py:255
  66.3 1.0 %collective-permute-start.9 = (f32[32,4096]{1,0:T(8,128)S(1)}, f32[32,4096]{1,0:T(8,128)S(1)}, u32[]{:S(2)}, u32[]{:S(2)}) collective-permute-start(f32[32,4096]{1,0:T(8,128)S(1)} %add.7), channel_id=1, source_target_pairs={{0,30},{1,31},{2,0},{3,1},{4,2},{5,3},{6,4},{7,5},{8,6},{9,7},{10,... | collective-permute-start | bytes 1572872 | tf_op jit(solution)/shard_map/ppermute | solution.py:255
  67.3 6.5 %collective-permute-done.7.top = f32[32,4096]{1,0:T(8,128)S(1)} collective-permute-done((f32[32,4096]{1,0:T(8,128)S(1)}, f32[32,4096]{1,0:T(8,128)S(1)}, u32[]{:S(2)}, u32[]{:S(2)}) %collective-permute-start.7) | collective-permute-done | bytes 524320 | tf_op jit(solution)/shard_map/ppermute | solution.py:255
  73.8 9.8 %collective-permute-done.9.bottom = f32[32,4096]{1,0:T(8,128)S(1)} collective-permute-done((f32[32,4096]{1,0:T(8,128)S(1)}, f32[32,4096]{1,0:T(8,128)S(1)}, u32[]{:S(2)}, u32[]{:S(2)}) %collective-permute-start.9) | collective-permute-done | bytes 524320 | tf_op jit(solution)/shard_map/ppermute | solution.py:255
  83.6 5.2 %collective-permute-done.5.two = f32[64,4096]{1,0:T(8,128)S(1)} collective-permute-done((f32[64,4096]{1,0:T(8,128)S(1)}, f32[64,4096]{1,0:T(8,128)S(1)}, u32[]{:S(2)}, u32[]{:S(2)}) %collective-permute-start.5) | collective-permute-done | bytes 1048608 | tf_op jit(solution)/shard_map/ppermute | solution.py:255
  88.9 1.3 %unpack.1 = f32[64,4096]{1,0:T(8,128)} custom-call(f32[1]{0:T(128)S(6)} %copy.10.occ, f32[64,4096]{1,0:T(8,128)S(1)} %get-tuple-element.25.one, f32[64,4096]{1,0:T(8,128)S(1)} %collective-permute-done.5.two, f32[32,4096]{1,0:T(8,128)S(1)} %collective-permute-done.7.top, f32[32,4096]{1,0:T(8,128)S(1)} %collective-permute-done.9.bottom), custom_call_target="tpu_custom_call" | custom-call | bytes 1048576 | tf_op jit(solution)/shard_map/unpack/pallas_call | solution.py:281
  (19 shorter events, 0.9 us)
Async XLA Ops:
  0.7 1.2 %copy-start = (f32[1,64,4096]{2,1,0:T(8,128)S(1)}, f32[1,64,4096]{2,1,0:T(8,128)}, u32[]{:S(2)}) copy-start(f32[1,64,4096]{2,1,0:T(8,128)} %param.9) | copy-start | bytes 3145732
  1.9 30.2 %copy-start.1 = (f32[2048,128]{1,0:T(8,128)S(1)}, f32[2048,128]{1,0:T(8,128)}, u32[]{:S(2)}) copy-start(f32[2048,128]{1,0:T(8,128)} %constant.20.clone.rest_6_) | copy-start | bytes 3145732
  2.3 19.4 %collective-permute-start.1 = (f32[32,4096]{1,0:T(8,128)S(1)}, f32[32,4096]{1,0:T(8,128)S(1)}, u32[]{:S(2)}, u32[]{:S(2)}) collective-permute-start(f32[32,4096]{1,0:T(8,128)S(1)} %get-tuple-element.19), channel_id=1, source_target_pairs={{0,2},{1,3},{2,4},{3,5},{4,6},{5,7},{6,8},{7,9},{8,10},{9,11},{10,... | collective-permute-start | bytes 1572872 | tf_op jit(solution)/shard_map/ppermute | solution.py:255
  4.4 27.7 %collective-permute-start.2 = (f32[32,4096]{1,0:T(8,128)S(1)}, f32[32,4096]{1,0:T(8,128)S(1)}, u32[]{:S(2)}, u32[]{:S(2)}) collective-permute-start(f32[32,4096]{1,0:T(8,128)S(1)} %get-tuple-element.20), channel_id=1, source_target_pairs={{0,2},{1,3},{2,4},{3,5},{4,6},{5,7},{6,8},{7,9},{8,10},{9,11},{10,... | collective-permute-start | bytes 1572872 | tf_op jit(solution)/shard_map/ppermute | solution.py:255
  6.3 40.0 %collective-permute-start = (f32[64,4096]{1,0:T(8,128)S(1)}, f32[64,4096]{1,0:T(8,128)S(1)}, u32[]{:S(2)}, u32[]{:S(2)}) collective-permute-start(f32[64,4096]{1,0:T(8,128)S(1)} %get-tuple-element.18.home), channel_id=1, source_target_pairs={{0,31},{1,0},{2,1},{3,2},{4,3},{5,4},{6,5},{7,6},{8,7},{9,8},{10,9... | collective-permute-start | bytes 3145736 | tf_op jit(solution)/shard_map/ppermute | solution.py:255
  21.7 19.0 %collective-permute-start.3 = (f32[32,4096]{1,0:T(8,128)S(1)}, f32[32,4096]{1,0:T(8,128)S(1)}, u32[]{:S(2)}, u32[]{:S(2)}) collective-permute-start(f32[32,4096]{1,0:T(8,128)S(1)} %collective-permute-done.1.top), channel_id=1, source_target_pairs={{0,32},{32,64},{64,96},{96,0},{1,33},{33,65},{65,97},{97,1},{2,34}... | collective-permute-start | bytes 1572872 | tf_op jit(solution)/shard_map/ppermute | solution.py:255
  32.1 14.2 %collective-permute-start.4 = (f32[32,4096]{1,0:T(8,128)S(1)}, f32[32,4096]{1,0:T(8,128)S(1)}, u32[]{:S(2)}, u32[]{:S(2)}) collective-permute-start(f32[32,4096]{1,0:T(8,128)S(1)} %collective-permute-done.2.bottom), channel_id=1, source_target_pairs={{0,32},{32,64},{64,96},{96,0},{1,33},{33,65},{65,97},{97,1},{2,34}... | collective-permute-start | bytes 1572872 | tf_op jit(solution)/shard_map/ppermute | solution.py:255
  32.1 0.9 %copy-start.2 = (bf16[256,256]{1,0:T(8,128)(2,1)S(1)}, bf16[256,256]{1,0:T(8,128)(2,1)}, u32[]{:S(2)}) copy-start(bf16[256,256]{1,0:T(8,128)(2,1)} %constant.17.clone.rest_3_) | copy-start | bytes 393220
  33.0 0.9 %copy-start.3 = (bf16[256,256]{1,0:T(8,128)(2,1)S(1)}, bf16[256,256]{1,0:T(8,128)(2,1)}, u32[]{:S(2)}) copy-start(bf16[256,256]{1,0:T(8,128)(2,1)} %constant.16.clone.rest_2_) | copy-start | bytes 393220
  33.9 0.8 copy-start.4
  34.7 0.8 copy-start.5
  35.4 0.7 copy-start.6
  36.1 0.7 copy-start.7
  50.0 8.9 %collective-permute-start.6 = (f32[32,4096]{1,0:T(8,128)S(1)}, f32[32,4096]{1,0:T(8,128)S(1)}, u32[]{:S(2)}, u32[]{:S(2)}) collective-permute-start(f32[32,4096]{1,0:T(8,128)S(1)} %get-tuple-element.28), channel_id=1, source_target_pairs={{0,96},{32,0},{64,32},{96,64},{1,97},{33,1},{65,33},{97,65},{2,98}... | collective-permute-start | bytes 1572872 | tf_op jit(solution)/shard_map/ppermute | solution.py:255
  50.0 16.2 %collective-permute-start.8 = (f32[32,4096]{1,0:T(8,128)S(1)}, f32[32,4096]{1,0:T(8,128)S(1)}, u32[]{:S(2)}, u32[]{:S(2)}) collective-permute-start(f32[32,4096]{1,0:T(8,128)S(1)} %get-tuple-element.30), channel_id=1, source_target_pairs={{0,96},{32,0},{64,32},{96,64},{1,97},{33,1},{65,33},{97,65},{2,98}... | collective-permute-start | bytes 1572872 | tf_op jit(solution)/shard_map/ppermute | solution.py:255
  58.8 30.1 %collective-permute-start.5 = (f32[64,4096]{1,0:T(8,128)S(1)}, f32[64,4096]{1,0:T(8,128)S(1)}, u32[]{:S(2)}, u32[]{:S(2)}) collective-permute-start(f32[64,4096]{1,0:T(8,128)S(1)} %get-tuple-element.26), channel_id=1, source_target_pairs={{0,1},{1,2},{2,3},{3,4},{4,5},{5,6},{6,7},{7,8},{8,9},{9,10},{10,1... | collective-permute-start | bytes 3145736 | tf_op jit(solution)/shard_map/ppermute | solution.py:255
  58.9 14.9 %collective-permute-start.7 = (f32[32,4096]{1,0:T(8,128)S(1)}, f32[32,4096]{1,0:T(8,128)S(1)}, u32[]{:S(2)}, u32[]{:S(2)}) collective-permute-start(f32[32,4096]{1,0:T(8,128)S(1)} %add.6), channel_id=1, source_target_pairs={{0,30},{1,31},{2,0},{3,1},{4,2},{5,3},{6,4},{7,5},{8,6},{9,7},{10,... | collective-permute-start | bytes 1572872 | tf_op jit(solution)/shard_map/ppermute | solution.py:255
  66.3 17.3 %collective-permute-start.9 = (f32[32,4096]{1,0:T(8,128)S(1)}, f32[32,4096]{1,0:T(8,128)S(1)}, u32[]{:S(2)}, u32[]{:S(2)}) collective-permute-start(f32[32,4096]{1,0:T(8,128)S(1)} %add.7), channel_id=1, source_target_pairs={{0,30},{1,31},{2,0},{3,1},{4,2},{5,3},{6,4},{7,5},{8,6},{9,7},{10,... | collective-permute-start | bytes 1572872 | tf_op jit(solution)/shard_map/ppermute | solution.py:255

commit v3 on v2

--- a/solution.py
+++ b/solution.py
@@ -59,15 +59,31 @@
     step = 2.0 * np.pi / SIZE
     kernel = (np.pi / (step * step * total + 0.25)).astype(np.float32)
     kernel = kernel.reshape(SIZE * HALF, 2 * SIZE)
-    return (
+    parts = (
         left_form(full),
         left_form(full.T),
         right_form(lane.T),
         right_form(lane),
         left_form(np.concatenate([even, odd], axis=0)),
         left_form(np.concatenate([even.T, odd.T], axis=0)),
-        kernel,
-    )
+    )
+    table = [np.pad(part, ((0, 0), (0, 256 - part.shape[1]))) for part in parts]
+    return np.concatenate(table, axis=0), kernel
+
+
+WHERE = {
+    "fa": (0, 64, 192),
+    "ba": (64, 64, 192),
+    "fl": (128, 256, 256),
+    "bl": (384, 256, 256),
+    "fm": (640, 64, 96),
+    "bm": (704, 64, 96),
+}
+
+
+def matrix(mats, name):
+    start, rows, columns = WHERE[name]
+    return mats[0][start : start + rows, :columns]
 
 
 def split(value):
@@ -119,36 +135,35 @@
     refs[1][:, lanes] = value[HALF:]
 
 
-def forward(left, right, mats, area, tiles=8):
-    fa, _, fl, _, _, _, _ = mats
+def forward(left, right, mats, area, tiles=16):
     for base in range(0, HALF, tiles):
         lanes = pl.ds(base * 128, tiles * 128)
-        value = along_rows(fa[...], take(left, lanes) * take(right, lanes))
-        value = along_lanes(to_rows(value), fl[...])
+        value = along_rows(matrix(mats, "fa"), take(left, lanes) * take(right, lanes))
+        value = along_lanes(to_rows(value), matrix(mats, "fl"))
         for n in range(tiles):
             area[pl.ds(base + n, SIZE, stride=ROWS), :] = value[n * SIZE : (n + 1) * SIZE]
 
 
-def middle(mats, area, count=8):
-    _, _, _, _, fm, bm, kernel = mats
+def middle(mats, area, other, count=32):
+    kernel = mats[1]
     for base in range(0, SIZE, count):
         value = jnp.concatenate(
             [area[pl.ds((base + n) * ROWS, HALF), :] for n in range(count)], axis=1
         )
-        value = pick(along_rows(fm[...], value))
+        value = pick(along_rows(matrix(mats, "fm"), value))
         value = value * to_lanes(kernel[pl.ds(base * HALF, count * HALF), :], HALF)
-        value = pick(along_rows(bm[...], value))
+        value = pick(along_rows(matrix(mats, "bm"), value))
         for n in range(count):
-            area[pl.ds((base + n) * ROWS, HALF), :] = value[:, n * 128 : (n + 1) * 128]
-
-
-def backward(mats, area, base, tiles=8):
-    _, ba, _, bl, _, _, _ = mats
+            other[pl.ds((base + n) * ROWS, HALF), :] = value[:, n * 128 : (n + 1) * 128]
+
+
+def backward(mats, other, base, tiles=16):
     value = jnp.concatenate(
-        [area[pl.ds(base + n, SIZE, stride=ROWS), :] for n in range(tiles)], axis=0
-    )
-    value = along_lanes(value, bl[...])
-    return along_rows(ba[...], to_lanes(value, SIZE))
+        [other[pl.ds(base + n, SIZE, stride=ROWS), :] for n in range(tiles)], axis=0
+    )
+    value = along_lanes(value, matrix(mats, "bl"))
+    return along_rows(matrix(mats, "ba"), to_lanes(value, SIZE))
+
 
 def pack_body(occ, orb, out, top, bottom):
     scale = jnp.sqrt(jnp.full((1, 128), occ[0], F32))
@@ -189,7 +204,7 @@
 AREA = pltpu.VMEM((SIZE * ROWS, 128), F32)
 
 
-def call(body, name, count, outs, scratch=(), work=0, first=VMEM):
+def call(body, count, outs, scratch=(), work=0, first=VMEM):
     return pl.pallas_call(
         body,
         out_shape=list(outs),
@@ -200,21 +215,20 @@
             flops=work * COST, bytes_accessed=1 << 20, transcendentals=0
         ),
         compiler_params=pltpu.CompilerParams(vmem_limit_bytes=20 << 20),
-        name=name,
-    )
-
-
-def edge(one, two, mats, area, finish):
-    forward(one, two, mats, area)
-    middle(mats, area)
-    for base in range(0, HALF, 8):
-        value = backward(mats, area, base)
-        lanes = pl.ds(base * 128, 1024)
+    )
+
+
+def edge(one, two, mats, areas, finish, tiles=16):
+    forward(one, two, mats, areas[0])
+    middle(mats, *areas)
+    for base in range(0, HALF, tiles):
+        value = backward(mats, areas[1], base, tiles)
+        lanes = pl.ds(base * 128, tiles * 128)
         finish(lanes, value * take(two, lanes), value * take(one, lanes))
 
 
 def right_body(home, top, bottom, *rest):
-    mats, (home_out, top_out, bottom_out, area) = rest[:7], rest[7:]
+    mats, (home_out, top_out, bottom_out, *area) = rest[:2], rest[2:]
 
     def finish(lanes, first, second):
         home_out[:, lanes] = first
@@ -224,7 +238,7 @@
 
 
 def far_body(left, top, bottom, *rest):
-    mats, (left_out, top_out, bottom_out, area) = rest[:7], rest[7:]
+    mats, (left_out, top_out, bottom_out, *area) = rest[:2], rest[2:]
 
     def finish(lanes, first, second):
         left_out[:, lanes] = first
@@ -234,8 +248,8 @@
 
 
 def left_body(left, home, top, bottom, left_in, home_in, top_in, bottom_in, *rest):
-    mats, outs = rest[:7], rest[7:]
-    left_out, home_out, top_out, bottom_out, area = outs
+    mats, outs = rest[:2], rest[2:]
+    left_out, home_out, top_out, bottom_out, *area = outs
 
     def finish_home(lanes, first, second):
         left_out[:, lanes] = left_in[:, lanes] + first
@@ -258,27 +272,23 @@
 def local(orbitals, occupation):
     mats = [jnp.asarray(item) for item in constants()]
     pair = [WHOLE, PART, PART]
-    home, top, bottom = call(pack_body, "pack", 2, pair, first=SMEM)(
-        occupation, orbitals[0]
-    )
-    right = [shift(part, "blk", 2) for part in (top, bottom)]
+    home, top, bottom = call(pack_body, 2, pair, first=SMEM)(occupation, orbitals[0])
     left = shift(home, "blk", -1)
+    right = []
+    for part in (top, bottom):
+        right.append(shift(part, "blk", 2))
     far = [shift(part, "group", 1) for part in right]
-    acc_home, *acc_right = call(right_body, "right", 10, pair, [AREA], 1)(
-        home, *right, *mats
-    )
-    acc_left, *acc_far = call(far_body, "far", 10, pair, [AREA], 1)(
-        left, *far, *mats
-    )
+    acc_home, *acc_right = call(right_body, 5, pair, [AREA] * 2, 1)(home, *right, *mats)
+    acc_left, *acc_far = call(far_body, 5, pair, [AREA] * 2, 1)(left, *far, *mats)
     from_far = [shift(part, "group", -1) for part in acc_far]
     acc_left, acc_home, *acc_right = call(
-        left_body, "left", 15, [WHOLE, WHOLE, PART, PART], [AREA], 2
+        left_body, 10, [WHOLE, WHOLE, PART, PART], [AREA] * 2, 2
     )(left, home, *right, acc_left, acc_home, *acc_right, *mats)
     from_left = shift(acc_left, "blk", 1)
     from_right = [
         shift(one + two, "blk", -2) for one, two in zip(acc_right, from_far)
     ]
-    out = call(unpack_body, "unpack", 5, [WHOLE], first=SMEM)(
+    out = call(unpack_body, 5, [WHOLE], first=SMEM)(
         occupation, acc_home, from_left, *from_right
     )[0]
     return out[None]

time: 90.6 us -> 87.9 us (0.970)
  waiting for transfers between devices: 52.9 us -> 58.2 us
  Pallas kernels: 16.2 us -> 12.3 us
  local copies, waits for them, and re-layouts: 5.98 us -> 2.22 us
    ppermute x10, waiting for transfers between devices: 52.9 us -> 58.2 us  [shift(): return lax.ppermute(value, axis, pairs)]
    pallas_call x5, Pallas kernels: 16.2 us -> 12.3 us  [the longest x1 5.16 us: local(): call(left_body, 10, [WHOLE, WHOLE, PART, PART], [AREA] * 2, 2)]
    unnamed x16 -> x6, local copies, waits for them, and re-layouts: 5.98 us -> 2.22 us
  transfers between devices with their start and end apart: 10 -> 10, of which waited for: 8 -> 9; matrix products, arithmetic and copies ran while one was open for 0% -> 0% of each run, Pallas kernels for 12% -> 9%
where the time goes in v3:
time: 87.9 us; the launch traced here: 87.7 us
  waiting for transfers between devices  58.2 us (66%)
  starting transfers between devices  14.1 us (16%)
  Pallas kernels  12.3 us (14%)
  local copies, waits for them, and re-layouts  2.22 us (3%)
    ppermute x10, waiting for transfers between devices, shift(): return lax.ppermute(value, axis, pairs)  58.2 us
    ppermute x10, starting transfers between devices, shift(): return lax.ppermute(value, axis, pairs)  14.1 us
    pallas_call x1, Pallas kernels, local(): call(left_body, 10, [WHOLE, WHOLE, PART, PART], [AREA] * 2, 2)  5.16 us
    pallas_call x1, Pallas kernels, local(): call(far_body, 5, pair, [AREA] * 2, 1)(left, *far, *mats)  2.74 us
    pallas_call x1, Pallas kernels, local(): call(right_body, 5, pair, [AREA] * 2, 1)(home, *right, *mats)  2.73 us
    unnamed x6, local copies, waits for them, and re-layouts  2.22 us
  transfers between devices with their start and end apart: 10, of which 9 were waited for; matrix products, arithmetic and copies ran while one was open for 0% of the time, Pallas kernels for 9%

profile of v3, /device:TPU:0, one launch (start us, length us, event | category | flops | bytes accessed | tf_op | source)
XLA Modules:
  0.0 87.7 jit_solution(5496400799841569728)
XLA Ops:
  0.7 1.2 %copy-done = f32[1,64,4096]{2,1,0:T(8,128)S(1)} copy-done((f32[1,64,4096]{2,1,0:T(8,128)S(1)}, f32[1,64,4096]{2,1,0:T(8,128)}, u32[]{:S(2)}) %copy-start) | copy-done | bytes 1048600
  1.9 0.4 shard_map.46
  2.3 2.1 %collective-permute-start.1 = (f32[32,4096]{1,0:T(8,128)S(1)}, f32[32,4096]{1,0:T(8,128)S(1)}, u32[]{:S(2)}, u32[]{:S(2)}) collective-permute-start(f32[32,4096]{1,0:T(8,128)S(1)} %get-tuple-element.19), channel_id=1, source_target_pairs={{0,2},{1,3},{2,4},{3,5},{4,6},{5,7},{6,8},{7,9},{8,10},{9,11},{10,... | collective-permute-start | bytes 1572872 | tf_op jit(solution)/shard_map/ppermute | solution.py:269
  4.4 1.9 %collective-permute-start.2 = (f32[32,4096]{1,0:T(8,128)S(1)}, f32[32,4096]{1,0:T(8,128)S(1)}, u32[]{:S(2)}, u32[]{:S(2)}) collective-permute-start(f32[32,4096]{1,0:T(8,128)S(1)} %get-tuple-element.20), channel_id=1, source_target_pairs={{0,2},{1,3},{2,4},{3,5},{4,6},{5,7},{6,8},{7,9},{8,10},{9,11},{10,... | collective-permute-start | bytes 1572872 | tf_op jit(solution)/shard_map/ppermute | solution.py:269
  6.3 5.9 %collective-permute-start = (f32[64,4096]{1,0:T(8,128)S(1)}, f32[64,4096]{1,0:T(8,128)S(1)}, u32[]{:S(2)}, u32[]{:S(2)}) collective-permute-start(f32[64,4096]{1,0:T(8,128)S(1)} %get-tuple-element.18.home), channel_id=1, source_target_pairs={{0,31},{1,0},{2,1},{3,2},{4,3},{5,4},{6,5},{7,6},{8,7},{9,8},{10,9... | collective-permute-start | bytes 3145736 | tf_op jit(solution)/shard_map/ppermute | solution.py:269
  12.2 9.5 %collective-permute-done.1.top = f32[32,4096]{1,0:T(8,128)S(1)} collective-permute-done((f32[32,4096]{1,0:T(8,128)S(1)}, f32[32,4096]{1,0:T(8,128)S(1)}, u32[]{:S(2)}, u32[]{:S(2)}) %collective-permute-start.1) | collective-permute-done | bytes 524320 | tf_op jit(solution)/shard_map/ppermute | solution.py:269
  21.7 10.4 %collective-permute-done.2.bottom = f32[32,4096]{1,0:T(8,128)S(1)} collective-permute-done((f32[32,4096]{1,0:T(8,128)S(1)}, f32[32,4096]{1,0:T(8,128)S(1)}, u32[]{:S(2)}, u32[]{:S(2)}) %collective-permute-start.2) | collective-permute-done | bytes 524320 | tf_op jit(solution)/shard_map/ppermute | solution.py:269
  32.1 1.0 %copy-done.2 = bf16[768,256]{1,0:T(8,128)(2,1)S(1)} copy-done((bf16[768,256]{1,0:T(8,128)(2,1)S(1)}, bf16[768,256]{1,0:T(8,128)(2,1)}, u32[]{:S(2)}) %copy-start.2) | copy-done | bytes 393240
  33.1 2.7 %shard_map.48 = (f32[64,4096]{1,0:T(8,128)S(1)}, f32[32,4096]{1,0:T(8,128)S(1)}, f32[32,4096]{1,0:T(8,128)S(1)}) custom-call(f32[64,4096]{1,0:T(8,128)S(1)} %get-tuple-element.18.home, f32[32,4096]{1,0:T(8,128)S(1)} %collective-permute-done.1.top, f32[32,4096]{1,0:T(8,128)S(1)} %collective-permute-done.2.bottom, bf16[768,256]{1,0:T(8,128)(2,1)S(1)} %copy-done.2, ...), custom_call_target="tpu_custom_call" | custom-call | flops 40265318400 | bytes 1048576 | tf_op jit(solution)/shard_map/pallas_call | solution.py:281
  35.8 4.9 %collective-permute-done.3.top = f32[32,4096]{1,0:T(8,128)S(1)} collective-permute-done((f32[32,4096]{1,0:T(8,128)S(1)}, f32[32,4096]{1,0:T(8,128)S(1)}, u32[]{:S(2)}, u32[]{:S(2)}) %collective-permute-start.3) | collective-permute-done | bytes 524320 | tf_op jit(solution)/shard_map/ppermute | solution.py:269
  40.7 5.6 %collective-permute-done.4.bottom = f32[32,4096]{1,0:T(8,128)S(1)} collective-permute-done((f32[32,4096]{1,0:T(8,128)S(1)}, f32[32,4096]{1,0:T(8,128)S(1)}, u32[]{:S(2)}, u32[]{:S(2)}) %collective-permute-start.4) | collective-permute-done | bytes 524320 | tf_op jit(solution)/shard_map/ppermute | solution.py:269
  46.3 2.7 %shard_map.47 = (f32[64,4096]{1,0:T(8,128)S(1)}, f32[32,4096]{1,0:T(8,128)S(1)}, f32[32,4096]{1,0:T(8,128)S(1)}) custom-call(f32[64,4096]{1,0:T(8,128)S(1)} %collective-permute-done.left, f32[32,4096]{1,0:T(8,128)S(1)} %collective-permute-done.3.top, f32[32,4096]{1,0:T(8,128)S(1)} %collective-permute-done.4.bottom, bf16[768,256]{1,0:T(8,128)(2,1)S(1)} %copy-done.2, ...), custom_call_target="tpu_custom_call" | custom-call | flops 40265318400 | bytes 1048576 | tf_op jit(solution)/shard_map/pallas_call | solution.py:282
  49.1 0.1 collective-permute-start.6
  49.1 1.5 %collective-permute-start.8 = (f32[32,4096]{1,0:T(8,128)S(1)}, f32[32,4096]{1,0:T(8,128)S(1)}, u32[]{:S(2)}, u32[]{:S(2)}) collective-permute-start(f32[32,4096]{1,0:T(8,128)S(1)} %get-tuple-element.30), channel_id=1, source_target_pairs={{0,96},{32,0},{64,32},{96,64},{1,97},{33,1},{65,33},{97,65},{2,98}... | collective-permute-start | bytes 1572872 | tf_op jit(solution)/shard_map/ppermute | solution.py:269
  50.7 5.2 %shard_map.49 = (f32[64,4096]{1,0:T(8,128)S(1)}, f32[64,4096]{1,0:T(8,128)S(1)}, f32[32,4096]{1,0:T(8,128)S(1)}, f32[32,4096]{1,0:T(8,128)S(1)}) custom-call(f32[64,4096]{1,0:T(8,128)S(1)} %collective-permute-done.left, f32[64,4096]{1,0:T(8,128)S(1)} %get-tuple-element.18.home, f32[32,4096]{1,0:T(8,128)S(1)} %collective-permute-done.1.top, ...), custom_call_target="tpu_custom_call" | custom-call | flops 80530636800 | bytes 1048576 | tf_op jit(solution)/shard_map/pallas_call | solution.py:284
  55.8 0.1 collective-permute-start.5
  55.9 0.2 collective-permute-done.6
  56.2 1.5 %collective-permute-start.7 = (f32[32,4096]{1,0:T(8,128)S(1)}, f32[32,4096]{1,0:T(8,128)S(1)}, u32[]{:S(2)}, u32[]{:S(2)}) collective-permute-start(f32[32,4096]{1,0:T(8,128)S(1)} %add.6), channel_id=1, source_target_pairs={{0,30},{1,31},{2,0},{3,1},{4,2},{5,3},{6,4},{7,5},{8,6},{9,7},{10,... | collective-permute-start | bytes 1572872 | tf_op jit(solution)/shard_map/ppermute | solution.py:269
  57.7 9.6 %collective-permute-done.8 = f32[32,4096]{1,0:T(8,128)S(1)} collective-permute-done((f32[32,4096]{1,0:T(8,128)S(1)}, f32[32,4096]{1,0:T(8,128)S(1)}, u32[]{:S(2)}, u32[]{:S(2)}) %collective-permute-start.8) | collective-permute-done | bytes 524320 | tf_op jit(solution)/shard_map/ppermute | solution.py:269
  67.4 1.0 %collective-permute-start.9 = (f32[32,4096]{1,0:T(8,128)S(1)}, f32[32,4096]{1,0:T(8,128)S(1)}, u32[]{:S(2)}, u32[]{:S(2)}) collective-permute-start(f32[32,4096]{1,0:T(8,128)S(1)} %add.7), channel_id=1, source_target_pairs={{0,30},{1,31},{2,0},{3,1},{4,2},{5,3},{6,4},{7,5},{8,6},{9,7},{10,... | collective-permute-start | bytes 1572872 | tf_op jit(solution)/shard_map/ppermute | solution.py:269
  68.4 1.9 %collective-permute-done.7.top = f32[32,4096]{1,0:T(8,128)S(1)} collective-permute-done((f32[32,4096]{1,0:T(8,128)S(1)}, f32[32,4096]{1,0:T(8,128)S(1)}, u32[]{:S(2)}, u32[]{:S(2)}) %collective-permute-start.7) | collective-permute-done | bytes 524320 | tf_op jit(solution)/shard_map/ppermute | solution.py:269
  70.3 10.9 %collective-permute-done.9.bottom = f32[32,4096]{1,0:T(8,128)S(1)} collective-permute-done((f32[32,4096]{1,0:T(8,128)S(1)}, f32[32,4096]{1,0:T(8,128)S(1)}, u32[]{:S(2)}, u32[]{:S(2)}) %collective-permute-start.9) | collective-permute-done | bytes 524320 | tf_op jit(solution)/shard_map/ppermute | solution.py:269
  81.2 5.1 %collective-permute-done.5.two = f32[64,4096]{1,0:T(8,128)S(1)} collective-permute-done((f32[64,4096]{1,0:T(8,128)S(1)}, f32[64,4096]{1,0:T(8,128)S(1)}, u32[]{:S(2)}, u32[]{:S(2)}) %collective-permute-start.5) | collective-permute-done | bytes 1048608 | tf_op jit(solution)/shard_map/ppermute | solution.py:269
  86.4 1.3 %shard_map.50 = f32[64,4096]{1,0:T(8,128)} custom-call(f32[1]{0:T(128)S(6)} %copy.5.occ, f32[64,4096]{1,0:T(8,128)S(1)} %get-tuple-element.25.one, f32[64,4096]{1,0:T(8,128)S(1)} %collective-permute-done.5.two, f32[32,4096]{1,0:T(8,128)S(1)} %collective-permute-done.7.top, f32[32,4096]{1,0:T(8,128)S(1)} %collective-permute-done.9.bottom), custom_call_target="tpu_custom_call" | custom-call | bytes 1048576 | tf_op jit(solution)/shard_map/pallas_call | solution.py:291
  (9 shorter events, 0.1 us)
Async XLA Ops:
  0.7 1.2 %copy-start = (f32[1,64,4096]{2,1,0:T(8,128)S(1)}, f32[1,64,4096]{2,1,0:T(8,128)}, u32[]{:S(2)}) copy-start(f32[1,64,4096]{2,1,0:T(8,128)} %param.4) | copy-start | bytes 3145732
  1.9 30.2 %copy-start.1 = (f32[2048,128]{1,0:T(8,128)S(1)}, f32[2048,128]{1,0:T(8,128)}, u32[]{:S(2)}) copy-start(f32[2048,128]{1,0:T(8,128)} %constant.5.clone.rest_1_) | copy-start | bytes 3145732
  2.3 19.4 %collective-permute-start.1 = (f32[32,4096]{1,0:T(8,128)S(1)}, f32[32,4096]{1,0:T(8,128)S(1)}, u32[]{:S(2)}, u32[]{:S(2)}) collective-permute-start(f32[32,4096]{1,0:T(8,128)S(1)} %get-tuple-element.19), channel_id=1, source_target_pairs={{0,2},{1,3},{2,4},{3,5},{4,6},{5,7},{6,8},{7,9},{8,10},{9,11},{10,... | collective-permute-start | bytes 1572872 | tf_op jit(solution)/shard_map/ppermute | solution.py:269
  4.4 27.7 %collective-permute-start.2 = (f32[32,4096]{1,0:T(8,128)S(1)}, f32[32,4096]{1,0:T(8,128)S(1)}, u32[]{:S(2)}, u32[]{:S(2)}) collective-permute-start(f32[32,4096]{1,0:T(8,128)S(1)} %get-tuple-element.20), channel_id=1, source_target_pairs={{0,2},{1,3},{2,4},{3,5},{4,6},{5,7},{6,8},{7,9},{8,10},{9,11},{10,... | collective-permute-start | bytes 1572872 | tf_op jit(solution)/shard_map/ppermute | solution.py:269
  6.3 40.0 %collective-permute-start = (f32[64,4096]{1,0:T(8,128)S(1)}, f32[64,4096]{1,0:T(8,128)S(1)}, u32[]{:S(2)}, u32[]{:S(2)}) collective-permute-start(f32[64,4096]{1,0:T(8,128)S(1)} %get-tuple-element.18.home), channel_id=1, source_target_pairs={{0,31},{1,0},{2,1},{3,2},{4,3},{5,4},{6,5},{7,6},{8,7},{9,8},{10,9... | collective-permute-start | bytes 3145736 | tf_op jit(solution)/shard_map/ppermute | solution.py:269
  21.7 19.0 %collective-permute-start.3 = (f32[32,4096]{1,0:T(8,128)S(1)}, f32[32,4096]{1,0:T(8,128)S(1)}, u32[]{:S(2)}, u32[]{:S(2)}) collective-permute-start(f32[32,4096]{1,0:T(8,128)S(1)} %collective-permute-done.1.top), channel_id=1, source_target_pairs={{0,32},{32,64},{64,96},{96,0},{1,33},{33,65},{65,97},{97,1},{2,34}... | collective-permute-start | bytes 1572872 | tf_op jit(solution)/shard_map/ppermute | solution.py:269
  32.1 14.2 %collective-permute-start.4 = (f32[32,4096]{1,0:T(8,128)S(1)}, f32[32,4096]{1,0:T(8,128)S(1)}, u32[]{:S(2)}, u32[]{:S(2)}) collective-permute-start(f32[32,4096]{1,0:T(8,128)S(1)} %collective-permute-done.2.bottom), channel_id=1, source_target_pairs={{0,32},{32,64},{64,96},{96,0},{1,33},{33,65},{65,97},{97,1},{2,34}... | collective-permute-start | bytes 1572872 | tf_op jit(solution)/shard_map/ppermute | solution.py:269
  32.1 1.0 %copy-start.2 = (bf16[768,256]{1,0:T(8,128)(2,1)S(1)}, bf16[768,256]{1,0:T(8,128)(2,1)}, u32[]{:S(2)}) copy-start(bf16[768,256]{1,0:T(8,128)(2,1)} %constant.4.clone.rest_0_) | copy-start | bytes 1179652
  49.1 7.0 %collective-permute-start.6 = (f32[32,4096]{1,0:T(8,128)S(1)}, f32[32,4096]{1,0:T(8,128)S(1)}, u32[]{:S(2)}, u32[]{:S(2)}) collective-permute-start(f32[32,4096]{1,0:T(8,128)S(1)} %get-tuple-element.28), channel_id=1, source_target_pairs={{0,96},{32,0},{64,32},{96,64},{1,97},{33,1},{65,33},{97,65},{2,98}... | collective-permute-start | bytes 1572872 | tf_op jit(solution)/shard_map/ppermute | solution.py:269
  49.1 18.2 %collective-permute-start.8 = (f32[32,4096]{1,0:T(8,128)S(1)}, f32[32,4096]{1,0:T(8,128)S(1)}, u32[]{:S(2)}, u32[]{:S(2)}) collective-permute-start(f32[32,4096]{1,0:T(8,128)S(1)} %get-tuple-element.30), channel_id=1, source_target_pairs={{0,96},{32,0},{64,32},{96,64},{1,97},{33,1},{65,33},{97,65},{2,98}... | collective-permute-start | bytes 1572872 | tf_op jit(solution)/shard_map/ppermute | solution.py:269
  55.8 30.5 %collective-permute-start.5 = (f32[64,4096]{1,0:T(8,128)S(1)}, f32[64,4096]{1,0:T(8,128)S(1)}, u32[]{:S(2)}, u32[]{:S(2)}) collective-permute-start(f32[64,4096]{1,0:T(8,128)S(1)} %get-tuple-element.26), channel_id=1, source_target_pairs={{0,1},{1,2},{2,3},{3,4},{4,5},{5,6},{6,7},{7,8},{8,9},{9,10},{10,1... | collective-permute-start | bytes 3145736 | tf_op jit(solution)/shard_map/ppermute | solution.py:269
  56.2 14.1 %collective-permute-start.7 = (f32[32,4096]{1,0:T(8,128)S(1)}, f32[32,4096]{1,0:T(8,128)S(1)}, u32[]{:S(2)}, u32[]{:S(2)}) collective-permute-start(f32[32,4096]{1,0:T(8,128)S(1)} %add.6), channel_id=1, source_target_pairs={{0,30},{1,31},{2,0},{3,1},{4,2},{5,3},{6,4},{7,5},{8,6},{9,7},{10,... | collective-permute-start | bytes 1572872 | tf_op jit(solution)/shard_map/ppermute | solution.py:269
  67.4 13.8 %collective-permute-start.9 = (f32[32,4096]{1,0:T(8,128)S(1)}, f32[32,4096]{1,0:T(8,128)S(1)}, u32[]{:S(2)}, u32[]{:S(2)}) collective-permute-start(f32[32,4096]{1,0:T(8,128)S(1)} %add.7), channel_id=1, source_target_pairs={{0,30},{1,31},{2,0},{3,1},{4,2},{5,3},{6,4},{7,5},{8,6},{9,7},{10,... | collective-permute-start | bytes 1572872 | tf_op jit(solution)/shard_map/ppermute | solution.py:269

commit v4 on v3

--- a/solution.py
+++ b/solution.py
@@ -227,69 +227,106 @@
         finish(lanes, value * take(two, lanes), value * take(one, lanes))
 
 
-def right_body(home, top, bottom, *rest):
-    mats, (home_out, top_out, bottom_out, *area) = rest[:2], rest[2:]
-
-    def finish(lanes, first, second):
+def first_body(home, right, near_top, near_bottom, *rest):
+    mats, outs = rest[:2], rest[2:]
+    home_out, right_out, top_out, bottom_out, *areas = outs
+
+    def finish_home(lanes, first, second):
         home_out[:, lanes] = first
-        put((top_out, bottom_out), lanes, second)
-
-    edge((home,), (top, bottom), mats, area, finish)
-
-
-def far_body(left, top, bottom, *rest):
-    mats, (left_out, top_out, bottom_out, *area) = rest[:2], rest[2:]
-
-    def finish(lanes, first, second):
-        left_out[:, lanes] = first
-        put((top_out, bottom_out), lanes, second)
-
-    edge((left,), (top, bottom), mats, area, finish)
-
-
-def left_body(left, home, top, bottom, left_in, home_in, top_in, bottom_in, *rest):
+        right_out[:, lanes] = second
+
+    def finish_near(lanes, first, second):
+        right_out[:, lanes] += second
+        put((top_out, bottom_out), lanes, first)
+
+    edge((home,), (right,), mats, areas, finish_home)
+    edge((near_top, near_bottom), (right,), mats, areas, finish_near)
+
+
+def second_body(left_top, left_bottom, home, right, far, home_in, right_in, *rest):
     mats, outs = rest[:2], rest[2:]
-    left_out, home_out, top_out, bottom_out, *area = outs
+    top_out, bottom_out, home_out, right_out, far_out, *areas = outs
+    left, left_outs = (left_top, left_bottom), (top_out, bottom_out)
+
+    def finish_far(lanes, first, second):
+        put(left_outs, lanes, first)
+        far_out[:, lanes] = second
+
+    def finish_right(lanes, first, second):
+        put(left_outs, lanes, take(left_outs, lanes) + first)
+        right_out[:, lanes] = right_in[:, lanes] + second
 
     def finish_home(lanes, first, second):
-        left_out[:, lanes] = left_in[:, lanes] + first
+        put(left_outs, lanes, take(left_outs, lanes) + first)
         home_out[:, lanes] = home_in[:, lanes] + second
 
-    def finish_right(lanes, first, second):
-        left_out[:, lanes] += first
-        put((top_out, bottom_out), lanes, take((top_in, bottom_in), lanes) + second)
-
-    edge((left,), (home,), mats, area, finish_home)
-    edge((left,), (top, bottom), mats, area, finish_right)
-
-
-def shift(value, axis, steps):
-    count = lax.axis_size(axis)
-    pairs = [(source, (source + steps) % count) for source in range(count)]
-    return lax.ppermute(value, axis, pairs)
+    edge(left, (far,), mats, areas, finish_far)
+    edge(left, (right,), mats, areas, finish_right)
+    edge(left, (home,), mats, areas, finish_home)
+
+
+AXES = ("group", "blk")
+
+
+def send(value, pairs):
+    return lax.ppermute(value, AXES, pairs)
+
+
+def routes(groups, blocks):
+    def at(group, place):
+        return (group % groups) * blocks + place % blocks
+
+    outward, inward, across = [], [], []
+    for group in range(groups):
+        for place in range(blocks):
+            source, target = at(group, place + 1), at(group, place)
+            if group % 2:
+                relay = at(group + 1, place + 1)
+                across.append((at(group - 1, place), target))
+            else:
+                relay = at(group - 1, place)
+            outward.append((source, relay))
+            inward.append((relay, target))
+    behind = [
+        (at(group, place - 2), at(group, place))
+        for group in range(groups)
+        for place in range(blocks)
+    ]
+    return outward, inward, across, behind
+
+
+def turned(pairs):
+    return [(target, source) for source, target in pairs]
 
 
 def local(orbitals, occupation):
     mats = [jnp.asarray(item) for item in constants()]
-    pair = [WHOLE, PART, PART]
-    home, top, bottom = call(pack_body, 2, pair, first=SMEM)(occupation, orbitals[0])
-    left = shift(home, "blk", -1)
-    right = []
-    for part in (top, bottom):
-        right.append(shift(part, "blk", 2))
-    far = [shift(part, "group", 1) for part in right]
-    acc_home, *acc_right = call(right_body, 5, pair, [AREA] * 2, 1)(home, *right, *mats)
-    acc_left, *acc_far = call(far_body, 5, pair, [AREA] * 2, 1)(left, *far, *mats)
-    from_far = [shift(part, "group", -1) for part in acc_far]
-    acc_left, acc_home, *acc_right = call(
-        left_body, 10, [WHOLE, WHOLE, PART, PART], [AREA] * 2, 2
-    )(left, home, *right, acc_left, acc_home, *acc_right, *mats)
-    from_left = shift(acc_left, "blk", 1)
-    from_right = [
-        shift(one + two, "blk", -2) for one, two in zip(acc_right, from_far)
+    groups, blocks = lax.axis_size("group"), lax.axis_size("blk")
+    outward, inward, across, behind = routes(groups, blocks)
+    odd = lax.axis_index("group") % 2 == 1
+    home, top, bottom = call(pack_body, 2, [WHOLE, PART, PART], first=SMEM)(
+        occupation, orbitals[0]
+    )
+    right = send(home, behind)
+    near = [send(top, outward), send(bottom, outward)]
+    left = [send(near[0], inward), send(near[1], inward)]
+    far = send(right, across)
+    near = [jnp.where(odd, part, 0.0) for part in near]
+    acc_home, acc_right, *acc_near = call(
+        first_body, 6, [WHOLE, WHOLE, PART, PART], [AREA] * 2, 2
+    )(home, right, *near, *mats)
+    *acc_left, acc_home, acc_right, acc_far = call(
+        second_body, 9, [PART, PART, WHOLE, WHOLE, WHOLE], [AREA] * 2, 3
+    )(*left, home, right, far, acc_home, acc_right, *mats)
+    back = [send(acc_left[0], turned(inward)), send(acc_left[1], turned(inward))]
+    from_far = send(acc_far, turned(across))
+    from_right = send(acc_right + from_far, turned(behind))
+    from_left = [
+        send(back[0] + acc_near[0], turned(outward)),
+        send(back[1] + acc_near[1], turned(outward)),
     ]
     out = call(unpack_body, 5, [WHOLE], first=SMEM)(
-        occupation, acc_home, from_left, *from_right
+        occupation, acc_home, from_right, *from_left
     )[0]
     return out[None]
 

time: 87.9 us -> 90.4 us (1.028)
  starting transfers between devices: 14.1 us -> 28.4 us
  waiting for transfers between devices: 58.2 us -> 45 us
  Pallas kernels: 12.3 us -> 14.4 us
  local copies, waits for them, and re-layouts: 2.22 us -> 1.23 us
    ppermute x10 -> x12, starting transfers between devices: 14.1 us -> 28.4 us  [send(): return lax.ppermute(value, AXES, pairs)]
    ppermute x10 -> x12, waiting for transfers between devices: 58.2 us -> 45 us  [send(): return lax.ppermute(value, AXES, pairs)]
    pallas_call x4 -> x3, Pallas kernels: 11 us -> 13.1 us  [the longest x1 7.56 us: local(): call(second_body, 9, [PART, PART, WHOLE, WHOLE, WHOLE], [AREA] * 2, 3)]
    unnamed x6, local copies, waits for them, and re-layouts: 2.22 us -> 1.23 us
  transfers between devices with their start and end apart: 10 -> 12, of which waited for: 9 -> 7; matrix products, arithmetic and copies ran while one was open for 0% -> 0% of each run, Pallas kernels for 9% -> 6%
where the time goes in v4:
time: 90.4 us; the launch traced here: 90.1 us
  waiting for transfers between devices  45 us (50%)
  starting transfers between devices  28.4 us (31%)
  Pallas kernels  14.4 us (16%)
  local copies, waits for them, and re-layouts  1.23 us (1%)
    ppermute x12, waiting for transfers between devices, send(): return lax.ppermute(value, AXES, pairs)  45 us
    ppermute x12, starting transfers between devices, send(): return lax.ppermute(value, AXES, pairs)  28.4 us
    pallas_call x1, Pallas kernels, local(): call(second_body, 9, [PART, PART, WHOLE, WHOLE, WHOLE], [AREA] * 2, 3)  7.56 us
    pallas_call x1, Pallas kernels, local(): call(first_body, 6, [WHOLE, WHOLE, PART, PART], [AREA] * 2, 2)  5.13 us
  transfers between devices with their start and end apart: 12, of which 7 were waited for; matrix products, arithmetic and copies ran while one was open for 0% of the time, Pallas kernels for 6%

profile of v4, /device:TPU:0, one launch (start us, length us, event | category | flops | bytes accessed | tf_op | source)
XLA Modules:
  0.0 90.1 jit_solution(10576835777235084139)
XLA Ops:
  0.7 1.2 %copy-done = f32[1,64,4096]{2,1,0:T(8,128)S(1)} copy-done((f32[1,64,4096]{2,1,0:T(8,128)S(1)}, f32[1,64,4096]{2,1,0:T(8,128)}, u32[]{:S(2)}) %copy-start) | copy-done | bytes 1048600
  1.9 0.4 shard_map.46
  2.3 8.3 %collective-permute-start = (f32[32,4096]{1,0:T(8,128)S(1)}, f32[32,4096]{1,0:T(8,128)}, u32[]{:S(2)}, u32[]{:S(2)}) collective-permute-start(f32[32,4096]{1,0:T(8,128)S(1)} %get-tuple-element.17), channel_id=1, source_target_pairs={{1,96},{2,97},{3,98},{4,99},{5,100},{6,101},{7,102},{8,103},{9,104... | collective-permute-start | bytes 1572872 | tf_op jit(solution)/shard_map/ppermute | solution.py:272
  10.6 1.1 %collective-permute-start.2 = (f32[32,4096]{1,0:T(8,128)S(1)}, f32[32,4096]{1,0:T(8,128)}, u32[]{:S(2)}, u32[]{:S(2)}) collective-permute-start(f32[32,4096]{1,0:T(8,128)S(1)} %get-tuple-element.18), channel_id=1, source_target_pairs={{1,96},{2,97},{3,98},{4,99},{5,100},{6,101},{7,102},{8,103},{9,104... | collective-permute-start | bytes 1572872 | tf_op jit(solution)/shard_map/ppermute | solution.py:272
  11.7 5.6 %collective-permute-done = f32[32,4096]{1,0:T(8,128)} collective-permute-done((f32[32,4096]{1,0:T(8,128)S(1)}, f32[32,4096]{1,0:T(8,128)}, u32[]{:S(2)}, u32[]{:S(2)}) %collective-permute-start) | collective-permute-done | bytes 524320 | tf_op jit(solution)/shard_map/ppermute | solution.py:272
  17.3 7.4 %collective-permute-start.1 = (f32[32,4096]{1,0:T(8,128)}, f32[32,4096]{1,0:T(8,128)S(1)}, u32[]{:S(2)}, u32[]{:S(2)}) collective-permute-start(f32[32,4096]{1,0:T(8,128)} %collective-permute-done), channel_id=1, source_target_pairs={{96,0},{97,1},{98,2},{99,3},{100,4},{101,5},{102,6},{103,7},{104,8... | collective-permute-start | bytes 1572872 | tf_op jit(solution)/shard_map/ppermute | solution.py:272
  24.8 5.6 %collective-permute-start.3 = (f32[32,4096]{1,0:T(8,128)}, f32[32,4096]{1,0:T(8,128)S(1)}, u32[]{:S(2)}, u32[]{:S(2)}) collective-permute-start(f32[32,4096]{1,0:T(8,128)} %collective-permute-done.2), channel_id=1, source_target_pairs={{96,0},{97,1},{98,2},{99,3},{100,4},{101,5},{102,6},{103,7},{104,8... | collective-permute-start | bytes 1572872 | tf_op jit(solution)/shard_map/ppermute | solution.py:272
  30.4 8.9 %collective-permute-done.4.right = f32[64,4096]{1,0:T(8,128)S(1)} collective-permute-done((f32[64,4096]{1,0:T(8,128)S(1)}, f32[64,4096]{1,0:T(8,128)S(1)}, u32[]{:S(2)}, u32[]{:S(2)}) %collective-permute-start.4) | collective-permute-done | bytes 1048608 | tf_op jit(solution)/shard_map/ppermute | solution.py:272
  39.3 1.5 %collective-permute-start.5 = (f32[64,4096]{1,0:T(8,128)S(1)}, f32[64,4096]{1,0:T(8,128)S(1)}, u32[]{:S(2)}, u32[]{:S(2)}) collective-permute-start(f32[64,4096]{1,0:T(8,128)S(1)} %collective-permute-done.4.right), channel_id=1, source_target_pairs={{0,32},{1,33},{2,34},{3,35},{4,36},{5,37},{6,38},{7,39},{8,40},{9,... | collective-permute-start | bytes 3145736 | tf_op jit(solution)/shard_map/ppermute | solution.py:272
  40.8 5.1 %shard_map.47 = (f32[64,4096]{1,0:T(8,128)S(1)}, f32[64,4096]{1,0:T(8,128)S(1)}, f32[32,4096]{1,0:T(8,128)S(1)}, f32[32,4096]{1,0:T(8,128)S(1)}) custom-call(f32[64,4096]{1,0:T(8,128)S(1)} %get-tuple-element.19.home, f32[64,4096]{1,0:T(8,128)S(1)} %collective-permute-done.4.right, f32[32,4096]{1,0:T(8,128)S(1)} %broadcast_select_fusion.1.near_top, ...), custom_call_target="tpu_custom_call" | custom-call | flops 80530636800 | bytes 1048576 | tf_op jit(solution)/shard_map/pallas_call | solution.py:315
  46.0 7.6 %shard_map.48 = (f32[32,4096]{1,0:T(8,128)S(1)}, f32[32,4096]{1,0:T(8,128)S(1)}, f32[64,4096]{1,0:T(8,128)S(1)}, f32[64,4096]{1,0:T(8,128)S(1)}, f32[64,4096]{1,0:T(8,128)S(1)}) custom-call(f32[32,4096]{1,0:T(8,128)S(1)} %collective-permute-done.1.left_top, f32[32,4096]{1,0:T(8,128)S(1)} %collective-permute-done.3.left_bottom, ...), custom_call_target="tpu_custom_call" | custom-call | flops 120795955200 | bytes 1048576 | tf_op jit(solution)/shard_map/pallas_call | solution.py:318
  53.6 1.3 %collective-permute-start.6 = (f32[64,4096]{1,0:T(8,128)S(1)}, f32[64,4096]{1,0:T(8,128)S(1)}, u32[]{:S(2)}, u32[]{:S(2)}) collective-permute-start(f32[64,4096]{1,0:T(8,128)S(1)} %get-tuple-element.24), channel_id=1, source_target_pairs={{32,0},{33,1},{34,2},{35,3},{36,4},{37,5},{38,6},{39,7},{40,8},{41... | collective-permute-start | bytes 3145736 | tf_op jit(solution)/shard_map/ppermute | solution.py:272
  54.9 2.9 %collective-permute-start.8 = (f32[32,4096]{1,0:T(8,128)S(1)}, f32[32,4096]{1,0:T(8,128)S(1)}, u32[]{:S(2)}, u32[]{:S(2)}) collective-permute-start(f32[32,4096]{1,0:T(8,128)S(1)} %get-tuple-element.25), channel_id=1, source_target_pairs={{0,96},{1,97},{2,98},{3,99},{4,100},{5,101},{6,102},{7,103},{8,104... | collective-permute-start | bytes 1572872 | tf_op jit(solution)/shard_map/ppermute | solution.py:272
  57.7 0.1 collective-permute-start.10
  57.8 0.3 collective-permute-done.6
  58.1 0.1 add.14
  58.3 0.1 collective-permute-start.7
  58.3 10.7 %collective-permute-done.8 = f32[32,4096]{1,0:T(8,128)S(1)} collective-permute-done((f32[32,4096]{1,0:T(8,128)S(1)}, f32[32,4096]{1,0:T(8,128)S(1)}, u32[]{:S(2)}, u32[]{:S(2)}) %collective-permute-start.8) | collective-permute-done | bytes 524320 | tf_op jit(solution)/shard_map/ppermute | solution.py:272
  69.0 0.1 collective-permute-start.9
  69.1 5.5 %collective-permute-done.10 = f32[32,4096]{1,0:T(8,128)S(1)} collective-permute-done((f32[32,4096]{1,0:T(8,128)S(1)}, f32[32,4096]{1,0:T(8,128)S(1)}, u32[]{:S(2)}, u32[]{:S(2)}) %collective-permute-start.10) | collective-permute-done | bytes 524320 | tf_op jit(solution)/shard_map/ppermute | solution.py:272
  74.7 0.1 collective-permute-start.11
  74.8 8.4 %collective-permute-done.9.top = f32[32,4096]{1,0:T(8,128)S(1)} collective-permute-done((f32[32,4096]{1,0:T(8,128)S(1)}, f32[32,4096]{1,0:T(8,128)S(1)}, u32[]{:S(2)}, u32[]{:S(2)}) %collective-permute-start.9) | collective-permute-done | bytes 524320 | tf_op jit(solution)/shard_map/ppermute | solution.py:272
  83.2 5.6 %collective-permute-done.11.bottom = f32[32,4096]{1,0:T(8,128)S(1)} collective-permute-done((f32[32,4096]{1,0:T(8,128)S(1)}, f32[32,4096]{1,0:T(8,128)S(1)}, u32[]{:S(2)}, u32[]{:S(2)}) %collective-permute-start.11) | collective-permute-done | bytes 524320 | tf_op jit(solution)/shard_map/ppermute | solution.py:272
  88.8 1.3 %shard_map.49 = f32[64,4096]{1,0:T(8,128)} custom-call(f32[1]{0:T(128)S(6)} %copy.5.occ, f32[64,4096]{1,0:T(8,128)S(1)} %get-tuple-element.22.one, f32[64,4096]{1,0:T(8,128)S(1)} %collective-permute-done.7.two, f32[32,4096]{1,0:T(8,128)S(1)} %collective-permute-done.9.top, f32[32,4096]{1,0:T(8,128)S(1)} %collective-permute-done.11.bottom), custom_call_target="tpu_custom_call" | custom-call | bytes 1048576 | tf_op jit(solution)/shard_map/pallas_call | solution.py:328
  (15 shorter events, 0.2 us)
Async XLA Ops:
  0.7 1.2 %copy-start = (f32[1,64,4096]{2,1,0:T(8,128)S(1)}, f32[1,64,4096]{2,1,0:T(8,128)}, u32[]{:S(2)}) copy-start(f32[1,64,4096]{2,1,0:T(8,128)} %param.4) | copy-start | bytes 3145732
  2.3 15.0 %collective-permute-start = (f32[32,4096]{1,0:T(8,128)S(1)}, f32[32,4096]{1,0:T(8,128)}, u32[]{:S(2)}, u32[]{:S(2)}) collective-permute-start(f32[32,4096]{1,0:T(8,128)S(1)} %get-tuple-element.17), channel_id=1, source_target_pairs={{1,96},{2,97},{3,98},{4,99},{5,100},{6,101},{7,102},{8,103},{9,104... | collective-permute-start | bytes 1572872 | tf_op jit(solution)/shard_map/ppermute | solution.py:272
  10.6 14.2 %collective-permute-start.2 = (f32[32,4096]{1,0:T(8,128)S(1)}, f32[32,4096]{1,0:T(8,128)}, u32[]{:S(2)}, u32[]{:S(2)}) collective-permute-start(f32[32,4096]{1,0:T(8,128)S(1)} %get-tuple-element.18), channel_id=1, source_target_pairs={{1,96},{2,97},{3,98},{4,99},{5,100},{6,101},{7,102},{8,103},{9,104... | collective-permute-start | bytes 1572872 | tf_op jit(solution)/shard_map/ppermute | solution.py:272
  11.7 27.6 %collective-permute-start.4 = (f32[64,4096]{1,0:T(8,128)S(1)}, f32[64,4096]{1,0:T(8,128)S(1)}, u32[]{:S(2)}, u32[]{:S(2)}) collective-permute-start(f32[64,4096]{1,0:T(8,128)S(1)} %get-tuple-element.19.home), channel_id=1, source_target_pairs={{30,0},{31,1},{0,2},{1,3},{2,4},{3,5},{4,6},{5,7},{6,8},{7,9},{8,1... | collective-permute-start | bytes 3145736 | tf_op jit(solution)/shard_map/ppermute | solution.py:272
  11.7 29.1 %copy-start.1 = (f32[2048,128]{1,0:T(8,128)S(1)}, f32[2048,128]{1,0:T(8,128)}, u32[]{:S(2)}) copy-start(f32[2048,128]{1,0:T(8,128)} %constant.27.clone.rest_1_) | copy-start | bytes 3145732
  17.3 28.7 %collective-permute-start.1 = (f32[32,4096]{1,0:T(8,128)}, f32[32,4096]{1,0:T(8,128)S(1)}, u32[]{:S(2)}, u32[]{:S(2)}) collective-permute-start(f32[32,4096]{1,0:T(8,128)} %collective-permute-done), channel_id=1, source_target_pairs={{96,0},{97,1},{98,2},{99,3},{100,4},{101,5},{102,6},{103,7},{104,8... | collective-permute-start | bytes 1572872 | tf_op jit(solution)/shard_map/ppermute | solution.py:272
  24.8 16.1 %copy-start.2 = (bf16[768,256]{1,0:T(8,128)(2,1)S(1)}, bf16[768,256]{1,0:T(8,128)(2,1)}, u32[]{:S(2)}) copy-start(bf16[768,256]{1,0:T(8,128)(2,1)} %constant.26.clone.rest_0_) | copy-start | bytes 1179652
  24.8 21.2 %collective-permute-start.3 = (f32[32,4096]{1,0:T(8,128)}, f32[32,4096]{1,0:T(8,128)S(1)}, u32[]{:S(2)}, u32[]{:S(2)}) collective-permute-start(f32[32,4096]{1,0:T(8,128)} %collective-permute-done.2), channel_id=1, source_target_pairs={{96,0},{97,1},{98,2},{99,3},{100,4},{101,5},{102,6},{103,7},{104,8... | collective-permute-start | bytes 1572872 | tf_op jit(solution)/shard_map/ppermute | solution.py:272
  39.3 6.7 %collective-permute-start.5 = (f32[64,4096]{1,0:T(8,128)S(1)}, f32[64,4096]{1,0:T(8,128)S(1)}, u32[]{:S(2)}, u32[]{:S(2)}) collective-permute-start(f32[64,4096]{1,0:T(8,128)S(1)} %collective-permute-done.4.right), channel_id=1, source_target_pairs={{0,32},{1,33},{2,34},{3,35},{4,36},{5,37},{6,38},{7,39},{8,40},{9,... | collective-permute-start | bytes 3145736 | tf_op jit(solution)/shard_map/ppermute | solution.py:272
  53.6 4.6 %collective-permute-start.6 = (f32[64,4096]{1,0:T(8,128)S(1)}, f32[64,4096]{1,0:T(8,128)S(1)}, u32[]{:S(2)}, u32[]{:S(2)}) collective-permute-start(f32[64,4096]{1,0:T(8,128)S(1)} %get-tuple-element.24), channel_id=1, source_target_pairs={{32,0},{33,1},{34,2},{35,3},{36,4},{37,5},{38,6},{39,7},{40,8},{41... | collective-permute-start | bytes 3145736 | tf_op jit(solution)/shard_map/ppermute | solution.py:272
  54.9 14.1 %collective-permute-start.8 = (f32[32,4096]{1,0:T(8,128)S(1)}, f32[32,4096]{1,0:T(8,128)S(1)}, u32[]{:S(2)}, u32[]{:S(2)}) collective-permute-start(f32[32,4096]{1,0:T(8,128)S(1)} %get-tuple-element.25), channel_id=1, source_target_pairs={{0,96},{1,97},{2,98},{3,99},{4,100},{5,101},{6,102},{7,103},{8,104... | collective-permute-start | bytes 1572872 | tf_op jit(solution)/shard_map/ppermute | solution.py:272
  57.7 16.9 %collective-permute-start.10 = (f32[32,4096]{1,0:T(8,128)S(1)}, f32[32,4096]{1,0:T(8,128)S(1)}, u32[]{:S(2)}, u32[]{:S(2)}) collective-permute-start(f32[32,4096]{1,0:T(8,128)S(1)} %get-tuple-element.27), channel_id=1, source_target_pairs={{0,96},{1,97},{2,98},{3,99},{4,100},{5,101},{6,102},{7,103},{8,104... | collective-permute-start | bytes 1572872 | tf_op jit(solution)/shard_map/ppermute | solution.py:272
  58.3 30.5 %collective-permute-start.7 = (f32[64,4096]{1,0:T(8,128)S(1)}, f32[64,4096]{1,0:T(8,128)S(1)}, u32[]{:S(2)}, u32[]{:S(2)}) collective-permute-start(f32[64,4096]{1,0:T(8,128)S(1)} %add.14), channel_id=1, source_target_pairs={{0,30},{1,31},{2,0},{3,1},{4,2},{5,3},{6,4},{7,5},{8,6},{9,7},{10,... | collective-permute-start | bytes 3145736 | tf_op jit(solution)/shard_map/ppermute | solution.py:272
  69.0 14.1 %collective-permute-start.9 = (f32[32,4096]{1,0:T(8,128)S(1)}, f32[32,4096]{1,0:T(8,128)S(1)}, u32[]{:S(2)}, u32[]{:S(2)}) collective-permute-start(f32[32,4096]{1,0:T(8,128)S(1)} %add.15), channel_id=1, source_target_pairs={{96,1},{97,2},{98,3},{99,4},{100,5},{101,6},{102,7},{103,8},{104,9... | collective-permute-start | bytes 1572872 | tf_op jit(solution)/shard_map/ppermute | solution.py:272
  74.7 14.1 %collective-permute-start.11 = (f32[32,4096]{1,0:T(8,128)S(1)}, f32[32,4096]{1,0:T(8,128)S(1)}, u32[]{:S(2)}, u32[]{:S(2)}) collective-permute-start(f32[32,4096]{1,0:T(8,128)S(1)} %add.16), channel_id=1, source_target_pairs={{96,1},{97,2},{98,3},{99,4},{100,5},{101,6},{102,7},{103,8},{104,9... | collective-permute-start | bytes 1572872 | tf_op jit(solution)/shard_map/ppermute | solution.py:272

commit v5 on v4

--- a/solution.py
+++ b/solution.py
@@ -243,24 +243,29 @@
     edge((near_top, near_bottom), (right,), mats, areas, finish_near)
 
 
-def second_body(left_top, left_bottom, home, right, far, home_in, right_in, *rest):
+def far_body(left_top, left_bottom, far, *rest):
+    mats, (top_out, bottom_out, far_out, *areas) = rest[:2], rest[2:]
+
+    def finish(lanes, first, second):
+        put((top_out, bottom_out), lanes, first)
+        far_out[:, lanes] = second
+
+    edge((left_top, left_bottom), (far,), mats, areas, finish)
+
+
+def second_body(left_top, left_bottom, home, right, top_in, bottom_in, home_in, right_in, *rest):
     mats, outs = rest[:2], rest[2:]
-    top_out, bottom_out, home_out, right_out, far_out, *areas = outs
+    top_out, bottom_out, home_out, right_out, *areas = outs
     left, left_outs = (left_top, left_bottom), (top_out, bottom_out)
 
-    def finish_far(lanes, first, second):
-        put(left_outs, lanes, first)
-        far_out[:, lanes] = second
-
     def finish_right(lanes, first, second):
-        put(left_outs, lanes, take(left_outs, lanes) + first)
+        put(left_outs, lanes, take((top_in, bottom_in), lanes) + first)
         right_out[:, lanes] = right_in[:, lanes] + second
 
     def finish_home(lanes, first, second):
         put(left_outs, lanes, take(left_outs, lanes) + first)
         home_out[:, lanes] = home_in[:, lanes] + second
 
-    edge(left, (far,), mats, areas, finish_far)
     edge(left, (right,), mats, areas, finish_right)
     edge(left, (home,), mats, areas, finish_home)
 
@@ -315,11 +320,14 @@
     acc_home, acc_right, *acc_near = call(
         first_body, 6, [WHOLE, WHOLE, PART, PART], [AREA] * 2, 2
     )(home, right, *near, *mats)
-    *acc_left, acc_home, acc_right, acc_far = call(
-        second_body, 9, [PART, PART, WHOLE, WHOLE, WHOLE], [AREA] * 2, 3
-    )(*left, home, right, far, acc_home, acc_right, *mats)
+    *acc_left, acc_far = call(far_body, 5, [PART, PART, WHOLE], [AREA] * 2, 1)(
+        *left, far, *mats
+    )
+    from_far = send(acc_far, turned(across))
+    *acc_left, acc_home, acc_right = call(
+        second_body, 10, [PART, PART, WHOLE, WHOLE], [AREA] * 2, 2
+    )(*left, home, right, *acc_left, acc_home, acc_right, *mats)
     back = [send(acc_left[0], turned(inward)), send(acc_left[1], turned(inward))]
-    from_far = send(acc_far, turned(across))
     from_right = send(acc_right + from_far, turned(behind))
     from_left = [
         send(back[0] + acc_near[0], turned(outward)),

time: 90.4 us -> 90.7 us (level)
    pallas_call x1 -> x2, Pallas kernels: 7.56 us -> 7.91 us  [the longest x1 5.18 us: local(): call(second_body, 10, [PART, PART, WHOLE, WHOLE], [AREA] * 2, 2)]
  transfers between devices with their start and end apart: 12 -> 12, of which waited for: 7 -> 6; matrix products, arithmetic and copies ran while one was open for 0% -> 0% of each run, Pallas kernels for 6% -> 11%
where the time goes in v5:
time: 90.7 us; the launch traced here: 90.5 us
  waiting for transfers between devices  45 us (50%)
  starting transfers between devices  28.4 us (31%)
  Pallas kernels  14.7 us (16%)
  local copies, waits for them, and re-layouts  1.23 us (1%)
    ppermute x12, waiting for transfers between devices, send(): return lax.ppermute(value, AXES, pairs)  45 us
    ppermute x12, starting transfers between devices, send(): return lax.ppermute(value, AXES, pairs)  28.4 us
    pallas_call x1, Pallas kernels, local(): call(second_body, 10, [PART, PART, WHOLE, WHOLE], [AREA] * 2, 2)  5.18 us
    pallas_call x1, Pallas kernels, local(): call(first_body, 6, [WHOLE, WHOLE, PART, PART], [AREA] * 2, 2)  5.12 us
    pallas_call x1, Pallas kernels, local(): call(far_body, 5, [PART, PART, WHOLE], [AREA] * 2, 1)(*left, far, *mats)  2.73 us
  transfers between devices with their start and end apart: 12, of which 6 were waited for; matrix products, arithmetic and copies ran while one was open for 0% of the time, Pallas kernels for 11%

profile of v5, /device:TPU:0, one launch (start us, length us, event | category | flops | bytes accessed | tf_op | source)
XLA Modules:
  0.0 90.5 jit_solution(15505286303413526403)
XLA Ops:
  0.7 1.2 %copy-done = f32[1,64,4096]{2,1,0:T(8,128)S(1)} copy-done((f32[1,64,4096]{2,1,0:T(8,128)S(1)}, f32[1,64,4096]{2,1,0:T(8,128)}, u32[]{:S(2)}) %copy-start) | copy-done | bytes 1048600
  1.9 0.4 shard_map.46
  2.3 8.3 %collective-permute-start = (f32[32,4096]{1,0:T(8,128)S(1)}, f32[32,4096]{1,0:T(8,128)}, u32[]{:S(2)}, u32[]{:S(2)}) collective-permute-start(f32[32,4096]{1,0:T(8,128)S(1)} %get-tuple-element.19), channel_id=1, source_target_pairs={{1,96},{2,97},{3,98},{4,99},{5,100},{6,101},{7,102},{8,103},{9,104... | collective-permute-start | bytes 1572872 | tf_op jit(solution)/shard_map/ppermute | solution.py:277
  10.6 1.1 %collective-permute-start.2 = (f32[32,4096]{1,0:T(8,128)S(1)}, f32[32,4096]{1,0:T(8,128)}, u32[]{:S(2)}, u32[]{:S(2)}) collective-permute-start(f32[32,4096]{1,0:T(8,128)S(1)} %get-tuple-element.20), channel_id=1, source_target_pairs={{1,96},{2,97},{3,98},{4,99},{5,100},{6,101},{7,102},{8,103},{9,104... | collective-permute-start | bytes 1572872 | tf_op jit(solution)/shard_map/ppermute | solution.py:277
  11.7 5.6 %collective-permute-done = f32[32,4096]{1,0:T(8,128)} collective-permute-done((f32[32,4096]{1,0:T(8,128)S(1)}, f32[32,4096]{1,0:T(8,128)}, u32[]{:S(2)}, u32[]{:S(2)}) %collective-permute-start) | collective-permute-done | bytes 524320 | tf_op jit(solution)/shard_map/ppermute | solution.py:277
  17.3 7.4 %collective-permute-start.1 = (f32[32,4096]{1,0:T(8,128)}, f32[32,4096]{1,0:T(8,128)S(1)}, u32[]{:S(2)}, u32[]{:S(2)}) collective-permute-start(f32[32,4096]{1,0:T(8,128)} %collective-permute-done), channel_id=1, source_target_pairs={{96,0},{97,1},{98,2},{99,3},{100,4},{101,5},{102,6},{103,7},{104,8... | collective-permute-start | bytes 1572872 | tf_op jit(solution)/shard_map/ppermute | solution.py:277
  24.8 5.6 %collective-permute-start.3 = (f32[32,4096]{1,0:T(8,128)}, f32[32,4096]{1,0:T(8,128)S(1)}, u32[]{:S(2)}, u32[]{:S(2)}) collective-permute-start(f32[32,4096]{1,0:T(8,128)} %collective-permute-done.2), channel_id=1, source_target_pairs={{96,0},{97,1},{98,2},{99,3},{100,4},{101,5},{102,6},{103,7},{104,8... | collective-permute-start | bytes 1572872 | tf_op jit(solution)/shard_map/ppermute | solution.py:277
  30.4 8.9 %collective-permute-done.4.right = f32[64,4096]{1,0:T(8,128)S(1)} collective-permute-done((f32[64,4096]{1,0:T(8,128)S(1)}, f32[64,4096]{1,0:T(8,128)S(1)}, u32[]{:S(2)}, u32[]{:S(2)}) %collective-permute-start.4) | collective-permute-done | bytes 1048608 | tf_op jit(solution)/shard_map/ppermute | solution.py:277
  39.3 1.3 %collective-permute-start.5 = (f32[64,4096]{1,0:T(8,128)S(1)}, f32[64,4096]{1,0:T(8,128)S(1)}, u32[]{:S(2)}, u32[]{:S(2)}) collective-permute-start(f32[64,4096]{1,0:T(8,128)S(1)} %collective-permute-done.4.right), channel_id=1, source_target_pairs={{0,32},{1,33},{2,34},{3,35},{4,36},{5,37},{6,38},{7,39},{8,40},{9,... | collective-permute-start | bytes 3145736 | tf_op jit(solution)/shard_map/ppermute | solution.py:277
  40.7 5.1 %shard_map.48 = (f32[64,4096]{1,0:T(8,128)S(1)}, f32[64,4096]{1,0:T(8,128)S(1)}, f32[32,4096]{1,0:T(8,128)S(1)}, f32[32,4096]{1,0:T(8,128)S(1)}) custom-call(f32[64,4096]{1,0:T(8,128)S(1)} %get-tuple-element.21.home, f32[64,4096]{1,0:T(8,128)S(1)} %collective-permute-done.4.right, f32[32,4096]{1,0:T(8,128)S(1)} %broadcast_select_fusion.1.near_top, ...), custom_call_target="tpu_custom_call" | custom-call | flops 80530636800 | bytes 1048576 | tf_op jit(solution)/shard_map/pallas_call | solution.py:320
  45.8 2.7 %shard_map.47 = (f32[32,4096]{1,0:T(8,128)S(1)}, f32[32,4096]{1,0:T(8,128)S(1)}, f32[64,4096]{1,0:T(8,128)S(1)}) custom-call(f32[32,4096]{1,0:T(8,128)S(1)} %collective-permute-done.1.left_top, f32[32,4096]{1,0:T(8,128)S(1)} %collective-permute-done.3.left_bottom, f32[64,4096]{1,0:T(8,128)S(1)} %collective-permute-done.5.far, ...), custom_call_target="tpu_custom_call" | custom-call | flops 40265318400 | bytes 1048576 | tf_op jit(solution)/shard_map/pallas_call | solution.py:323
  48.6 1.5 %collective-permute-start.6 = (f32[64,4096]{1,0:T(8,128)S(1)}, f32[64,4096]{1,0:T(8,128)S(1)}, u32[]{:S(2)}, u32[]{:S(2)}) collective-permute-start(f32[64,4096]{1,0:T(8,128)S(1)} %get-tuple-element.28), channel_id=1, source_target_pairs={{32,0},{33,1},{34,2},{35,3},{36,4},{37,5},{38,6},{39,7},{40,8},{41... | collective-permute-start | bytes 3145736 | tf_op jit(solution)/shard_map/ppermute | solution.py:277
  50.0 5.2 %shard_map.49 = (f32[32,4096]{1,0:T(8,128)S(1)}, f32[32,4096]{1,0:T(8,128)S(1)}, f32[64,4096]{1,0:T(8,128)S(1)}, f32[64,4096]{1,0:T(8,128)S(1)}) custom-call(f32[32,4096]{1,0:T(8,128)S(1)} %collective-permute-done.1.left_top, f32[32,4096]{1,0:T(8,128)S(1)} %collective-permute-done.3.left_bottom, f32[64,4096]{1,0:T(8,128)S(1)} %get-tuple-element.21.home, ...), custom_call_target="tpu_custom_call" | custom-call | flops 80530636800 | bytes 1048576 | tf_op jit(solution)/shard_map/pallas_call | solution.py:327
  55.2 2.9 %collective-permute-start.8 = (f32[32,4096]{1,0:T(8,128)S(1)}, f32[32,4096]{1,0:T(8,128)S(1)}, u32[]{:S(2)}, u32[]{:S(2)}) collective-permute-start(f32[32,4096]{1,0:T(8,128)S(1)} %get-tuple-element.29), channel_id=1, source_target_pairs={{0,96},{1,97},{2,98},{3,99},{4,100},{5,101},{6,102},{7,103},{8,104... | collective-permute-start | bytes 1572872 | tf_op jit(solution)/shard_map/ppermute | solution.py:277
  58.1 0.1 collective-permute-start.10
  58.2 0.1 add.14
  58.3 0.1 collective-permute-start.7
  58.4 11.0 %collective-permute-done.8 = f32[32,4096]{1,0:T(8,128)S(1)} collective-permute-done((f32[32,4096]{1,0:T(8,128)S(1)}, f32[32,4096]{1,0:T(8,128)S(1)}, u32[]{:S(2)}, u32[]{:S(2)}) %collective-permute-start.8) | collective-permute-done | bytes 524320 | tf_op jit(solution)/shard_map/ppermute | solution.py:277
  69.4 0.1 collective-permute-start.9
  69.5 5.5 %collective-permute-done.10 = f32[32,4096]{1,0:T(8,128)S(1)} collective-permute-done((f32[32,4096]{1,0:T(8,128)S(1)}, f32[32,4096]{1,0:T(8,128)S(1)}, u32[]{:S(2)}, u32[]{:S(2)}) %collective-permute-start.10) | collective-permute-done | bytes 524320 | tf_op jit(solution)/shard_map/ppermute | solution.py:277
  75.0 0.1 collective-permute-start.11
  75.1 8.4 %collective-permute-done.9.top = f32[32,4096]{1,0:T(8,128)S(1)} collective-permute-done((f32[32,4096]{1,0:T(8,128)S(1)}, f32[32,4096]{1,0:T(8,128)S(1)}, u32[]{:S(2)}, u32[]{:S(2)}) %collective-permute-start.9) | collective-permute-done | bytes 524320 | tf_op jit(solution)/shard_map/ppermute | solution.py:277
  83.5 5.6 %collective-permute-done.11.bottom = f32[32,4096]{1,0:T(8,128)S(1)} collective-permute-done((f32[32,4096]{1,0:T(8,128)S(1)}, f32[32,4096]{1,0:T(8,128)S(1)}, u32[]{:S(2)}, u32[]{:S(2)}) %collective-permute-start.11) | collective-permute-done | bytes 524320 | tf_op jit(solution)/shard_map/ppermute | solution.py:277
  89.1 1.3 %shard_map.50 = f32[64,4096]{1,0:T(8,128)} custom-call(f32[1]{0:T(128)S(6)} %copy.5.occ, f32[64,4096]{1,0:T(8,128)S(1)} %get-tuple-element.26.one, f32[64,4096]{1,0:T(8,128)S(1)} %collective-permute-done.7.two, f32[32,4096]{1,0:T(8,128)S(1)} %collective-permute-done.9.top, f32[32,4096]{1,0:T(8,128)S(1)} %collective-permute-done.11.bottom), custom_call_target="tpu_custom_call" | custom-call | bytes 1048576 | tf_op jit(solution)/shard_map/pallas_call | solution.py:336
  (16 shorter events, 0.2 us)
Async XLA Ops:
  0.7 1.2 %copy-start = (f32[1,64,4096]{2,1,0:T(8,128)S(1)}, f32[1,64,4096]{2,1,0:T(8,128)}, u32[]{:S(2)}) copy-start(f32[1,64,4096]{2,1,0:T(8,128)} %param.4) | copy-start | bytes 3145732
  2.3 15.0 %collective-permute-start = (f32[32,4096]{1,0:T(8,128)S(1)}, f32[32,4096]{1,0:T(8,128)}, u32[]{:S(2)}, u32[]{:S(2)}) collective-permute-start(f32[32,4096]{1,0:T(8,128)S(1)} %get-tuple-element.19), channel_id=1, source_target_pairs={{1,96},{2,97},{3,98},{4,99},{5,100},{6,101},{7,102},{8,103},{9,104... | collective-permute-start | bytes 1572872 | tf_op jit(solution)/shard_map/ppermute | solution.py:277
  10.6 14.2 %collective-permute-start.2 = (f32[32,4096]{1,0:T(8,128)S(1)}, f32[32,4096]{1,0:T(8,128)}, u32[]{:S(2)}, u32[]{:S(2)}) collective-permute-start(f32[32,4096]{1,0:T(8,128)S(1)} %get-tuple-element.20), channel_id=1, source_target_pairs={{1,96},{2,97},{3,98},{4,99},{5,100},{6,101},{7,102},{8,103},{9,104... | collective-permute-start | bytes 1572872 | tf_op jit(solution)/shard_map/ppermute | solution.py:277
  11.7 27.6 %collective-permute-start.4 = (f32[64,4096]{1,0:T(8,128)S(1)}, f32[64,4096]{1,0:T(8,128)S(1)}, u32[]{:S(2)}, u32[]{:S(2)}) collective-permute-start(f32[64,4096]{1,0:T(8,128)S(1)} %get-tuple-element.21.home), channel_id=1, source_target_pairs={{30,0},{31,1},{0,2},{1,3},{2,4},{3,5},{4,6},{5,7},{6,8},{7,9},{8,1... | collective-permute-start | bytes 3145736 | tf_op jit(solution)/shard_map/ppermute | solution.py:277
  11.7 29.0 %copy-start.1 = (f32[2048,128]{1,0:T(8,128)S(1)}, f32[2048,128]{1,0:T(8,128)}, u32[]{:S(2)}) copy-start(f32[2048,128]{1,0:T(8,128)} %constant.27.clone.rest_1_) | copy-start | bytes 3145732
  17.3 28.5 %collective-permute-start.1 = (f32[32,4096]{1,0:T(8,128)}, f32[32,4096]{1,0:T(8,128)S(1)}, u32[]{:S(2)}, u32[]{:S(2)}) collective-permute-start(f32[32,4096]{1,0:T(8,128)} %collective-permute-done), channel_id=1, source_target_pairs={{96,0},{97,1},{98,2},{99,3},{100,4},{101,5},{102,6},{103,7},{104,8... | collective-permute-start | bytes 1572872 | tf_op jit(solution)/shard_map/ppermute | solution.py:277
  24.8 15.9 %copy-start.2 = (bf16[768,256]{1,0:T(8,128)(2,1)S(1)}, bf16[768,256]{1,0:T(8,128)(2,1)}, u32[]{:S(2)}) copy-start(bf16[768,256]{1,0:T(8,128)(2,1)} %constant.26.clone.rest_0_) | copy-start | bytes 1179652
  24.8 21.0 %collective-permute-start.3 = (f32[32,4096]{1,0:T(8,128)}, f32[32,4096]{1,0:T(8,128)S(1)}, u32[]{:S(2)}, u32[]{:S(2)}) collective-permute-start(f32[32,4096]{1,0:T(8,128)} %collective-permute-done.2), channel_id=1, source_target_pairs={{96,0},{97,1},{98,2},{99,3},{100,4},{101,5},{102,6},{103,7},{104,8... | collective-permute-start | bytes 1572872 | tf_op jit(solution)/shard_map/ppermute | solution.py:277
  39.3 6.5 %collective-permute-start.5 = (f32[64,4096]{1,0:T(8,128)S(1)}, f32[64,4096]{1,0:T(8,128)S(1)}, u32[]{:S(2)}, u32[]{:S(2)}) collective-permute-start(f32[64,4096]{1,0:T(8,128)S(1)} %collective-permute-done.4.right), channel_id=1, source_target_pairs={{0,32},{1,33},{2,34},{3,35},{4,36},{5,37},{6,38},{7,39},{8,40},{9,... | collective-permute-start | bytes 3145736 | tf_op jit(solution)/shard_map/ppermute | solution.py:277
  48.6 9.6 %collective-permute-start.6 = (f32[64,4096]{1,0:T(8,128)S(1)}, f32[64,4096]{1,0:T(8,128)S(1)}, u32[]{:S(2)}, u32[]{:S(2)}) collective-permute-start(f32[64,4096]{1,0:T(8,128)S(1)} %get-tuple-element.28), channel_id=1, source_target_pairs={{32,0},{33,1},{34,2},{35,3},{36,4},{37,5},{38,6},{39,7},{40,8},{41... | collective-permute-start | bytes 3145736 | tf_op jit(solution)/shard_map/ppermute | solution.py:277
  55.2 14.1 %collective-permute-start.8 = (f32[32,4096]{1,0:T(8,128)S(1)}, f32[32,4096]{1,0:T(8,128)S(1)}, u32[]{:S(2)}, u32[]{:S(2)}) collective-permute-start(f32[32,4096]{1,0:T(8,128)S(1)} %get-tuple-element.29), channel_id=1, source_target_pairs={{0,96},{1,97},{2,98},{3,99},{4,100},{5,101},{6,102},{7,103},{8,104... | collective-permute-start | bytes 1572872 | tf_op jit(solution)/shard_map/ppermute | solution.py:277
  58.1 16.9 %collective-permute-start.10 = (f32[32,4096]{1,0:T(8,128)S(1)}, f32[32,4096]{1,0:T(8,128)S(1)}, u32[]{:S(2)}, u32[]{:S(2)}) collective-permute-start(f32[32,4096]{1,0:T(8,128)S(1)} %get-tuple-element.31), channel_id=1, source_target_pairs={{0,96},{1,97},{2,98},{3,99},{4,100},{5,101},{6,102},{7,103},{8,104... | collective-permute-start | bytes 1572872 | tf_op jit(solution)/shard_map/ppermute | solution.py:277
  58.3 30.8 %collective-permute-start.7 = (f32[64,4096]{1,0:T(8,128)S(1)}, f32[64,4096]{1,0:T(8,128)S(1)}, u32[]{:S(2)}, u32[]{:S(2)}) collective-permute-start(f32[64,4096]{1,0:T(8,128)S(1)} %add.14), channel_id=1, source_target_pairs={{0,30},{1,31},{2,0},{3,1},{4,2},{5,3},{6,4},{7,5},{8,6},{9,7},{10,... | collective-permute-start | bytes 3145736 | tf_op jit(solution)/shard_map/ppermute | solution.py:277
  69.4 14.1 %collective-permute-start.9 = (f32[32,4096]{1,0:T(8,128)S(1)}, f32[32,4096]{1,0:T(8,128)S(1)}, u32[]{:S(2)}, u32[]{:S(2)}) collective-permute-start(f32[32,4096]{1,0:T(8,128)S(1)} %add.15), channel_id=1, source_target_pairs={{96,1},{97,2},{98,3},{99,4},{100,5},{101,6},{102,7},{103,8},{104,9... | collective-permute-start | bytes 1572872 | tf_op jit(solution)/shard_map/ppermute | solution.py:277
  75.0 14.1 %collective-permute-start.11 = (f32[32,4096]{1,0:T(8,128)S(1)}, f32[32,4096]{1,0:T(8,128)S(1)}, u32[]{:S(2)}, u32[]{:S(2)}) collective-permute-start(f32[32,4096]{1,0:T(8,128)S(1)} %add.16), channel_id=1, source_target_pairs={{96,1},{97,2},{98,3},{99,4},{100,5},{101,6},{102,7},{103,8},{104,9... | collective-permute-start | bytes 1572872 | tf_op jit(solution)/shard_map/ppermute | solution.py:277

commit v6 on v5

--- a/solution.py
+++ b/solution.py
@@ -180,14 +180,14 @@
             bottom[:, lanes] = value[HALF:]
 
 
-def unpack_body(occ, one, two, top, bottom, out):
+def unpack_body(occ, one, two, whole, top, bottom, out):
     scale = -lax.rsqrt(jnp.full((1, 128), occ[0], F32))
     low = lax.broadcasted_iota(jnp.int32, (SIZE, 128), 1) < SIZE
     for n in range(HALF // 2):
         parts = []
         for m in (2 * n, 2 * n + 1):
             lanes = slice(m * 128, (m + 1) * 128)
-            three = take((top, bottom), lanes)
+            three = whole[:, lanes] + take((top, bottom), lanes)
             parts.append((one[:, lanes] + two[:, lanes] + three) * scale)
         even, odd = parts
         out[:, n * 128 : (n + 1) * 128] = jnp.where(low, even, pltpu.roll(odd, SIZE, 1))
@@ -255,7 +255,7 @@
 
 def second_body(left_top, left_bottom, home, right, top_in, bottom_in, home_in, right_in, *rest):
     mats, outs = rest[:2], rest[2:]
-    top_out, bottom_out, home_out, right_out, *areas = outs
+    whole_out, top_out, bottom_out, home_out, right_out, *areas = outs
     left, left_outs = (left_top, left_bottom), (top_out, bottom_out)
 
     def finish_right(lanes, first, second):
@@ -263,7 +263,9 @@
         right_out[:, lanes] = right_in[:, lanes] + second
 
     def finish_home(lanes, first, second):
-        put(left_outs, lanes, take(left_outs, lanes) + first)
+        total = take(left_outs, lanes) + first
+        put(left_outs, lanes, total)
+        whole_out[:, lanes] = total
         home_out[:, lanes] = home_in[:, lanes] + second
 
     edge(left, (right,), mats, areas, finish_right)
@@ -281,23 +283,19 @@
     def at(group, place):
         return (group % groups) * blocks + place % blocks
 
-    outward, inward, across = [], [], []
+    outward, inward, direct, across, behind = [], [], [], [], []
     for group in range(groups):
         for place in range(blocks):
             source, target = at(group, place + 1), at(group, place)
+            relay = at(group - 1, place)
             if group % 2:
-                relay = at(group + 1, place + 1)
-                across.append((at(group - 1, place), target))
+                direct.append((source, target))
+                across.append((relay, target))
             else:
-                relay = at(group - 1, place)
-            outward.append((source, relay))
-            inward.append((relay, target))
-    behind = [
-        (at(group, place - 2), at(group, place))
-        for group in range(groups)
-        for place in range(blocks)
-    ]
-    return outward, inward, across, behind
+                outward.append((source, relay))
+                inward.append((relay, target))
+            behind.append((at(group, place - 2), target))
+    return outward, inward, direct, across, behind
 
 
 def turned(pairs):
@@ -307,16 +305,16 @@
 def local(orbitals, occupation):
     mats = [jnp.asarray(item) for item in constants()]
     groups, blocks = lax.axis_size("group"), lax.axis_size("blk")
-    outward, inward, across, behind = routes(groups, blocks)
-    odd = lax.axis_index("group") % 2 == 1
+    outward, inward, direct, across, behind = routes(groups, blocks)
     home, top, bottom = call(pack_body, 2, [WHOLE, PART, PART], first=SMEM)(
         occupation, orbitals[0]
     )
     right = send(home, behind)
     near = [send(top, outward), send(bottom, outward)]
+    whole = send(home, direct)
     left = [send(near[0], inward), send(near[1], inward)]
+    left = [left[0] + whole[:HALF], left[1] + whole[HALF:]]
     far = send(right, across)
-    near = [jnp.where(odd, part, 0.0) for part in near]
     acc_home, acc_right, *acc_near = call(
         first_body, 6, [WHOLE, WHOLE, PART, PART], [AREA] * 2, 2
     )(home, right, *near, *mats)
@@ -324,17 +322,18 @@
         *left, far, *mats
     )
     from_far = send(acc_far, turned(across))
-    *acc_left, acc_home, acc_right = call(
-        second_body, 10, [PART, PART, WHOLE, WHOLE], [AREA] * 2, 2
+    acc_whole, *acc_left, acc_home, acc_right = call(
+        second_body, 10, [WHOLE, PART, PART, WHOLE, WHOLE], [AREA] * 2, 2
     )(*left, home, right, *acc_left, acc_home, acc_right, *mats)
     back = [send(acc_left[0], turned(inward)), send(acc_left[1], turned(inward))]
+    from_whole = send(acc_whole, turned(direct))
     from_right = send(acc_right + from_far, turned(behind))
     from_left = [
         send(back[0] + acc_near[0], turned(outward)),
         send(back[1] + acc_near[1], turned(outward)),
     ]
-    out = call(unpack_body, 5, [WHOLE], first=SMEM)(
-        occupation, acc_home, from_right, *from_left
+    out = call(unpack_body, 6, [WHOLE], first=SMEM)(
+        occupation, acc_home, from_right, from_whole, *from_left
     )[0]
     return out[None]
 

time: 90.7 us -> 102 us (1.12)
  waiting for transfers between devices: 45 us -> 52.5 us
  starting transfers between devices: 28.4 us -> 30.2 us
  local copies, waits for them, and re-layouts: 1.23 us -> 3.02 us
    ppermute x12 -> x14, waiting for transfers between devices: 45 us -> 52.5 us  [send(): return lax.ppermute(value, AXES, pairs)]
    ppermute x12 -> x14, starting transfers between devices: 28.4 us -> 30.2 us  [send(): return lax.ppermute(value, AXES, pairs)]
    unnamed x6 -> x8, local copies, waits for them, and re-layouts: 1.23 us -> 3.02 us
  transfers between devices with their start and end apart: 12 -> 14, of which waited for: 6 -> 6; matrix products, arithmetic and copies ran while one was open for 0% -> 0% of each run, Pallas kernels for 11% -> 10%
where the time goes in v6:
time: 102 us
  waiting for transfers between devices  52.5 us (51%)
  starting transfers between devices  30.2 us (30%)
  Pallas kernels  14.9 us (15%)
  local copies, waits for them, and re-layouts  3.02 us (3%)
    ppermute x14, waiting for transfers between devices, send(): return lax.ppermute(value, AXES, pairs)  52.5 us
    ppermute x14, starting transfers between devices, send(): return lax.ppermute(value, AXES, pairs)  30.2 us
    pallas_call x1, Pallas kernels, local(): call(second_body, 10, [WHOLE, PART, PART, WHOLE, WHOLE], [AREA] * 2, 2)  5.24 us
    pallas_call x1, Pallas kernels, local(): call(first_body, 6, [WHOLE, WHOLE, PART, PART], [AREA] * 2, 2)  5.14 us
    unnamed x8, local copies, waits for them, and re-layouts  3.02 us
    pallas_call x1, Pallas kernels, local(): call(far_body, 5, [PART, PART, WHOLE], [AREA] * 2, 1)(*left, far, *mats)  2.72 us
  transfers between devices with their start and end apart: 14, of which 6 were waited for; matrix products, arithmetic and copies ran while one was open for 0% of the time, Pallas kernels for 10%

profile of v6, /device:TPU:0, one launch (start us, length us, event | category | flops | bytes accessed | tf_op | source)
XLA Modules:
  0.0 101.8 jit_solution(13825269978283458975)
XLA Ops:
  0.7 1.2 %copy-done = f32[1,64,4096]{2,1,0:T(8,128)S(1)} copy-done((f32[1,64,4096]{2,1,0:T(8,128)S(1)}, f32[1,64,4096]{2,1,0:T(8,128)}, u32[]{:S(2)}) %copy-start) | copy-done | bytes 1048600
  2.3 2.1 %collective-permute-start.5 = (f32[64,4096]{1,0:T(8,128)S(1)}, f32[64,4096]{1,0:T(8,128)S(1)}, u32[]{:S(2)}, u32[]{:S(2)}) collective-permute-start(f32[64,4096]{1,0:T(8,128)S(1)} %get-tuple-element.21.home), channel_id=1, source_target_pairs={{30,0},{31,1},{0,2},{1,3},{2,4},{3,5},{4,6},{5,7},{6,8},{7,9},{8,1... | collective-permute-start | bytes 3145736 | tf_op jit(solution)/shard_map/ppermute | solution.py:279
  4.4 8.2 %collective-permute-start = (f32[32,4096]{1,0:T(8,128)S(1)}, f32[32,4096]{1,0:T(8,128)S(1)}, u32[]{:S(2)}, u32[]{:S(2)}) collective-permute-start(f32[32,4096]{1,0:T(8,128)S(1)} %get-tuple-element.20), channel_id=1, source_target_pairs={{1,96},{2,97},{3,98},{4,99},{5,100},{6,101},{7,102},{8,103},{9,104... | collective-permute-start | bytes 1572872 | tf_op jit(solution)/shard_map/ppermute | solution.py:279
  12.5 1.3 %collective-permute-start.3 = (f32[32,4096]{1,0:T(8,128)S(1)}, f32[32,4096]{1,0:T(8,128)S(1)}, u32[]{:S(2)}, u32[]{:S(2)}) collective-permute-start(f32[32,4096]{1,0:T(8,128)S(1)} %get-tuple-element.22), channel_id=1, source_target_pairs={{1,96},{2,97},{3,98},{4,99},{5,100},{6,101},{7,102},{8,103},{9,104... | collective-permute-start | bytes 1572872 | tf_op jit(solution)/shard_map/ppermute | solution.py:279
  14.6 15.8 %collective-permute-done.near_top = f32[32,4096]{1,0:T(8,128)S(1)} collective-permute-done((f32[32,4096]{1,0:T(8,128)S(1)}, f32[32,4096]{1,0:T(8,128)S(1)}, u32[]{:S(2)}, u32[]{:S(2)}) %collective-permute-start) | collective-permute-done | bytes 524320 | tf_op jit(solution)/shard_map/ppermute | solution.py:279
  30.4 1.3 %collective-permute-start.1 = (f32[32,4096]{1,0:T(8,128)S(1)}, f32[32,4096]{1,0:T(8,128)S(1)}, u32[]{:S(2)}, u32[]{:S(2)}) collective-permute-start(f32[32,4096]{1,0:T(8,128)S(1)} %collective-permute-done.near_top), channel_id=1, source_target_pairs={{96,0},{97,1},{98,2},{99,3},{100,4},{101,5},{102,6},{103,7},{104,8... | collective-permute-start | bytes 1572872 | tf_op jit(solution)/shard_map/ppermute | solution.py:279
  31.7 4.3 %collective-permute-done.3.near_bottom = f32[32,4096]{1,0:T(8,128)S(1)} collective-permute-done((f32[32,4096]{1,0:T(8,128)S(1)}, f32[32,4096]{1,0:T(8,128)S(1)}, u32[]{:S(2)}, u32[]{:S(2)}) %collective-permute-start.3) | collective-permute-done | bytes 524320 | tf_op jit(solution)/shard_map/ppermute | solution.py:279
  36.0 1.3 %collective-permute-start.4 = (f32[32,4096]{1,0:T(8,128)S(1)}, f32[32,4096]{1,0:T(8,128)S(1)}, u32[]{:S(2)}, u32[]{:S(2)}) collective-permute-start(f32[32,4096]{1,0:T(8,128)S(1)} %collective-permute-done.3.near_bottom), channel_id=1, source_target_pairs={{96,0},{97,1},{98,2},{99,3},{100,4},{101,5},{102,6},{103,7},{104,8... | collective-permute-start | bytes 1572872 | tf_op jit(solution)/shard_map/ppermute | solution.py:279
  37.3 3.0 %collective-permute-start.6 = (f32[64,4096]{1,0:T(8,128)S(1)}, f32[64,4096]{1,0:T(8,128)S(1)}, u32[]{:S(2)}, u32[]{:S(2)}) collective-permute-start(f32[64,4096]{1,0:T(8,128)S(1)} %collective-permute-done.5.right), channel_id=1, source_target_pairs={{0,32},{1,33},{2,34},{3,35},{4,36},{5,37},{6,38},{7,39},{8,40},{9,... | collective-permute-start | bytes 3145736 | tf_op jit(solution)/shard_map/ppermute | solution.py:279
  40.3 1.0 copy-done.2
  41.3 5.1 %shard_map.48 = (f32[64,4096]{1,0:T(8,128)S(1)}, f32[64,4096]{1,0:T(8,128)S(1)}, f32[32,4096]{1,0:T(8,128)S(1)}, f32[32,4096]{1,0:T(8,128)S(1)}) custom-call(f32[64,4096]{1,0:T(8,128)S(1)} %get-tuple-element.21.home, f32[64,4096]{1,0:T(8,128)S(1)} %collective-permute-done.5.right, f32[32,4096]{1,0:T(8,128)S(1)} %collective-permute-done.near_top, ...), custom_call_target="tpu_custom_call" | custom-call | flops 80530636800 | bytes 1048576 | tf_op jit(solution)/shard_map/pallas_call | solution.py:318
  47.4 2.7 %shard_map.47 = (f32[32,4096]{1,0:T(8,128)S(1)}, f32[32,4096]{1,0:T(8,128)S(1)}, f32[64,4096]{1,0:T(8,128)S(1)}) custom-call(f32[32,4096]{1,0:T(8,128)S(1)} %get-tuple-element.36.left_top, f32[32,4096]{1,0:T(8,128)S(1)} %get-tuple-element.35.left_bottom, f32[64,4096]{1,0:T(8,128)S(1)} %collective-permute-done.6.far, bf16[768,256]{1,0:T(8,128)(2,1)S(1)} %copy-done.3, ...), custom_call_target="tpu_custom_call" | custom-call | flops 40265318400 | bytes 1048576 | tf_op jit(solution)/shard_map/pallas_call | solution.py:321
  50.2 1.5 %collective-permute-start.7 = (f32[64,4096]{1,0:T(8,128)S(1)}, f32[64,4096]{1,0:T(8,128)S(1)}, u32[]{:S(2)}, u32[]{:S(2)}) collective-permute-start(f32[64,4096]{1,0:T(8,128)S(1)} %get-tuple-element.29), channel_id=1, source_target_pairs={{32,0},{33,1},{34,2},{35,3},{36,4},{37,5},{38,6},{39,7},{40,8},{41... | collective-permute-start | bytes 3145736 | tf_op jit(solution)/shard_map/ppermute | solution.py:279
  51.7 5.2 %shard_map.49 = (f32[64,4096]{1,0:T(8,128)S(1)}, f32[32,4096]{1,0:T(8,128)S(1)}, f32[32,4096]{1,0:T(8,128)S(1)}, f32[64,4096]{1,0:T(8,128)S(1)}, f32[64,4096]{1,0:T(8,128)S(1)}) custom-call(f32[32,4096]{1,0:T(8,128)S(1)} %get-tuple-element.36.left_top, f32[32,4096]{1,0:T(8,128)S(1)} %get-tuple-element.35.left_bottom, f32[64,4096]{1,0:T(8,128)S(1)} %get-tuple-element.21.home, ...), custom_call_target="tpu_custom_call" | custom-call | flops 80530636800 | bytes 1048576 | tf_op jit(solution)/shard_map/pallas_call | solution.py:325
  56.9 4.5 %collective-permute-start.10 = (f32[32,4096]{1,0:T(8,128)S(1)}, f32[32,4096]{1,0:T(8,128)S(1)}, u32[]{:S(2)}, u32[]{:S(2)}) collective-permute-start(f32[32,4096]{1,0:T(8,128)S(1)} %get-tuple-element.31), channel_id=1, source_target_pairs={{0,96},{1,97},{2,98},{3,99},{4,100},{5,101},{6,102},{7,103},{8,104... | collective-permute-start | bytes 1572872 | tf_op jit(solution)/shard_map/ppermute | solution.py:279
  61.4 1.3 %collective-permute-start.12 = (f32[32,4096]{1,0:T(8,128)S(1)}, f32[32,4096]{1,0:T(8,128)S(1)}, u32[]{:S(2)}, u32[]{:S(2)}) collective-permute-start(f32[32,4096]{1,0:T(8,128)S(1)} %get-tuple-element.33), channel_id=1, source_target_pairs={{0,96},{1,97},{2,98},{3,99},{4,100},{5,101},{6,102},{7,103},{8,104... | collective-permute-start | bytes 1572872 | tf_op jit(solution)/shard_map/ppermute | solution.py:279
  63.6 1.8 %collective-permute-start.8 = (f32[64,4096]{1,0:T(8,128)S(1)}, f32[64,4096]{1,0:T(8,128)S(1)}, u32[]{:S(2)}, u32[]{:S(2)}) collective-permute-start(f32[64,4096]{1,0:T(8,128)S(1)} %add.17), channel_id=1, source_target_pairs={{0,30},{1,31},{2,0},{3,1},{4,2},{5,3},{6,4},{7,5},{8,6},{9,7},{10,... | collective-permute-start | bytes 3145736 | tf_op jit(solution)/shard_map/ppermute | solution.py:279
  65.4 7.7 %collective-permute-done.10 = f32[32,4096]{1,0:T(8,128)S(1)} collective-permute-done((f32[32,4096]{1,0:T(8,128)S(1)}, f32[32,4096]{1,0:T(8,128)S(1)}, u32[]{:S(2)}, u32[]{:S(2)}) %collective-permute-start.10) | collective-permute-done | bytes 524320 | tf_op jit(solution)/shard_map/ppermute | solution.py:279
  73.2 1.3 %collective-permute-start.11 = (f32[32,4096]{1,0:T(8,128)S(1)}, f32[32,4096]{1,0:T(8,128)S(1)}, u32[]{:S(2)}, u32[]{:S(2)}) collective-permute-start(f32[32,4096]{1,0:T(8,128)S(1)} %add.18), channel_id=1, source_target_pairs={{96,1},{97,2},{98,3},{99,4},{100,5},{101,6},{102,7},{103,8},{104,9... | collective-permute-start | bytes 1572872 | tf_op jit(solution)/shard_map/ppermute | solution.py:279
  74.5 9.9 %collective-permute-done.12 = f32[32,4096]{1,0:T(8,128)S(1)} collective-permute-done((f32[32,4096]{1,0:T(8,128)S(1)}, f32[32,4096]{1,0:T(8,128)S(1)}, u32[]{:S(2)}, u32[]{:S(2)}) %collective-permute-start.12) | collective-permute-done | bytes 524320 | tf_op jit(solution)/shard_map/ppermute | solution.py:279
  84.5 1.3 %collective-permute-start.13 = (f32[32,4096]{1,0:T(8,128)S(1)}, f32[32,4096]{1,0:T(8,128)S(1)}, u32[]{:S(2)}, u32[]{:S(2)}) collective-permute-start(f32[32,4096]{1,0:T(8,128)S(1)} %add.19), channel_id=1, source_target_pairs={{96,1},{97,2},{98,3},{99,4},{100,5},{101,6},{102,7},{103,8},{104,9... | collective-permute-start | bytes 1572872 | tf_op jit(solution)/shard_map/ppermute | solution.py:279
  85.8 8.3 %collective-permute-done.11.top = f32[32,4096]{1,0:T(8,128)S(1)} collective-permute-done((f32[32,4096]{1,0:T(8,128)S(1)}, f32[32,4096]{1,0:T(8,128)S(1)}, u32[]{:S(2)}, u32[]{:S(2)}) %collective-permute-start.11) | collective-permute-done | bytes 524320 | tf_op jit(solution)/shard_map/ppermute | solution.py:279
  94.1 6.3 %collective-permute-done.13.bottom = f32[32,4096]{1,0:T(8,128)S(1)} collective-permute-done((f32[32,4096]{1,0:T(8,128)S(1)}, f32[32,4096]{1,0:T(8,128)S(1)}, u32[]{:S(2)}, u32[]{:S(2)}) %collective-permute-start.13) | collective-permute-done | bytes 524320 | tf_op jit(solution)/shard_map/ppermute | solution.py:279
  100.4 1.4 %shard_map.50 = f32[64,4096]{1,0:T(8,128)} custom-call(f32[1]{0:T(128)S(6)} %copy.5.occ, f32[64,4096]{1,0:T(8,128)S(1)} %get-tuple-element.27.one, f32[64,4096]{1,0:T(8,128)S(1)} %collective-permute-done.8.two, f32[64,4096]{1,0:T(8,128)S(1)} %collective-permute-done.9.whole, f32[32,4096]{1,0:T(8,128)S(1)} %collective-permute-done.11.top, ...), custom_call_target="tpu_custom_call" | custom-call | bytes 1048576 | tf_op jit(solution)/shard_map/pallas_call | solution.py:335
  (21 shorter events, 3.0 us)
Async XLA Ops:
  0.7 1.2 %copy-start = (f32[1,64,4096]{2,1,0:T(8,128)S(1)}, f32[1,64,4096]{2,1,0:T(8,128)}, u32[]{:S(2)}) copy-start(f32[1,64,4096]{2,1,0:T(8,128)} %param.4) | copy-start | bytes 3145732
  1.9 38.4 %copy-start.1 = (f32[2048,128]{1,0:T(8,128)S(1)}, f32[2048,128]{1,0:T(8,128)}, u32[]{:S(2)}) copy-start(f32[2048,128]{1,0:T(8,128)} %constant.5.clone.rest_1_) | copy-start | bytes 3145732
  2.3 35.1 %collective-permute-start.5 = (f32[64,4096]{1,0:T(8,128)S(1)}, f32[64,4096]{1,0:T(8,128)S(1)}, u32[]{:S(2)}, u32[]{:S(2)}) collective-permute-start(f32[64,4096]{1,0:T(8,128)S(1)} %get-tuple-element.21.home), channel_id=1, source_target_pairs={{30,0},{31,1},{0,2},{1,3},{2,4},{3,5},{4,6},{5,7},{6,8},{7,9},{8,1... | collective-permute-start | bytes 3145736 | tf_op jit(solution)/shard_map/ppermute | solution.py:279
  4.4 26.0 %collective-permute-start = (f32[32,4096]{1,0:T(8,128)S(1)}, f32[32,4096]{1,0:T(8,128)S(1)}, u32[]{:S(2)}, u32[]{:S(2)}) collective-permute-start(f32[32,4096]{1,0:T(8,128)S(1)} %get-tuple-element.20), channel_id=1, source_target_pairs={{1,96},{2,97},{3,98},{4,99},{5,100},{6,101},{7,102},{8,103},{9,104... | collective-permute-start | bytes 1572872 | tf_op jit(solution)/shard_map/ppermute | solution.py:279
  12.5 23.5 %collective-permute-start.3 = (f32[32,4096]{1,0:T(8,128)S(1)}, f32[32,4096]{1,0:T(8,128)S(1)}, u32[]{:S(2)}, u32[]{:S(2)}) collective-permute-start(f32[32,4096]{1,0:T(8,128)S(1)} %get-tuple-element.22), channel_id=1, source_target_pairs={{1,96},{2,97},{3,98},{4,99},{5,100},{6,101},{7,102},{8,103},{9,104... | collective-permute-start | bytes 1572872 | tf_op jit(solution)/shard_map/ppermute | solution.py:279
  13.9 32.7 %collective-permute-start.2 = (f32[64,4096]{1,0:T(8,128)S(1)}, f32[64,4096]{1,0:T(8,128)S(1)}, u32[]{:S(2)}, u32[]{:S(2)}) collective-permute-start(f32[64,4096]{1,0:T(8,128)S(1)} %get-tuple-element.21.home), channel_id=1, source_target_pairs={{33,32},{34,33},{35,34},{36,35},{37,36},{38,37},{39,38},{40,39},{4... | collective-permute-start | bytes 3145736 | tf_op jit(solution)/shard_map/ppermute | solution.py:279
  30.4 16.1 %collective-permute-start.1 = (f32[32,4096]{1,0:T(8,128)S(1)}, f32[32,4096]{1,0:T(8,128)S(1)}, u32[]{:S(2)}, u32[]{:S(2)}) collective-permute-start(f32[32,4096]{1,0:T(8,128)S(1)} %collective-permute-done.near_top), channel_id=1, source_target_pairs={{96,0},{97,1},{98,2},{99,3},{100,4},{101,5},{102,6},{103,7},{104,8... | collective-permute-start | bytes 1572872 | tf_op jit(solution)/shard_map/ppermute | solution.py:279
  36.0 10.5 %collective-permute-start.4 = (f32[32,4096]{1,0:T(8,128)S(1)}, f32[32,4096]{1,0:T(8,128)S(1)}, u32[]{:S(2)}, u32[]{:S(2)}) collective-permute-start(f32[32,4096]{1,0:T(8,128)S(1)} %collective-permute-done.3.near_bottom), channel_id=1, source_target_pairs={{96,0},{97,1},{98,2},{99,3},{100,4},{101,5},{102,6},{103,7},{104,8... | collective-permute-start | bytes 1572872 | tf_op jit(solution)/shard_map/ppermute | solution.py:279
  37.3 9.3 %collective-permute-start.6 = (f32[64,4096]{1,0:T(8,128)S(1)}, f32[64,4096]{1,0:T(8,128)S(1)}, u32[]{:S(2)}, u32[]{:S(2)}) collective-permute-start(f32[64,4096]{1,0:T(8,128)S(1)} %collective-permute-done.5.right), channel_id=1, source_target_pairs={{0,32},{1,33},{2,34},{3,35},{4,36},{5,37},{6,38},{7,39},{8,40},{9,... | collective-permute-start | bytes 3145736 | tf_op jit(solution)/shard_map/ppermute | solution.py:279
  40.3 1.0 copy-start.2
  46.4 1.0 copy-start.3
  50.2 13.3 %collective-permute-start.7 = (f32[64,4096]{1,0:T(8,128)S(1)}, f32[64,4096]{1,0:T(8,128)S(1)}, u32[]{:S(2)}, u32[]{:S(2)}) collective-permute-start(f32[64,4096]{1,0:T(8,128)S(1)} %get-tuple-element.29), channel_id=1, source_target_pairs={{32,0},{33,1},{34,2},{35,3},{36,4},{37,5},{38,6},{39,7},{40,8},{41... | collective-permute-start | bytes 3145736 | tf_op jit(solution)/shard_map/ppermute | solution.py:279
  56.9 16.3 %collective-permute-start.10 = (f32[32,4096]{1,0:T(8,128)S(1)}, f32[32,4096]{1,0:T(8,128)S(1)}, u32[]{:S(2)}, u32[]{:S(2)}) collective-permute-start(f32[32,4096]{1,0:T(8,128)S(1)} %get-tuple-element.31), channel_id=1, source_target_pairs={{0,96},{1,97},{2,98},{3,99},{4,100},{5,101},{6,102},{7,103},{8,104... | collective-permute-start | bytes 1572872 | tf_op jit(solution)/shard_map/ppermute | solution.py:279
  61.4 23.0 %collective-permute-start.12 = (f32[32,4096]{1,0:T(8,128)S(1)}, f32[32,4096]{1,0:T(8,128)S(1)}, u32[]{:S(2)}, u32[]{:S(2)}) collective-permute-start(f32[32,4096]{1,0:T(8,128)S(1)} %get-tuple-element.33), channel_id=1, source_target_pairs={{0,96},{1,97},{2,98},{3,99},{4,100},{5,101},{6,102},{7,103},{8,104... | collective-permute-start | bytes 1572872 | tf_op jit(solution)/shard_map/ppermute | solution.py:279
  62.8 23.0 %collective-permute-start.9 = (f32[64,4096]{1,0:T(8,128)S(1)}, f32[64,4096]{1,0:T(8,128)S(1)}, u32[]{:S(2)}, u32[]{:S(2)}) collective-permute-start(f32[64,4096]{1,0:T(8,128)S(1)} %get-tuple-element.30), channel_id=1, source_target_pairs={{32,33},{33,34},{34,35},{35,36},{36,37},{37,38},{38,39},{39,40},{4... | collective-permute-start | bytes 3145736 | tf_op jit(solution)/shard_map/ppermute | solution.py:279
  63.6 36.8 %collective-permute-start.8 = (f32[64,4096]{1,0:T(8,128)S(1)}, f32[64,4096]{1,0:T(8,128)S(1)}, u32[]{:S(2)}, u32[]{:S(2)}) collective-permute-start(f32[64,4096]{1,0:T(8,128)S(1)} %add.17), channel_id=1, source_target_pairs={{0,30},{1,31},{2,0},{3,1},{4,2},{5,3},{6,4},{7,5},{8,6},{9,7},{10,... | collective-permute-start | bytes 3145736 | tf_op jit(solution)/shard_map/ppermute | solution.py:279
  73.2 20.8 %collective-permute-start.11 = (f32[32,4096]{1,0:T(8,128)S(1)}, f32[32,4096]{1,0:T(8,128)S(1)}, u32[]{:S(2)}, u32[]{:S(2)}) collective-permute-start(f32[32,4096]{1,0:T(8,128)S(1)} %add.18), channel_id=1, source_target_pairs={{96,1},{97,2},{98,3},{99,4},{100,5},{101,6},{102,7},{103,8},{104,9... | collective-permute-start | bytes 1572872 | tf_op jit(solution)/shard_map/ppermute | solution.py:279
  84.5 15.9 %collective-permute-start.13 = (f32[32,4096]{1,0:T(8,128)S(1)}, f32[32,4096]{1,0:T(8,128)S(1)}, u32[]{:S(2)}, u32[]{:S(2)}) collective-permute-start(f32[32,4096]{1,0:T(8,128)S(1)} %add.19), channel_id=1, source_target_pairs={{96,1},{97,2},{98,3},{99,4},{100,5},{101,6},{102,7},{103,8},{104,9... | collective-permute-start | bytes 1572872 | tf_op jit(solution)/shard_map/ppermute | solution.py:279

commit v7 on v4

--- a/solution.py
+++ b/solution.py
@@ -135,34 +135,58 @@
     refs[1][:, lanes] = value[HALF:]
 
 
-def forward(left, right, mats, area, tiles=16):
-    for base in range(0, HALF, tiles):
+def skewed(first, second, edges, bases):
+    prior = None
+    for base in bases:
+        for edge in edges:
+            value = first(edge, base)
+            if prior is not None:
+                second(*prior)
+            prior = (edge, base, value)
+    second(*prior)
+
+
+def solve(edges, mats, areas, tiles=16, count=32):
+    waves, others = areas[: len(edges)], areas[len(edges) :]
+    number = range(len(edges))
+    kernel = mats[1]
+
+    def rows_in(n, base):
+        left, right, _ = edges[n]
         lanes = pl.ds(base * 128, tiles * 128)
-        value = along_rows(matrix(mats, "fa"), take(left, lanes) * take(right, lanes))
+        return along_rows(matrix(mats, "fa"), take(left, lanes) * take(right, lanes))
+
+    def lanes_in(n, base, value):
         value = along_lanes(to_rows(value), matrix(mats, "fl"))
-        for n in range(tiles):
-            area[pl.ds(base + n, SIZE, stride=ROWS), :] = value[n * SIZE : (n + 1) * SIZE]
-
-
-def middle(mats, area, other, count=32):
-    kernel = mats[1]
-    for base in range(0, SIZE, count):
-        value = jnp.concatenate(
-            [area[pl.ds((base + n) * ROWS, HALF), :] for n in range(count)], axis=1
-        )
+        for m in range(tiles):
+            part = value[m * SIZE : (m + 1) * SIZE]
+            waves[n][pl.ds(base + m, SIZE, stride=ROWS), :] = part
+
+    def middle_in(n, base):
+        rows = [waves[n][pl.ds((base + m) * ROWS, HALF), :] for m in range(count)]
+        value = jnp.concatenate(rows, axis=1)
         value = pick(along_rows(matrix(mats, "fm"), value))
-        value = value * to_lanes(kernel[pl.ds(base * HALF, count * HALF), :], HALF)
+        return value * to_lanes(kernel[pl.ds(base * HALF, count * HALF), :], HALF)
+
+    def middle_out(n, base, value):
         value = pick(along_rows(matrix(mats, "bm"), value))
-        for n in range(count):
-            other[pl.ds((base + n) * ROWS, HALF), :] = value[:, n * 128 : (n + 1) * 128]
-
-
-def backward(mats, other, base, tiles=16):
-    value = jnp.concatenate(
-        [other[pl.ds(base + n, SIZE, stride=ROWS), :] for n in range(tiles)], axis=0
-    )
-    value = along_lanes(value, matrix(mats, "bl"))
-    return along_rows(matrix(mats, "ba"), to_lanes(value, SIZE))
+        for m in range(count):
+            part = value[:, m * 128 : (m + 1) * 128]
+            others[n][pl.ds((base + m) * ROWS, HALF), :] = part
+
+    def lanes_out(n, base):
+        rows = [others[n][pl.ds(base + m, SIZE, stride=ROWS), :] for m in range(tiles)]
+        return along_lanes(jnp.concatenate(rows, axis=0), matrix(mats, "bl"))
+
+    def rows_out(n, base, value):
+        left, right, finish = edges[n]
+        value = along_rows(matrix(mats, "ba"), to_lanes(value, SIZE))
+        lanes = pl.ds(base * 128, tiles * 128)
+        finish(lanes, value * take(right, lanes), value * take(left, lanes))
+
+    skewed(rows_in, lanes_in, number, range(0, HALF, tiles))
+    skewed(middle_in, middle_out, number, range(0, SIZE, count))
+    skewed(lanes_out, rows_out, number, range(0, HALF, tiles))
 
 
 def pack_body(occ, orb, out, top, bottom):
@@ -214,17 +238,8 @@
         cost_estimate=pl.CostEstimate(
             flops=work * COST, bytes_accessed=1 << 20, transcendentals=0
         ),
-        compiler_params=pltpu.CompilerParams(vmem_limit_bytes=20 << 20),
-    )
-
-
-def edge(one, two, mats, areas, finish, tiles=16):
-    forward(one, two, mats, areas[0])
-    middle(mats, *areas)
-    for base in range(0, HALF, tiles):
-        value = backward(mats, areas[1], base, tiles)
-        lanes = pl.ds(base * 128, tiles * 128)
-        finish(lanes, value * take(two, lanes), value * take(one, lanes))
+        compiler_params=pltpu.CompilerParams(vmem_limit_bytes=28 << 20),
+    )
 
 
 def first_body(home, right, near_top, near_bottom, *rest):
@@ -239,8 +254,11 @@
         right_out[:, lanes] += second
         put((top_out, bottom_out), lanes, first)
 
-    edge((home,), (right,), mats, areas, finish_home)
-    edge((near_top, near_bottom), (right,), mats, areas, finish_near)
+    edges = (
+        ((home,), (right,), finish_home),
+        ((near_top, near_bottom), (right,), finish_near),
+    )
+    solve(edges, mats, areas)
 
 
 def second_body(left_top, left_bottom, home, right, far, home_in, right_in, *rest):
@@ -260,9 +278,12 @@
         put(left_outs, lanes, take(left_outs, lanes) + first)
         home_out[:, lanes] = home_in[:, lanes] + second
 
-    edge(left, (far,), mats, areas, finish_far)
-    edge(left, (right,), mats, areas, finish_right)
-    edge(left, (home,), mats, areas, finish_home)
+    edges = (
+        (left, (far,), finish_far),
+        (left, (right,), finish_right),
+        (left, (home,), finish_home),
+    )
+    solve(edges, mats, areas)
 
 
 AXES = ("group", "blk")
@@ -313,10 +334,10 @@
     far = send(right, across)
     near = [jnp.where(odd, part, 0.0) for part in near]
     acc_home, acc_right, *acc_near = call(
-        first_body, 6, [WHOLE, WHOLE, PART, PART], [AREA] * 2, 2
+        first_body, 6, [WHOLE, WHOLE, PART, PART], [AREA] * 4, 2
     )(home, right, *near, *mats)
     *acc_left, acc_home, acc_right, acc_far = call(
-        second_body, 9, [PART, PART, WHOLE, WHOLE, WHOLE], [AREA] * 2, 3
+        second_body, 9, [PART, PART, WHOLE, WHOLE, WHOLE], [AREA] * 6, 3
     )(*left, home, right, far, acc_home, acc_right, *mats)
     back = [send(acc_left[0], turned(inward)), send(acc_left[1], turned(inward))]
     from_far = send(acc_far, turned(across))

time: 90.4 us -> 86.5 us (0.957)
  Pallas kernels: 14.4 us -> 10.7 us
    pallas_call x2, Pallas kernels: 12.7 us -> 9 us  [the longest x1 5.21 us: local(): call(second_body, 9, [PART, PART, WHOLE, WHOLE, WHOLE], [AREA] * 6, 3)]
  transfers between devices with their start and end apart: 12 -> 12, of which waited for: 7 -> 7; matrix products, arithmetic and copies ran while one was open for 0% -> 0% of each run, Pallas kernels for 6% -> 4%
where the time goes in v7:
time: 86.5 us; the launch traced here: 86.2 us
  waiting for transfers between devices  45 us (52%)
  starting transfers between devices  28.2 us (33%)
  Pallas kernels  10.7 us (12%)
  local copies, waits for them, and re-layouts  1.23 us (1%)
    ppermute x12, waiting for transfers between devices, send(): return lax.ppermute(value, AXES, pairs)  45 us
    ppermute x12, starting transfers between devices, send(): return lax.ppermute(value, AXES, pairs)  28.2 us
    pallas_call x1, Pallas kernels, local(): call(second_body, 9, [PART, PART, WHOLE, WHOLE, WHOLE], [AREA] * 6, 3)  5.21 us
    pallas_call x1, Pallas kernels, local(): call(first_body, 6, [WHOLE, WHOLE, PART, PART], [AREA] * 4, 2)  3.79 us
  transfers between devices with their start and end apart: 12, of which 7 were waited for; matrix products, arithmetic and copies ran while one was open for 0% of the time, Pallas kernels for 4%

profile of v7, /device:TPU:0, one launch (start us, length us, event | category | flops | bytes accessed | tf_op | source)
XLA Modules:
  0.0 86.2 jit_solution(3689662191093679500)
XLA Ops:
  0.7 1.2 %copy-done = f32[1,64,4096]{2,1,0:T(8,128)S(1)} copy-done((f32[1,64,4096]{2,1,0:T(8,128)S(1)}, f32[1,64,4096]{2,1,0:T(8,128)}, u32[]{:S(2)}) %copy-start) | copy-done | bytes 1048600
  1.9 0.4 shard_map.46
  2.3 8.3 %collective-permute-start = (f32[32,4096]{1,0:T(8,128)S(1)}, f32[32,4096]{1,0:T(8,128)}, u32[]{:S(2)}, u32[]{:S(2)}) collective-permute-start(f32[32,4096]{1,0:T(8,128)S(1)} %get-tuple-element.17), channel_id=1, source_target_pairs={{1,96},{2,97},{3,98},{4,99},{5,100},{6,101},{7,102},{8,103},{9,104... | collective-permute-start | bytes 1572872 | tf_op jit(solution)/shard_map/ppermute | solution.py:293
  10.6 1.1 %collective-permute-start.2 = (f32[32,4096]{1,0:T(8,128)S(1)}, f32[32,4096]{1,0:T(8,128)}, u32[]{:S(2)}, u32[]{:S(2)}) collective-permute-start(f32[32,4096]{1,0:T(8,128)S(1)} %get-tuple-element.18), channel_id=1, source_target_pairs={{1,96},{2,97},{3,98},{4,99},{5,100},{6,101},{7,102},{8,103},{9,104... | collective-permute-start | bytes 1572872 | tf_op jit(solution)/shard_map/ppermute | solution.py:293
  11.7 5.6 %collective-permute-done = f32[32,4096]{1,0:T(8,128)} collective-permute-done((f32[32,4096]{1,0:T(8,128)S(1)}, f32[32,4096]{1,0:T(8,128)}, u32[]{:S(2)}, u32[]{:S(2)}) %collective-permute-start) | collective-permute-done | bytes 524320 | tf_op jit(solution)/shard_map/ppermute | solution.py:293
  17.3 7.4 %collective-permute-start.1 = (f32[32,4096]{1,0:T(8,128)}, f32[32,4096]{1,0:T(8,128)S(1)}, u32[]{:S(2)}, u32[]{:S(2)}) collective-permute-start(f32[32,4096]{1,0:T(8,128)} %collective-permute-done), channel_id=1, source_target_pairs={{96,0},{97,1},{98,2},{99,3},{100,4},{101,5},{102,6},{103,7},{104,8... | collective-permute-start | bytes 1572872 | tf_op jit(solution)/shard_map/ppermute | solution.py:293
  24.8 5.6 %collective-permute-start.3 = (f32[32,4096]{1,0:T(8,128)}, f32[32,4096]{1,0:T(8,128)S(1)}, u32[]{:S(2)}, u32[]{:S(2)}) collective-permute-start(f32[32,4096]{1,0:T(8,128)} %collective-permute-done.2), channel_id=1, source_target_pairs={{96,0},{97,1},{98,2},{99,3},{100,4},{101,5},{102,6},{103,7},{104,8... | collective-permute-start | bytes 1572872 | tf_op jit(solution)/shard_map/ppermute | solution.py:293
  30.4 8.9 %collective-permute-done.4.right = f32[64,4096]{1,0:T(8,128)S(1)} collective-permute-done((f32[64,4096]{1,0:T(8,128)S(1)}, f32[64,4096]{1,0:T(8,128)S(1)}, u32[]{:S(2)}, u32[]{:S(2)}) %collective-permute-start.4) | collective-permute-done | bytes 1048608 | tf_op jit(solution)/shard_map/ppermute | solution.py:293
  39.3 1.3 %collective-permute-start.5 = (f32[64,4096]{1,0:T(8,128)S(1)}, f32[64,4096]{1,0:T(8,128)S(1)}, u32[]{:S(2)}, u32[]{:S(2)}) collective-permute-start(f32[64,4096]{1,0:T(8,128)S(1)} %collective-permute-done.4.right), channel_id=1, source_target_pairs={{0,32},{1,33},{2,34},{3,35},{4,36},{5,37},{6,38},{7,39},{8,40},{9,... | collective-permute-start | bytes 3145736 | tf_op jit(solution)/shard_map/ppermute | solution.py:293
  40.7 3.8 %shard_map.47 = (f32[64,4096]{1,0:T(8,128)S(1)}, f32[64,4096]{1,0:T(8,128)S(1)}, f32[32,4096]{1,0:T(8,128)S(1)}, f32[32,4096]{1,0:T(8,128)S(1)}) custom-call(f32[64,4096]{1,0:T(8,128)S(1)} %get-tuple-element.19.home, f32[64,4096]{1,0:T(8,128)S(1)} %collective-permute-done.4.right, f32[32,4096]{1,0:T(8,128)S(1)} %broadcast_select_fusion.1.near_top, ...), custom_call_target="tpu_custom_call" | custom-call | flops 80530636800 | bytes 1048576 | tf_op jit(solution)/shard_map/pallas_call | solution.py:336
  44.5 5.2 %shard_map.48 = (f32[32,4096]{1,0:T(8,128)S(1)}, f32[32,4096]{1,0:T(8,128)S(1)}, f32[64,4096]{1,0:T(8,128)S(1)}, f32[64,4096]{1,0:T(8,128)S(1)}, f32[64,4096]{1,0:T(8,128)S(1)}) custom-call(f32[32,4096]{1,0:T(8,128)S(1)} %collective-permute-done.1.left_top, f32[32,4096]{1,0:T(8,128)S(1)} %collective-permute-done.3.left_bottom, ...), custom_call_target="tpu_custom_call" | custom-call | flops 120795955200 | bytes 1048576 | tf_op jit(solution)/shard_map/pallas_call | solution.py:339
  49.7 1.3 %collective-permute-start.6 = (f32[64,4096]{1,0:T(8,128)S(1)}, f32[64,4096]{1,0:T(8,128)S(1)}, u32[]{:S(2)}, u32[]{:S(2)}) collective-permute-start(f32[64,4096]{1,0:T(8,128)S(1)} %get-tuple-element.24), channel_id=1, source_target_pairs={{32,0},{33,1},{34,2},{35,3},{36,4},{37,5},{38,6},{39,7},{40,8},{41... | collective-permute-start | bytes 3145736 | tf_op jit(solution)/shard_map/ppermute | solution.py:293
  51.0 2.9 %collective-permute-start.8 = (f32[32,4096]{1,0:T(8,128)S(1)}, f32[32,4096]{1,0:T(8,128)S(1)}, u32[]{:S(2)}, u32[]{:S(2)}) collective-permute-start(f32[32,4096]{1,0:T(8,128)S(1)} %get-tuple-element.25), channel_id=1, source_target_pairs={{0,96},{1,97},{2,98},{3,99},{4,100},{5,101},{6,102},{7,103},{8,104... | collective-permute-start | bytes 1572872 | tf_op jit(solution)/shard_map/ppermute | solution.py:293
  53.9 0.1 collective-permute-start.10
  54.0 0.3 collective-permute-done.6
  54.3 0.1 add.14
  54.4 0.1 collective-permute-start.7
  54.5 10.7 %collective-permute-done.8 = f32[32,4096]{1,0:T(8,128)S(1)} collective-permute-done((f32[32,4096]{1,0:T(8,128)S(1)}, f32[32,4096]{1,0:T(8,128)S(1)}, u32[]{:S(2)}, u32[]{:S(2)}) %collective-permute-start.8) | collective-permute-done | bytes 524320 | tf_op jit(solution)/shard_map/ppermute | solution.py:293
  65.2 0.1 collective-permute-start.9
  65.3 5.5 %collective-permute-done.10 = f32[32,4096]{1,0:T(8,128)S(1)} collective-permute-done((f32[32,4096]{1,0:T(8,128)S(1)}, f32[32,4096]{1,0:T(8,128)S(1)}, u32[]{:S(2)}, u32[]{:S(2)}) %collective-permute-start.10) | collective-permute-done | bytes 524320 | tf_op jit(solution)/shard_map/ppermute | solution.py:293
  70.8 0.1 collective-permute-start.11
  70.9 8.4 %collective-permute-done.9.top = f32[32,4096]{1,0:T(8,128)S(1)} collective-permute-done((f32[32,4096]{1,0:T(8,128)S(1)}, f32[32,4096]{1,0:T(8,128)S(1)}, u32[]{:S(2)}, u32[]{:S(2)}) %collective-permute-start.9) | collective-permute-done | bytes 524320 | tf_op jit(solution)/shard_map/ppermute | solution.py:293
  79.3 5.6 %collective-permute-done.11.bottom = f32[32,4096]{1,0:T(8,128)S(1)} collective-permute-done((f32[32,4096]{1,0:T(8,128)S(1)}, f32[32,4096]{1,0:T(8,128)S(1)}, u32[]{:S(2)}, u32[]{:S(2)}) %collective-permute-start.11) | collective-permute-done | bytes 524320 | tf_op jit(solution)/shard_map/ppermute | solution.py:293
  84.9 1.3 %shard_map.49 = f32[64,4096]{1,0:T(8,128)} custom-call(f32[1]{0:T(128)S(6)} %copy.5.occ, f32[64,4096]{1,0:T(8,128)S(1)} %get-tuple-element.22.one, f32[64,4096]{1,0:T(8,128)S(1)} %collective-permute-done.7.two, f32[32,4096]{1,0:T(8,128)S(1)} %collective-permute-done.9.top, f32[32,4096]{1,0:T(8,128)S(1)} %collective-permute-done.11.bottom), custom_call_target="tpu_custom_call" | custom-call | bytes 1048576 | tf_op jit(solution)/shard_map/pallas_call | solution.py:349
  (15 shorter events, 0.2 us)
Async XLA Ops:
  0.7 1.2 %copy-start = (f32[1,64,4096]{2,1,0:T(8,128)S(1)}, f32[1,64,4096]{2,1,0:T(8,128)}, u32[]{:S(2)}) copy-start(f32[1,64,4096]{2,1,0:T(8,128)} %param.4) | copy-start | bytes 3145732
  2.3 15.0 %collective-permute-start = (f32[32,4096]{1,0:T(8,128)S(1)}, f32[32,4096]{1,0:T(8,128)}, u32[]{:S(2)}, u32[]{:S(2)}) collective-permute-start(f32[32,4096]{1,0:T(8,128)S(1)} %get-tuple-element.17), channel_id=1, source_target_pairs={{1,96},{2,97},{3,98},{4,99},{5,100},{6,101},{7,102},{8,103},{9,104... | collective-permute-start | bytes 1572872 | tf_op jit(solution)/shard_map/ppermute | solution.py:293
  10.6 14.2 %collective-permute-start.2 = (f32[32,4096]{1,0:T(8,128)S(1)}, f32[32,4096]{1,0:T(8,128)}, u32[]{:S(2)}, u32[]{:S(2)}) collective-permute-start(f32[32,4096]{1,0:T(8,128)S(1)} %get-tuple-element.18), channel_id=1, source_target_pairs={{1,96},{2,97},{3,98},{4,99},{5,100},{6,101},{7,102},{8,103},{9,104... | collective-permute-start | bytes 1572872 | tf_op jit(solution)/shard_map/ppermute | solution.py:293
  11.7 27.6 %collective-permute-start.4 = (f32[64,4096]{1,0:T(8,128)S(1)}, f32[64,4096]{1,0:T(8,128)S(1)}, u32[]{:S(2)}, u32[]{:S(2)}) collective-permute-start(f32[64,4096]{1,0:T(8,128)S(1)} %get-tuple-element.19.home), channel_id=1, source_target_pairs={{30,0},{31,1},{0,2},{1,3},{2,4},{3,5},{4,6},{5,7},{6,8},{7,9},{8,1... | collective-permute-start | bytes 3145736 | tf_op jit(solution)/shard_map/ppermute | solution.py:293
  11.7 29.0 %copy-start.1 = (f32[2048,128]{1,0:T(8,128)S(1)}, f32[2048,128]{1,0:T(8,128)}, u32[]{:S(2)}) copy-start(f32[2048,128]{1,0:T(8,128)} %constant.27.clone.rest_1_) | copy-start | bytes 3145732
  17.3 27.2 %collective-permute-start.1 = (f32[32,4096]{1,0:T(8,128)}, f32[32,4096]{1,0:T(8,128)S(1)}, u32[]{:S(2)}, u32[]{:S(2)}) collective-permute-start(f32[32,4096]{1,0:T(8,128)} %collective-permute-done), channel_id=1, source_target_pairs={{96,0},{97,1},{98,2},{99,3},{100,4},{101,5},{102,6},{103,7},{104,8... | collective-permute-start | bytes 1572872 | tf_op jit(solution)/shard_map/ppermute | solution.py:293
  24.8 15.9 %copy-start.2 = (bf16[768,256]{1,0:T(8,128)(2,1)S(1)}, bf16[768,256]{1,0:T(8,128)(2,1)}, u32[]{:S(2)}) copy-start(bf16[768,256]{1,0:T(8,128)(2,1)} %constant.26.clone.rest_0_) | copy-start | bytes 1179652
  24.8 19.7 %collective-permute-start.3 = (f32[32,4096]{1,0:T(8,128)}, f32[32,4096]{1,0:T(8,128)S(1)}, u32[]{:S(2)}, u32[]{:S(2)}) collective-permute-start(f32[32,4096]{1,0:T(8,128)} %collective-permute-done.2), channel_id=1, source_target_pairs={{96,0},{97,1},{98,2},{99,3},{100,4},{101,5},{102,6},{103,7},{104,8... | collective-permute-start | bytes 1572872 | tf_op jit(solution)/shard_map/ppermute | solution.py:293
  39.3 5.2 %collective-permute-start.5 = (f32[64,4096]{1,0:T(8,128)S(1)}, f32[64,4096]{1,0:T(8,128)S(1)}, u32[]{:S(2)}, u32[]{:S(2)}) collective-permute-start(f32[64,4096]{1,0:T(8,128)S(1)} %collective-permute-done.4.right), channel_id=1, source_target_pairs={{0,32},{1,33},{2,34},{3,35},{4,36},{5,37},{6,38},{7,39},{8,40},{9,... | collective-permute-start | bytes 3145736 | tf_op jit(solution)/shard_map/ppermute | solution.py:293
  49.7 4.6 %collective-permute-start.6 = (f32[64,4096]{1,0:T(8,128)S(1)}, f32[64,4096]{1,0:T(8,128)S(1)}, u32[]{:S(2)}, u32[]{:S(2)}) collective-permute-start(f32[64,4096]{1,0:T(8,128)S(1)} %get-tuple-element.24), channel_id=1, source_target_pairs={{32,0},{33,1},{34,2},{35,3},{36,4},{37,5},{38,6},{39,7},{40,8},{41... | collective-permute-start | bytes 3145736 | tf_op jit(solution)/shard_map/ppermute | solution.py:293
  51.0 14.1 %collective-permute-start.8 = (f32[32,4096]{1,0:T(8,128)S(1)}, f32[32,4096]{1,0:T(8,128)S(1)}, u32[]{:S(2)}, u32[]{:S(2)}) collective-permute-start(f32[32,4096]{1,0:T(8,128)S(1)} %get-tuple-element.25), channel_id=1, source_target_pairs={{0,96},{1,97},{2,98},{3,99},{4,100},{5,101},{6,102},{7,103},{8,104... | collective-permute-start | bytes 1572872 | tf_op jit(solution)/shard_map/ppermute | solution.py:293
  53.9 16.9 %collective-permute-start.10 = (f32[32,4096]{1,0:T(8,128)S(1)}, f32[32,4096]{1,0:T(8,128)S(1)}, u32[]{:S(2)}, u32[]{:S(2)}) collective-permute-start(f32[32,4096]{1,0:T(8,128)S(1)} %get-tuple-element.27), channel_id=1, source_target_pairs={{0,96},{1,97},{2,98},{3,99},{4,100},{5,101},{6,102},{7,103},{8,104... | collective-permute-start | bytes 1572872 | tf_op jit(solution)/shard_map/ppermute | solution.py:293
  54.4 30.5 %collective-permute-start.7 = (f32[64,4096]{1,0:T(8,128)S(1)}, f32[64,4096]{1,0:T(8,128)S(1)}, u32[]{:S(2)}, u32[]{:S(2)}) collective-permute-start(f32[64,4096]{1,0:T(8,128)S(1)} %add.14), channel_id=1, source_target_pairs={{0,30},{1,31},{2,0},{3,1},{4,2},{5,3},{6,4},{7,5},{8,6},{9,7},{10,... | collective-permute-start | bytes 3145736 | tf_op jit(solution)/shard_map/ppermute | solution.py:293
  65.2 14.1 %collective-permute-start.9 = (f32[32,4096]{1,0:T(8,128)S(1)}, f32[32,4096]{1,0:T(8,128)S(1)}, u32[]{:S(2)}, u32[]{:S(2)}) collective-permute-start(f32[32,4096]{1,0:T(8,128)S(1)} %add.15), channel_id=1, source_target_pairs={{96,1},{97,2},{98,3},{99,4},{100,5},{101,6},{102,7},{103,8},{104,9... | collective-permute-start | bytes 1572872 | tf_op jit(solution)/shard_map/ppermute | solution.py:293
  70.8 14.1 %collective-permute-start.11 = (f32[32,4096]{1,0:T(8,128)S(1)}, f32[32,4096]{1,0:T(8,128)S(1)}, u32[]{:S(2)}, u32[]{:S(2)}) collective-permute-start(f32[32,4096]{1,0:T(8,128)S(1)} %add.16), channel_id=1, source_target_pairs={{96,1},{97,2},{98,3},{99,4},{100,5},{101,6},{102,7},{103,8},{104,9... | collective-permute-start | bytes 1572872 | tf_op jit(solution)/shard_map/ppermute | solution.py:293

commit v8 on v7

--- a/solution.py
+++ b/solution.py
@@ -187,6 +187,16 @@
     skewed(rows_in, lanes_in, number, range(0, HALF, tiles))
     skewed(middle_in, middle_out, number, range(0, SIZE, count))
     skewed(lanes_out, rows_out, number, range(0, HALF, tiles))
+
+
+def pieces(left, right, sems):
+    copies = []
+    for n in range(8):
+        lanes = pl.ds(n * 512, 512)
+        copies.append(
+            pltpu.make_async_copy(left.at[:, lanes], right.at[:, lanes], sems.at[n])
+        )
+    return copies
 
 
 def pack_body(occ, orb, out, top, bottom):
@@ -204,7 +214,8 @@
             bottom[:, lanes] = value[HALF:]
 
 
-def unpack_body(occ, one, two, top, bottom, out):
+def unpack_body(occ, one, two, top, bottom, target, out, sems):
+    copies = pieces(out, target, sems)
     scale = -lax.rsqrt(jnp.full((1, 128), occ[0], F32))
     low = lax.broadcasted_iota(jnp.int32, (SIZE, 128), 1) < SIZE
     for n in range(HALF // 2):
@@ -218,6 +229,11 @@
         out[:, (n + 16) * 128 : (n + 17) * 128] = jnp.where(
             low, pltpu.roll(even, SIZE, 1), odd
         )
+        if n % 4 == 3:
+            copies[n // 4].start()
+            copies[n // 4 + 4].start()
+    for copy in copies:
+        copy.wait()
 
 
 WHOLE = jax.ShapeDtypeStruct((SIZE, SIZE * SIZE), F32)
@@ -225,15 +241,17 @@
 SMEM = pl.BlockSpec(memory_space=pltpu.SMEM)
 VMEM = pl.BlockSpec(memory_space=pltpu.VMEM)
 COST = 2 * 6 * SIZE**4 * 200
+HBM = pl.BlockSpec(memory_space=pltpu.HBM)
+MOVE = (pltpu.VMEM((SIZE, SIZE * SIZE), F32), pltpu.SemaphoreType.DMA((8,)))
 AREA = pltpu.VMEM((SIZE * ROWS, 128), F32)
 
 
-def call(body, count, outs, scratch=(), work=0, first=VMEM):
+def call(body, count, outs, scratch=(), work=0, first=VMEM, out=VMEM):
     return pl.pallas_call(
         body,
         out_shape=list(outs),
         in_specs=[first] + [VMEM] * (count - 1),
-        out_specs=[VMEM] * len(outs),
+        out_specs=[out] * len(outs),
         scratch_shapes=list(scratch),
         cost_estimate=pl.CostEstimate(
             flops=work * COST, bytes_accessed=1 << 20, transcendentals=0
@@ -346,7 +364,7 @@
         send(back[0] + acc_near[0], turned(outward)),
         send(back[1] + acc_near[1], turned(outward)),
     ]
-    out = call(unpack_body, 5, [WHOLE], first=SMEM)(
+    out = call(unpack_body, 5, [WHOLE], MOVE, first=SMEM, out=HBM)(
         occupation, acc_home, from_right, *from_left
     )[0]
     return out[None]

time: 86.5 us -> 86.3 us (level)
  no operation moved by 1% of the time
where the time goes in v8:
time: 86.3 us; the launch traced here: 86.1 us
  waiting for transfers between devices  45 us (52%)
  starting transfers between devices  28.2 us (33%)
  Pallas kernels  10.6 us (12%)
  local copies, waits for them, and re-layouts  1.23 us (1%)
    ppermute x12, waiting for transfers between devices, send(): return lax.ppermute(value, AXES, pairs)  45 us
    ppermute x12, starting transfers between devices, send(): return lax.ppermute(value, AXES, pairs)  28.2 us
    pallas_call x1, Pallas kernels, local(): call(second_body, 9, [PART, PART, WHOLE, WHOLE, WHOLE], [AREA] * 6, 3)  5.21 us
    pallas_call x1, Pallas kernels, local(): call(first_body, 6, [WHOLE, WHOLE, PART, PART], [AREA] * 4, 2)  3.79 us
  transfers between devices with their start and end apart: 12, of which 7 were waited for; matrix products, arithmetic and copies ran while one was open for 0% of the time, Pallas kernels for 4%

profile of v8, /device:TPU:0, one launch (start us, length us, event | category | flops | bytes accessed | tf_op | source)
XLA Modules:
  0.0 86.1 jit_solution(10680445513540385939)
XLA Ops:
  0.7 1.2 %copy-done = f32[1,64,4096]{2,1,0:T(8,128)S(1)} copy-done((f32[1,64,4096]{2,1,0:T(8,128)S(1)}, f32[1,64,4096]{2,1,0:T(8,128)}, u32[]{:S(2)}) %copy-start) | copy-done | bytes 1048600
  1.9 0.4 shard_map.46
  2.3 8.3 %collective-permute-start = (f32[32,4096]{1,0:T(8,128)S(1)}, f32[32,4096]{1,0:T(8,128)}, u32[]{:S(2)}, u32[]{:S(2)}) collective-permute-start(f32[32,4096]{1,0:T(8,128)S(1)} %get-tuple-element.17), channel_id=1, source_target_pairs={{1,96},{2,97},{3,98},{4,99},{5,100},{6,101},{7,102},{8,103},{9,104... | collective-permute-start | bytes 1572872 | tf_op jit(solution)/shard_map/ppermute | solution.py:311
  10.6 1.1 %collective-permute-start.2 = (f32[32,4096]{1,0:T(8,128)S(1)}, f32[32,4096]{1,0:T(8,128)}, u32[]{:S(2)}, u32[]{:S(2)}) collective-permute-start(f32[32,4096]{1,0:T(8,128)S(1)} %get-tuple-element.18), channel_id=1, source_target_pairs={{1,96},{2,97},{3,98},{4,99},{5,100},{6,101},{7,102},{8,103},{9,104... | collective-permute-start | bytes 1572872 | tf_op jit(solution)/shard_map/ppermute | solution.py:311
  11.7 5.6 %collective-permute-done = f32[32,4096]{1,0:T(8,128)} collective-permute-done((f32[32,4096]{1,0:T(8,128)S(1)}, f32[32,4096]{1,0:T(8,128)}, u32[]{:S(2)}, u32[]{:S(2)}) %collective-permute-start) | collective-permute-done | bytes 524320 | tf_op jit(solution)/shard_map/ppermute | solution.py:311
  17.3 7.4 %collective-permute-start.1 = (f32[32,4096]{1,0:T(8,128)}, f32[32,4096]{1,0:T(8,128)S(1)}, u32[]{:S(2)}, u32[]{:S(2)}) collective-permute-start(f32[32,4096]{1,0:T(8,128)} %collective-permute-done), channel_id=1, source_target_pairs={{96,0},{97,1},{98,2},{99,3},{100,4},{101,5},{102,6},{103,7},{104,8... | collective-permute-start | bytes 1572872 | tf_op jit(solution)/shard_map/ppermute | solution.py:311
  24.8 5.6 %collective-permute-start.3 = (f32[32,4096]{1,0:T(8,128)}, f32[32,4096]{1,0:T(8,128)S(1)}, u32[]{:S(2)}, u32[]{:S(2)}) collective-permute-start(f32[32,4096]{1,0:T(8,128)} %collective-permute-done.2), channel_id=1, source_target_pairs={{96,0},{97,1},{98,2},{99,3},{100,4},{101,5},{102,6},{103,7},{104,8... | collective-permute-start | bytes 1572872 | tf_op jit(solution)/shard_map/ppermute | solution.py:311
  30.4 8.9 %collective-permute-done.4.right = f32[64,4096]{1,0:T(8,128)S(1)} collective-permute-done((f32[64,4096]{1,0:T(8,128)S(1)}, f32[64,4096]{1,0:T(8,128)S(1)}, u32[]{:S(2)}, u32[]{:S(2)}) %collective-permute-start.4) | collective-permute-done | bytes 1048608 | tf_op jit(solution)/shard_map/ppermute | solution.py:311
  39.3 1.3 %collective-permute-start.5 = (f32[64,4096]{1,0:T(8,128)S(1)}, f32[64,4096]{1,0:T(8,128)S(1)}, u32[]{:S(2)}, u32[]{:S(2)}) collective-permute-start(f32[64,4096]{1,0:T(8,128)S(1)} %collective-permute-done.4.right), channel_id=1, source_target_pairs={{0,32},{1,33},{2,34},{3,35},{4,36},{5,37},{6,38},{7,39},{8,40},{9,... | collective-permute-start | bytes 3145736 | tf_op jit(solution)/shard_map/ppermute | solution.py:311
  40.7 3.8 %shard_map.47 = (f32[64,4096]{1,0:T(8,128)S(1)}, f32[64,4096]{1,0:T(8,128)S(1)}, f32[32,4096]{1,0:T(8,128)S(1)}, f32[32,4096]{1,0:T(8,128)S(1)}) custom-call(f32[64,4096]{1,0:T(8,128)S(1)} %get-tuple-element.19.home, f32[64,4096]{1,0:T(8,128)S(1)} %collective-permute-done.4.right, f32[32,4096]{1,0:T(8,128)S(1)} %broadcast_select_fusion.1.near_top, ...), custom_call_target="tpu_custom_call" | custom-call | flops 80530636800 | bytes 1048576 | tf_op jit(solution)/shard_map/pallas_call | solution.py:354
  44.5 5.2 %shard_map.48 = (f32[32,4096]{1,0:T(8,128)S(1)}, f32[32,4096]{1,0:T(8,128)S(1)}, f32[64,4096]{1,0:T(8,128)S(1)}, f32[64,4096]{1,0:T(8,128)S(1)}, f32[64,4096]{1,0:T(8,128)S(1)}) custom-call(f32[32,4096]{1,0:T(8,128)S(1)} %collective-permute-done.1.left_top, f32[32,4096]{1,0:T(8,128)S(1)} %collective-permute-done.3.left_bottom, ...), custom_call_target="tpu_custom_call" | custom-call | flops 120795955200 | bytes 1048576 | tf_op jit(solution)/shard_map/pallas_call | solution.py:357
  49.7 1.3 %collective-permute-start.6 = (f32[64,4096]{1,0:T(8,128)S(1)}, f32[64,4096]{1,0:T(8,128)S(1)}, u32[]{:S(2)}, u32[]{:S(2)}) collective-permute-start(f32[64,4096]{1,0:T(8,128)S(1)} %get-tuple-element.24), channel_id=1, source_target_pairs={{32,0},{33,1},{34,2},{35,3},{36,4},{37,5},{38,6},{39,7},{40,8},{41... | collective-permute-start | bytes 3145736 | tf_op jit(solution)/shard_map/ppermute | solution.py:311
  51.0 2.9 %collective-permute-start.8 = (f32[32,4096]{1,0:T(8,128)S(1)}, f32[32,4096]{1,0:T(8,128)S(1)}, u32[]{:S(2)}, u32[]{:S(2)}) collective-permute-start(f32[32,4096]{1,0:T(8,128)S(1)} %get-tuple-element.25), channel_id=1, source_target_pairs={{0,96},{1,97},{2,98},{3,99},{4,100},{5,101},{6,102},{7,103},{8,104... | collective-permute-start | bytes 1572872 | tf_op jit(solution)/shard_map/ppermute | solution.py:311
  53.9 0.1 collective-permute-start.10
  54.0 0.3 collective-permute-done.6
  54.3 0.1 add.14
  54.4 0.1 collective-permute-start.7
  54.5 10.7 %collective-permute-done.8 = f32[32,4096]{1,0:T(8,128)S(1)} collective-permute-done((f32[32,4096]{1,0:T(8,128)S(1)}, f32[32,4096]{1,0:T(8,128)S(1)}, u32[]{:S(2)}, u32[]{:S(2)}) %collective-permute-start.8) | collective-permute-done | bytes 524320 | tf_op jit(solution)/shard_map/ppermute | solution.py:311
  65.2 0.1 collective-permute-start.9
  65.3 5.5 %collective-permute-done.10 = f32[32,4096]{1,0:T(8,128)S(1)} collective-permute-done((f32[32,4096]{1,0:T(8,128)S(1)}, f32[32,4096]{1,0:T(8,128)S(1)}, u32[]{:S(2)}, u32[]{:S(2)}) %collective-permute-start.10) | collective-permute-done | bytes 524320 | tf_op jit(solution)/shard_map/ppermute | solution.py:311
  70.8 0.1 collective-permute-start.11
  70.9 8.4 %collective-permute-done.9.top = f32[32,4096]{1,0:T(8,128)S(1)} collective-permute-done((f32[32,4096]{1,0:T(8,128)S(1)}, f32[32,4096]{1,0:T(8,128)S(1)}, u32[]{:S(2)}, u32[]{:S(2)}) %collective-permute-start.9) | collective-permute-done | bytes 524320 | tf_op jit(solution)/shard_map/ppermute | solution.py:311
  79.3 5.6 %collective-permute-done.11.bottom = f32[32,4096]{1,0:T(8,128)S(1)} collective-permute-done((f32[32,4096]{1,0:T(8,128)S(1)}, f32[32,4096]{1,0:T(8,128)S(1)}, u32[]{:S(2)}, u32[]{:S(2)}) %collective-permute-start.11) | collective-permute-done | bytes 524320 | tf_op jit(solution)/shard_map/ppermute | solution.py:311
  84.9 1.2 %shard_map.49 = f32[64,4096]{1,0:T(8,128)} custom-call(f32[1]{0:T(128)S(6)} %copy.5.occ, f32[64,4096]{1,0:T(8,128)S(1)} %get-tuple-element.22.one, f32[64,4096]{1,0:T(8,128)S(1)} %collective-permute-done.7.two, f32[32,4096]{1,0:T(8,128)S(1)} %collective-permute-done.9.top, f32[32,4096]{1,0:T(8,128)S(1)} %collective-permute-done.11.bottom), custom_call_target="tpu_custom_call" | custom-call | bytes 1048576 | tf_op jit(solution)/shard_map/pallas_call | solution.py:367
  (15 shorter events, 0.2 us)
Async XLA Ops:
  0.7 1.2 %copy-start = (f32[1,64,4096]{2,1,0:T(8,128)S(1)}, f32[1,64,4096]{2,1,0:T(8,128)}, u32[]{:S(2)}) copy-start(f32[1,64,4096]{2,1,0:T(8,128)} %param.4) | copy-start | bytes 3145732
  2.3 15.0 %collective-permute-start = (f32[32,4096]{1,0:T(8,128)S(1)}, f32[32,4096]{1,0:T(8,128)}, u32[]{:S(2)}, u32[]{:S(2)}) collective-permute-start(f32[32,4096]{1,0:T(8,128)S(1)} %get-tuple-element.17), channel_id=1, source_target_pairs={{1,96},{2,97},{3,98},{4,99},{5,100},{6,101},{7,102},{8,103},{9,104... | collective-permute-start | bytes 1572872 | tf_op jit(solution)/shard_map/ppermute | solution.py:311
  10.6 14.2 %collective-permute-start.2 = (f32[32,4096]{1,0:T(8,128)S(1)}, f32[32,4096]{1,0:T(8,128)}, u32[]{:S(2)}, u32[]{:S(2)}) collective-permute-start(f32[32,4096]{1,0:T(8,128)S(1)} %get-tuple-element.18), channel_id=1, source_target_pairs={{1,96},{2,97},{3,98},{4,99},{5,100},{6,101},{7,102},{8,103},{9,104... | collective-permute-start | bytes 1572872 | tf_op jit(solution)/shard_map/ppermute | solution.py:311
  11.7 27.6 %collective-permute-start.4 = (f32[64,4096]{1,0:T(8,128)S(1)}, f32[64,4096]{1,0:T(8,128)S(1)}, u32[]{:S(2)}, u32[]{:S(2)}) collective-permute-start(f32[64,4096]{1,0:T(8,128)S(1)} %get-tuple-element.19.home), channel_id=1, source_target_pairs={{30,0},{31,1},{0,2},{1,3},{2,4},{3,5},{4,6},{5,7},{6,8},{7,9},{8,1... | collective-permute-start | bytes 3145736 | tf_op jit(solution)/shard_map/ppermute | solution.py:311
  11.7 29.0 %copy-start.1 = (f32[2048,128]{1,0:T(8,128)S(1)}, f32[2048,128]{1,0:T(8,128)}, u32[]{:S(2)}) copy-start(f32[2048,128]{1,0:T(8,128)} %constant.27.clone.rest_1_) | copy-start | bytes 3145732
  17.3 27.2 %collective-permute-start.1 = (f32[32,4096]{1,0:T(8,128)}, f32[32,4096]{1,0:T(8,128)S(1)}, u32[]{:S(2)}, u32[]{:S(2)}) collective-permute-start(f32[32,4096]{1,0:T(8,128)} %collective-permute-done), channel_id=1, source_target_pairs={{96,0},{97,1},{98,2},{99,3},{100,4},{101,5},{102,6},{103,7},{104,8... | collective-permute-start | bytes 1572872 | tf_op jit(solution)/shard_map/ppermute | solution.py:311
  24.8 15.9 %copy-start.2 = (bf16[768,256]{1,0:T(8,128)(2,1)S(1)}, bf16[768,256]{1,0:T(8,128)(2,1)}, u32[]{:S(2)}) copy-start(bf16[768,256]{1,0:T(8,128)(2,1)} %constant.26.clone.rest_0_) | copy-start | bytes 1179652
  24.8 19.7 %collective-permute-start.3 = (f32[32,4096]{1,0:T(8,128)}, f32[32,4096]{1,0:T(8,128)S(1)}, u32[]{:S(2)}, u32[]{:S(2)}) collective-permute-start(f32[32,4096]{1,0:T(8,128)} %collective-permute-done.2), channel_id=1, source_target_pairs={{96,0},{97,1},{98,2},{99,3},{100,4},{101,5},{102,6},{103,7},{104,8... | collective-permute-start | bytes 1572872 | tf_op jit(solution)/shard_map/ppermute | solution.py:311
  39.3 5.2 %collective-permute-start.5 = (f32[64,4096]{1,0:T(8,128)S(1)}, f32[64,4096]{1,0:T(8,128)S(1)}, u32[]{:S(2)}, u32[]{:S(2)}) collective-permute-start(f32[64,4096]{1,0:T(8,128)S(1)} %collective-permute-done.4.right), channel_id=1, source_target_pairs={{0,32},{1,33},{2,34},{3,35},{4,36},{5,37},{6,38},{7,39},{8,40},{9,... | collective-permute-start | bytes 3145736 | tf_op jit(solution)/shard_map/ppermute | solution.py:311
  49.7 4.6 %collective-permute-start.6 = (f32[64,4096]{1,0:T(8,128)S(1)}, f32[64,4096]{1,0:T(8,128)S(1)}, u32[]{:S(2)}, u32[]{:S(2)}) collective-permute-start(f32[64,4096]{1,0:T(8,128)S(1)} %get-tuple-element.24), channel_id=1, source_target_pairs={{32,0},{33,1},{34,2},{35,3},{36,4},{37,5},{38,6},{39,7},{40,8},{41... | collective-permute-start | bytes 3145736 | tf_op jit(solution)/shard_map/ppermute | solution.py:311
  51.0 14.1 %collective-permute-start.8 = (f32[32,4096]{1,0:T(8,128)S(1)}, f32[32,4096]{1,0:T(8,128)S(1)}, u32[]{:S(2)}, u32[]{:S(2)}) collective-permute-start(f32[32,4096]{1,0:T(8,128)S(1)} %get-tuple-element.25), channel_id=1, source_target_pairs={{0,96},{1,97},{2,98},{3,99},{4,100},{5,101},{6,102},{7,103},{8,104... | collective-permute-start | bytes 1572872 | tf_op jit(solution)/shard_map/ppermute | solution.py:311
  53.9 16.9 %collective-permute-start.10 = (f32[32,4096]{1,0:T(8,128)S(1)}, f32[32,4096]{1,0:T(8,128)S(1)}, u32[]{:S(2)}, u32[]{:S(2)}) collective-permute-start(f32[32,4096]{1,0:T(8,128)S(1)} %get-tuple-element.27), channel_id=1, source_target_pairs={{0,96},{1,97},{2,98},{3,99},{4,100},{5,101},{6,102},{7,103},{8,104... | collective-permute-start | bytes 1572872 | tf_op jit(solution)/shard_map/ppermute | solution.py:311
  54.4 30.5 %collective-permute-start.7 = (f32[64,4096]{1,0:T(8,128)S(1)}, f32[64,4096]{1,0:T(8,128)S(1)}, u32[]{:S(2)}, u32[]{:S(2)}) collective-permute-start(f32[64,4096]{1,0:T(8,128)S(1)} %add.14), channel_id=1, source_target_pairs={{0,30},{1,31},{2,0},{3,1},{4,2},{5,3},{6,4},{7,5},{8,6},{9,7},{10,... | collective-permute-start | bytes 3145736 | tf_op jit(solution)/shard_map/ppermute | solution.py:311
  65.2 14.1 %collective-permute-start.9 = (f32[32,4096]{1,0:T(8,128)S(1)}, f32[32,4096]{1,0:T(8,128)S(1)}, u32[]{:S(2)}, u32[]{:S(2)}) collective-permute-start(f32[32,4096]{1,0:T(8,128)S(1)} %add.15), channel_id=1, source_target_pairs={{96,1},{97,2},{98,3},{99,4},{100,5},{101,6},{102,7},{103,8},{104,9... | collective-permute-start | bytes 1572872 | tf_op jit(solution)/shard_map/ppermute | solution.py:311
  70.8 14.1 %collective-permute-start.11 = (f32[32,4096]{1,0:T(8,128)S(1)}, f32[32,4096]{1,0:T(8,128)S(1)}, u32[]{:S(2)}, u32[]{:S(2)}) collective-permute-start(f32[32,4096]{1,0:T(8,128)S(1)} %add.16), channel_id=1, source_target_pairs={{96,1},{97,2},{98,3},{99,4},{100,5},{101,6},{102,7},{103,8},{104,9... | collective-permute-start | bytes 1572872 | tf_op jit(solution)/shard_map/ppermute | solution.py:311
